TPU v7x, 512 devices: a whole 4x4x16 slice. The times are simulated.
512 devices in a mesh: row: 16 (over z), col: 32 (over x, y, core).
Axes of the slice: x: 4, y: 4, z: 16, core: 2. Of those that a mesh axis runs over, the one named last changes fastest.
Arguments:
- rhs_panels: float32 [3, 16, 32, 64, 256], P(None, 'row', 'col'), may hold values from -6 to 6
- inverse_diag: bfloat16 [3, 16, 32, 256, 256], P(None, 'row', 'col'), may hold values from -0.375 to 0.375
- factor_blocks: bfloat16 [3, 16, 320, 256, 256], P(None, 'row', 'col'), may hold values from -0.078125 to 0.078125
- block_target: int32 [3, 16, 320], P(None, 'row', 'col'), may hold values from 0 to 15, as said below
- block_source: int32 [3, 16, 320], P(None, 'row', 'col'), may hold values from 0 to 31, as said below
Outputs:
- solution: float32 [3, 16, 32, 64, 256], P(None, 'row', 'col')
Inputs may be any that keep to these rules, and one draw needn't show every extreme that they name: (block_target[p, r, q] - r) modulo 16 is below 2, or equals 8, or equals 15; each of 1, 8 and 15 occurs. (block_source[p, r, q] - q // 10) modulo 32 is below 2, or equals 16, or equals 31; each of 1, 16 and 31 occurs.
All inputs are finite; a program needn't handle non-finite values.
Results may differ from a plain program's by a relative error of at most 0.014.
Values may be sent and summed in bfloat16 or wider, within the bound.
No kernel may reach another device: no remote copies, remote signals or barrier semaphores. Data moves between devices by JAX's collectives and lax.ppermute only.
A program may use at most 64 MiB of HBM per device.

v0:
```python
import jax
import jax.numpy as jnp
from jax import lax
from jax.sharding import PartitionSpec as P

WINDOW = 2


def from_behind(value, axis, steps):
    count = lax.axis_size(axis)
    pairs = [(source, (source + steps) % count) for source in range(count)]
    return lax.ppermute(value, axis, pairs)


def laid_out(pieces, dim):
    dims = list(pieces.shape[1:])
    dims[dim] *= pieces.shape[0]
    return jnp.moveaxis(pieces, 0, dim).reshape(dims)


def from_everyone(value, axis):
    count = lax.axis_size(axis)
    return lax.all_to_all(
        jnp.broadcast_to(value[None], (count, *value.shape)), axis, 0, 0, tiled=True
    )


def collect(value, axis, dim):
    return laid_out(from_everyone(value, axis), dim)


def pair_table(levels):
    return [
        (target_lvl, source_lvl)
        for target_lvl in range(1, levels)
        for source_lvl in range(target_lvl)
    ]


def offset_choices(window, count):
    values = sorted(set(list(range(window)) + [count // 2, count - 1]))
    return values


def offset_places(offsets, values):
    places = jnp.zeros(offsets.shape, jnp.int32)
    for position, value in enumerate(values):
        places = places + jnp.where(offsets == value, position, 0).astype(jnp.int32)
    return places


def spread_rows(indices, row_count, products):
    onehot = (indices[None, :] == jnp.arange(row_count, dtype=jnp.int32)[:, None]).astype(
        jnp.float32
    )
    flattened = products.reshape(products.shape[0], -1)
    summed = jnp.dot(
        onehot, flattened, precision=lax.Precision.HIGHEST, preferred_element_type=jnp.float32
    )
    return summed.reshape((row_count,) + products.shape[1:])


def deliver_rows(partial_value, values):
    summed = partial_value[0].astype(jnp.bfloat16).astype(jnp.float32)
    for position in range(1, partial_value.shape[0]):
        moved = from_behind(partial_value[position].astype(jnp.bfloat16), "row", values[position])
        summed = summed + moved.astype(jnp.float32)
    return summed


def deliver_cols(partial_value, values):
    summed = partial_value[0].astype(jnp.bfloat16).astype(jnp.float32)
    for position in range(1, partial_value.shape[0]):
        moved = from_behind(partial_value[position].astype(jnp.bfloat16), "col", values[position])
        summed = summed + moved.astype(jnp.float32)
    return summed


def shards(rhs_panels, inverse_diag, factor_blocks, block_target, block_source):
    levels = rhs_panels.shape[0]
    row_devices = lax.axis_size("row")
    col_devices = lax.axis_size("col")
    pair_list = pair_table(levels)
    blocks = factor_blocks[:, 0]
    targets = block_target[:, 0]
    sources = block_source[:, 0]
    row_values = offset_choices(WINDOW, row_devices)
    col_values = offset_choices(WINDOW, col_devices)
    row_keys = offset_places((targets - lax.axis_index("row")) % row_devices, row_values)
    col_keys = offset_places((sources - lax.axis_index("col")) % col_devices, col_values)
    row_width = len(row_values)
    col_width = len(col_values)
    forward = []
    gathered = {}
    for current in range(levels):
        residual = rhs_panels[current, 0, 0]
        if current > 0:
            partial_value = jnp.zeros((row_width,) + residual.shape, jnp.float32)
            for pair_idx, pair_info in enumerate(pair_list):
                if pair_info[0] == current:
                    picked = jnp.take(gathered[pair_info[1]], sources[pair_idx], axis=0)
                    products = jnp.einsum(
                        "snb,sab->sna", picked, blocks[pair_idx], preferred_element_type=jnp.float32
                    )
                    partial_value = partial_value + spread_rows(
                        row_keys[pair_idx], row_width, products
                    )
            summed = deliver_rows(partial_value, row_values)
            residual = residual - summed
        reduced = residual.astype(jnp.bfloat16)
        panel_now = lax.dot_general(
            reduced,
            inverse_diag[current, 0, 0],
            (((1,), (1,)), ((), ())),
            preferred_element_type=jnp.float32,
        )
        forward.append(panel_now)
        if current < levels - 1:
            outgoing = panel_now.astype(jnp.bfloat16)[None]
            gathered[current] = collect(outgoing, "col", 0)
    solutions = [None] * levels
    gathered_back = {}
    for current in reversed(range(levels)):
        residual = forward[current]
        if current < levels - 1:
            partial_value = jnp.zeros((col_width,) + residual.shape, jnp.float32)
            for pair_idx, pair_info in enumerate(pair_list):
                if pair_info[1] == current:
                    picked = jnp.take(gathered_back[pair_info[0]], targets[pair_idx], axis=0)
                    products = jnp.einsum(
                        "snb,sba->sna", picked, blocks[pair_idx], preferred_element_type=jnp.float32
                    )
                    partial_value = partial_value + spread_rows(
                        col_keys[pair_idx], col_width, products
                    )
            summed = deliver_cols(partial_value, col_values)
            residual = residual - summed
        reduced = residual.astype(jnp.bfloat16)
        answer = jnp.dot(reduced, inverse_diag[current, 0, 0], preferred_element_type=jnp.float32)
        solutions[current] = answer
        if current > 0:
            outgoing = answer.astype(jnp.bfloat16)[None]
            gathered_back[current] = lax.all_gather(outgoing, "row", axis=0, tiled=True)
    return jnp.stack(solutions)[:, None, None]


def solution(mesh):
    placed = (
        P(None, "row", "col", None, None),
        P(None, "row", "col", None, None),
        P(None, "row", "col", None, None),
        P(None, "row", "col"),
        P(None, "row", "col"),
    )
    return jax.shard_map(
        shards,
        mesh=mesh,
        in_specs=placed,
        out_specs=P(None, "row", "col", None, None),
        check_vma=False,
    )
```

profile of v0, /device:TPU:32, one launch (start us, length us, event | category | flops | bytes accessed | tf_op | source)
XLA Modules:
  0.0 198.4 jit_solution(18369573394711938383)
XLA Ops:
  0.0 1.1 fusion.101
  1.1 1.1 broadcast_in_dim.67
  2.2 7.3 %all-to-all-start = ((bf16[32,1,64,256]{3,2,1,0:T(8,128)(2,1)}), bf16[32,1,64,256]{3,2,1,0:T(8,128)(2,1)S(1)}, u32[]{:S(2)}, u32[]{:S(2)}) async-start(bf16[32,1,64,256]{3,2,1,0:T(8,128)(2,1)} %broadcast_in_dim.67), calls=%async_computation | async-start | bytes 2097152 | tf_op jit(solution)/shard_map/all_to_all | solution.py:23
  9.6 0.7 compare_and_fusion.3
  10.3 0.7 broadcast_subtract_fusion.1
  10.9 0.7 broadcast_subtract_fusion
  11.6 0.7 compare_and_fusion.1
  12.4 14.0 %all-to-all-done = bf16[32,1,64,256]{3,2,1,0:T(8,128)(2,1)S(1)} async-done(((bf16[32,1,64,256]{3,2,1,0:T(8,128)(2,1)}), bf16[32,1,64,256]{3,2,1,0:T(8,128)(2,1)S(1)}, u32[]{:S(2)}, u32[]{:S(2)}) %all-to-all-start) | async-done | bytes 1048608 | tf_op jit(solution)/shard_map/all_to_all | solution.py:23
  26.3 0.6 gather_fusion
  26.9 1.9 fusion.10
  28.8 0.1 pad.9
  28.9 0.6 copy.42
  29.5 0.5 convolution_convert_fusion.1
  30.0 0.6 slice_reduce_fusion.5
  30.6 14.8 %collective-permute-start.1 = (bf16[64,256]{1,0:T(8,128)(2,1)S(1)}, bf16[64,256]{1,0:T(8,128)(2,1)S(1)}, u32[]{:S(2)}, u32[]{:S(2)}) collective-permute-start(bf16[64,256]{1,0:T(8,128)(2,1)S(1)} %convert_element_type.159), channel_id=1, source_target_pairs={{0,256},{32,288},{64,320},{96,352},{128,384},{160,416},{192,448},{... | collective-permute-start | bytes 98312 | tf_op jit(solution)/shard_map/ppermute | solution.py:12
  45.5 2.9 %collective-permute-start.2 = (bf16[64,256]{1,0:T(8,128)(2,1)S(1)}, bf16[64,256]{1,0:T(8,128)(2,1)S(1)}, u32[]{:S(2)}, u32[]{:S(2)}) collective-permute-start(bf16[64,256]{1,0:T(8,128)(2,1)S(1)} %convert_element_type.161), channel_id=1, source_target_pairs={{0,480},{32,0},{64,32},{96,64},{128,96},{160,128},{192,160},{224,1... | collective-permute-start | bytes 98312 | tf_op jit(solution)/shard_map/ppermute | solution.py:12
  48.4 2.9 %collective-permute-start = (bf16[64,256]{1,0:T(8,128)(2,1)S(1)}, bf16[64,256]{1,0:T(8,128)(2,1)S(1)}, u32[]{:S(2)}, u32[]{:S(2)}) collective-permute-start(bf16[64,256]{1,0:T(8,128)(2,1)S(1)} %convert_element_type.157), channel_id=1, source_target_pairs={{0,32},{32,64},{64,96},{96,128},{128,160},{160,192},{192,224},{224... | collective-permute-start | bytes 98312 | tf_op jit(solution)/shard_map/ppermute | solution.py:12
  51.3 0.2 fusion.62
  51.6 2.6 %collective-permute-done = bf16[64,256]{1,0:T(8,128)(2,1)S(1)} collective-permute-done((bf16[64,256]{1,0:T(8,128)(2,1)S(1)}, bf16[64,256]{1,0:T(8,128)(2,1)S(1)}, u32[]{:S(2)}, u32[]{:S(2)}) %collective-permute-start) | collective-permute-done | bytes 32800 | tf_op jit(solution)/shard_map/ppermute | solution.py:12
  54.2 0.2 fusion.102
  54.4 1.1 broadcast_in_dim.68
  55.5 4.1 %all-to-all-start.1 = ((bf16[32,1,64,256]{3,2,1,0:T(8,128)(2,1)}), bf16[32,1,64,256]{3,2,1,0:T(8,128)(2,1)S(1)}, u32[]{:S(2)}, u32[]{:S(2)}) async-start(bf16[32,1,64,256]{3,2,1,0:T(8,128)(2,1)} %broadcast_in_dim.68), calls=%async_computation.1 | async-start | bytes 2097152 | tf_op jit(solution)/shard_map/all_to_all | solution.py:23
  59.6 0.6 gather_fusion.1
  60.2 1.8 fusion.6
  62.1 0.8 fusion.25
  62.9 13.5 %all-to-all-done.1 = bf16[32,1,64,256]{3,2,1,0:T(8,128)(2,1)S(1)} async-done(((bf16[32,1,64,256]{3,2,1,0:T(8,128)(2,1)}), bf16[32,1,64,256]{3,2,1,0:T(8,128)(2,1)S(1)}, u32[]{:S(2)}, u32[]{:S(2)}) %all-to-all-start.1) | async-done | bytes 1048608 | tf_op jit(solution)/shard_map/all_to_all | solution.py:23
  76.3 0.6 gather_fusion.2
  76.9 1.8 fusion.2
  78.8 0.8 fusion.18
  79.6 0.2 fusion.100
  79.9 6.3 %collective-permute-start.4 = (bf16[64,256]{1,0:T(8,128)(2,1)S(1)}, bf16[64,256]{1,0:T(8,128)(2,1)S(1)}, u32[]{:S(2)}, u32[]{:S(2)}) collective-permute-start(bf16[64,256]{1,0:T(8,128)(2,1)S(1)} %bitcast.224), channel_id=1, source_target_pairs={{0,256},{32,288},{64,320},{96,352},{128,384},{160,416},{192,448},{... | collective-permute-start | bytes 98312 | tf_op jit(solution)/shard_map/ppermute | solution.py:12
  86.2 5.1 %collective-permute-start.5 = (bf16[64,256]{1,0:T(8,128)(2,1)S(1)}, bf16[64,256]{1,0:T(8,128)(2,1)S(1)}, u32[]{:S(2)}, u32[]{:S(2)}) collective-permute-start(bf16[64,256]{1,0:T(8,128)(2,1)S(1)} %bitcast.223), channel_id=1, source_target_pairs={{0,480},{32,0},{64,32},{96,64},{128,96},{160,128},{192,160},{224,1... | collective-permute-start | bytes 98312 | tf_op jit(solution)/shard_map/ppermute | solution.py:12
  91.3 1.9 collective-permute-start.3
  93.3 1.1 collective-permute-done.4
  94.4 2.7 %collective-permute-done.3 = bf16[64,256]{1,0:T(8,128)(2,1)S(1)} collective-permute-done((bf16[64,256]{1,0:T(8,128)(2,1)S(1)}, bf16[64,256]{1,0:T(8,128)(2,1)S(1)}, u32[]{:S(2)}, u32[]{:S(2)}) %collective-permute-start.3) | collective-permute-done | bytes 32800 | tf_op jit(solution)/shard_map/ppermute | solution.py:12
  97.1 0.3 fusion.103
  97.5 30.1 %all-gather = bf16[1024,256]{1,0:T(8,128)(2,1)S(1)} all-gather(bf16[64,256]{1,0:T(8,128)(2,1)S(1)} %get-tuple-element.50), channel_id=2, replica_groups=mesh['row'=16,'col'=32] {'row'}, dimensions={0}, use_global_device_ids=true | all-gather | bytes 557056 | tf_op jit(solution)/shard_map/all_gather | solution.py:143
  127.5 0.6 gather_fusion.5
  128.1 0.6 gather_fusion.3
  128.7 1.7 fusion.4
  130.4 0.1 slice_bitcast_fusion
  130.5 1.7 fusion
  132.2 0.1 pad.12
  132.3 0.6 copy.47
  132.9 0.5 convolution_convert_fusion
  133.4 0.6 slice_reduce_fusion.2
  134.0 3.4 %collective-permute-start.7 = (bf16[64,256]{1,0:T(8,128)(2,1)S(1)}, bf16[64,256]{1,0:T(8,128)(2,1)S(1)}, u32[]{:S(2)}, u32[]{:S(2)}) collective-permute-start(bf16[64,256]{1,0:T(8,128)(2,1)S(1)} %convert_element_type.180), channel_id=1, source_target_pairs={{0,16},{1,17},{2,18},{3,19},{4,20},{5,21},{6,22},{7,23},{8,24},{9,... | collective-permute-start | bytes 98312 | tf_op jit(solution)/shard_map/ppermute | solution.py:12
  137.4 1.9 collective-permute-start.8
  139.3 2.4 %collective-permute-start.6 = (bf16[64,256]{1,0:T(8,128)(2,1)S(1)}, bf16[64,256]{1,0:T(8,128)(2,1)S(1)}, u32[]{:S(2)}, u32[]{:S(2)}) collective-permute-start(bf16[64,256]{1,0:T(8,128)(2,1)S(1)} %convert_element_type.178), channel_id=1, source_target_pairs={{0,1},{1,2},{2,3},{3,4},{4,5},{5,6},{6,7},{7,8},{8,9},{9,10},{10,1... | collective-permute-start | bytes 98312 | tf_op jit(solution)/shard_map/ppermute | solution.py:12
  141.8 0.8 fusion.20
  142.6 0.2 fusion.61
  142.8 5.1 %collective-permute-done.6 = bf16[64,256]{1,0:T(8,128)(2,1)S(1)} collective-permute-done((bf16[64,256]{1,0:T(8,128)(2,1)S(1)}, bf16[64,256]{1,0:T(8,128)(2,1)S(1)}, u32[]{:S(2)}, u32[]{:S(2)}) %collective-permute-start.6) | collective-permute-done | bytes 32800 | tf_op jit(solution)/shard_map/ppermute | solution.py:12
  147.9 0.1 fusion.108
  148.0 30.0 %all-gather.1 = bf16[1024,256]{1,0:T(8,128)(2,1)S(1)} all-gather(bf16[64,256]{1,0:T(8,128)(2,1)S(1)} %get-tuple-element.52), channel_id=3, replica_groups=mesh['row'=16,'col'=32] {'row'}, dimensions={0}, use_global_device_ids=true | all-gather | bytes 557056 | tf_op jit(solution)/shard_map/all_gather | solution.py:143
  178.1 0.6 gather_fusion.4
  178.6 1.7 fusion.8
  180.4 0.8 fusion.22
  181.2 0.1 fusion.39
  181.3 1.9 collective-permute-start.9
  183.2 7.0 %collective-permute-start.11 = (bf16[64,256]{1,0:T(8,128)(2,1)S(1)}, bf16[64,256]{1,0:T(8,128)(2,1)S(1)}, u32[]{:S(2)}, u32[]{:S(2)}) collective-permute-start(bf16[64,256]{1,0:T(8,128)(2,1)S(1)} %get-tuple-element.26), channel_id=1, source_target_pairs={{0,31},{1,0},{2,1},{3,2},{4,3},{5,4},{6,5},{7,6},{8,7},{9,8},{10,9... | collective-permute-start | bytes 98312 | tf_op jit(solution)/shard_map/ppermute | solution.py:12
  190.2 1.9 collective-permute-start.10
  192.2 5.4 %collective-permute-done.10 = bf16[64,256]{1,0:T(8,128)(2,1)S(1)} collective-permute-done((bf16[64,256]{1,0:T(8,128)(2,1)S(1)}, bf16[64,256]{1,0:T(8,128)(2,1)S(1)}, u32[]{:S(2)}, u32[]{:S(2)}) %collective-permute-start.10) | collective-permute-done | bytes 32800 | tf_op jit(solution)/shard_map/ppermute | solution.py:12
  197.5 0.2 convolution_bitcast_fusion
  197.7 0.7 maximum_bitcast_fusion
  (34 shorter events, 0.4 us)
Async XLA Ops:
  2.2 24.1 %all-to-all-start = ((bf16[32,1,64,256]{3,2,1,0:T(8,128)(2,1)}), bf16[32,1,64,256]{3,2,1,0:T(8,128)(2,1)S(1)}, u32[]{:S(2)}, u32[]{:S(2)}) async-start(bf16[32,1,64,256]{3,2,1,0:T(8,128)(2,1)} %broadcast_in_dim.67), calls=%async_computation | async-start | bytes 2097152 | tf_op jit(solution)/shard_map/all_to_all | solution.py:23
  26.9 27.3 %copy-start = (bf16[3,1,1,256,256]{4,3,2,1,0:T(8,128)(2,1)S(1)}, bf16[3,1,1,256,256]{4,3,2,1,0:T(8,128)(2,1)}, u32[]{:S(2)}) copy-start(bf16[3,1,1,256,256]{4,3,2,1,0:T(8,128)(2,1)} %param.10) | copy-start | bytes 1179652
  26.9 27.3 %copy-start.1 = (f32[3,1,1,64,256]{4,3,2,1,0:T(8,128)S(1)}, f32[3,1,1,64,256]{4,3,2,1,0:T(8,128)}, u32[]{:S(2)}) copy-start(f32[3,1,1,64,256]{4,3,2,1,0:T(8,128)} %param.9) | copy-start | bytes 589828
  30.6 20.9 %collective-permute-start.1 = (bf16[64,256]{1,0:T(8,128)(2,1)S(1)}, bf16[64,256]{1,0:T(8,128)(2,1)S(1)}, u32[]{:S(2)}, u32[]{:S(2)}) collective-permute-start(bf16[64,256]{1,0:T(8,128)(2,1)S(1)} %convert_element_type.159), channel_id=1, source_target_pairs={{0,256},{32,288},{64,320},{96,352},{128,384},{160,416},{192,448},{... | collective-permute-start | bytes 98312 | tf_op jit(solution)/shard_map/ppermute | solution.py:12
  45.5 6.1 %collective-permute-start.2 = (bf16[64,256]{1,0:T(8,128)(2,1)S(1)}, bf16[64,256]{1,0:T(8,128)(2,1)S(1)}, u32[]{:S(2)}, u32[]{:S(2)}) collective-permute-start(bf16[64,256]{1,0:T(8,128)(2,1)S(1)} %convert_element_type.161), channel_id=1, source_target_pairs={{0,480},{32,0},{64,32},{96,64},{128,96},{160,128},{192,160},{224,1... | collective-permute-start | bytes 98312 | tf_op jit(solution)/shard_map/ppermute | solution.py:12
  48.4 5.8 %collective-permute-start = (bf16[64,256]{1,0:T(8,128)(2,1)S(1)}, bf16[64,256]{1,0:T(8,128)(2,1)S(1)}, u32[]{:S(2)}, u32[]{:S(2)}) collective-permute-start(bf16[64,256]{1,0:T(8,128)(2,1)S(1)} %convert_element_type.157), channel_id=1, source_target_pairs={{0,32},{32,64},{64,96},{96,128},{128,160},{160,192},{192,224},{224... | collective-permute-start | bytes 98312 | tf_op jit(solution)/shard_map/ppermute | solution.py:12
  55.5 20.8 %all-to-all-start.1 = ((bf16[32,1,64,256]{3,2,1,0:T(8,128)(2,1)}), bf16[32,1,64,256]{3,2,1,0:T(8,128)(2,1)S(1)}, u32[]{:S(2)}, u32[]{:S(2)}) async-start(bf16[32,1,64,256]{3,2,1,0:T(8,128)(2,1)} %broadcast_in_dim.68), calls=%async_computation.1 | async-start | bytes 2097152 | tf_op jit(solution)/shard_map/all_to_all | solution.py:23
  79.9 14.5 %collective-permute-start.4 = (bf16[64,256]{1,0:T(8,128)(2,1)S(1)}, bf16[64,256]{1,0:T(8,128)(2,1)S(1)}, u32[]{:S(2)}, u32[]{:S(2)}) collective-permute-start(bf16[64,256]{1,0:T(8,128)(2,1)S(1)} %bitcast.224), channel_id=1, source_target_pairs={{0,256},{32,288},{64,320},{96,352},{128,384},{160,416},{192,448},{... | collective-permute-start | bytes 98312 | tf_op jit(solution)/shard_map/ppermute | solution.py:12
  86.2 8.2 %collective-permute-start.5 = (bf16[64,256]{1,0:T(8,128)(2,1)S(1)}, bf16[64,256]{1,0:T(8,128)(2,1)S(1)}, u32[]{:S(2)}, u32[]{:S(2)}) collective-permute-start(bf16[64,256]{1,0:T(8,128)(2,1)S(1)} %bitcast.223), channel_id=1, source_target_pairs={{0,480},{32,0},{64,32},{96,64},{128,96},{160,128},{192,160},{224,1... | collective-permute-start | bytes 98312 | tf_op jit(solution)/shard_map/ppermute | solution.py:12
  91.3 5.8 %collective-permute-start.3 = (bf16[64,256]{1,0:T(8,128)(2,1)S(1)}, bf16[64,256]{1,0:T(8,128)(2,1)S(1)}, u32[]{:S(2)}, u32[]{:S(2)}) collective-permute-start(bf16[64,256]{1,0:T(8,128)(2,1)S(1)} %bitcast.222), channel_id=1, source_target_pairs={{0,32},{32,64},{64,96},{96,128},{128,160},{160,192},{192,224},{224... | collective-permute-start | bytes 98312 | tf_op jit(solution)/shard_map/ppermute | solution.py:12
  134.0 8.8 %collective-permute-start.7 = (bf16[64,256]{1,0:T(8,128)(2,1)S(1)}, bf16[64,256]{1,0:T(8,128)(2,1)S(1)}, u32[]{:S(2)}, u32[]{:S(2)}) collective-permute-start(bf16[64,256]{1,0:T(8,128)(2,1)S(1)} %convert_element_type.180), channel_id=1, source_target_pairs={{0,16},{1,17},{2,18},{3,19},{4,20},{5,21},{6,22},{7,23},{8,24},{9,... | collective-permute-start | bytes 98312 | tf_op jit(solution)/shard_map/ppermute | solution.py:12
  137.4 5.4 %collective-permute-start.8 = (bf16[64,256]{1,0:T(8,128)(2,1)S(1)}, bf16[64,256]{1,0:T(8,128)(2,1)S(1)}, u32[]{:S(2)}, u32[]{:S(2)}) collective-permute-start(bf16[64,256]{1,0:T(8,128)(2,1)S(1)} %convert_element_type.182), channel_id=1, source_target_pairs={{0,31},{1,0},{2,1},{3,2},{4,3},{5,4},{6,5},{7,6},{8,7},{9,8},{10,9... | collective-permute-start | bytes 98312 | tf_op jit(solution)/shard_map/ppermute | solution.py:12
  139.3 8.6 %collective-permute-start.6 = (bf16[64,256]{1,0:T(8,128)(2,1)S(1)}, bf16[64,256]{1,0:T(8,128)(2,1)S(1)}, u32[]{:S(2)}, u32[]{:S(2)}) collective-permute-start(bf16[64,256]{1,0:T(8,128)(2,1)S(1)} %convert_element_type.178), channel_id=1, source_target_pairs={{0,1},{1,2},{2,3},{3,4},{4,5},{5,6},{6,7},{7,8},{8,9},{9,10},{10,1... | collective-permute-start | bytes 98312 | tf_op jit(solution)/shard_map/ppermute | solution.py:12
  181.3 10.8 %collective-permute-start.9 = (bf16[64,256]{1,0:T(8,128)(2,1)S(1)}, bf16[64,256]{1,0:T(8,128)(2,1)S(1)}, u32[]{:S(2)}, u32[]{:S(2)}) collective-permute-start(bf16[64,256]{1,0:T(8,128)(2,1)S(1)} %get-tuple-element.25), channel_id=1, source_target_pairs={{0,1},{1,2},{2,3},{3,4},{4,5},{5,6},{6,7},{7,8},{8,9},{9,10},{10,1... | collective-permute-start | bytes 98312 | tf_op jit(solution)/shard_map/ppermute | solution.py:12
  183.2 8.9 %collective-permute-start.11 = (bf16[64,256]{1,0:T(8,128)(2,1)S(1)}, bf16[64,256]{1,0:T(8,128)(2,1)S(1)}, u32[]{:S(2)}, u32[]{:S(2)}) collective-permute-start(bf16[64,256]{1,0:T(8,128)(2,1)S(1)} %get-tuple-element.26), channel_id=1, source_target_pairs={{0,31},{1,0},{2,1},{3,2},{4,3},{5,4},{6,5},{7,6},{8,7},{9,8},{10,9... | collective-permute-start | bytes 98312 | tf_op jit(solution)/shard_map/ppermute | solution.py:12
  190.2 7.3 %collective-permute-start.10 = (bf16[64,256]{1,0:T(8,128)(2,1)S(1)}, bf16[64,256]{1,0:T(8,128)(2,1)S(1)}, u32[]{:S(2)}, u32[]{:S(2)}) collective-permute-start(bf16[64,256]{1,0:T(8,128)(2,1)S(1)} %get-tuple-element.27), channel_id=1, source_target_pairs={{0,16},{1,17},{2,18},{3,19},{4,20},{5,21},{6,22},{7,23},{8,24},{9,... | collective-permute-start | bytes 98312 | tf_op jit(solution)/shard_map/ppermute | solution.py:12
where the time goes:
time: 199 us; the launch traced here: 198 us
  starting transfers between devices  63.9 us (32%)
  blocking collectives  60.1 us (30%)
  waiting for transfers between devices  44.4 us (22%)
  matrix products  16.8 us (8%)
  local copies, waits for them, and re-layouts  8.54 us (4%)
  other arithmetic  4.13 us (2%)
    all_gather x2, blocking collectives, shards(): gathered_back[current] = lax.all_gather(outgoing, 'row', axis=0, tiled=True)  60.1 us
    ppermute x12, starting transfers between devices, from_behind(): return lax.ppermute(value, axis, pairs)  52.6 us
    all_to_all x2, waiting for transfers between devices, from_everyone(): lax.all_to_all(jnp.broadcast_to(value[None], (count, *value.shape)), axis...  27.4 us
    ppermute x12, waiting for transfers between devices, from_behind(): return lax.ppermute(value, axis, pairs)  17 us
    all_to_all x2, starting transfers between devices, from_everyone(): lax.all_to_all(jnp.broadcast_to(value[None], (count, *value.shape)), axis...  11.4 us
    dot_general x3, matrix products, shards(): jnp.einsum('snb,sab->sna', picked, blocks[pair_idx], preferred_element_ty...  5.58 us
    dot_general x3, matrix products, shards(): jnp.einsum('snb,sba->sna', picked, blocks[pair_idx], preferred_element_ty...  5.14 us
    dot_general x6, matrix products, spread_rows(): jnp.dot(onehot, flattened, precision=lax.Precision.HIGHEST, preferred_ele...  4.19 us
  transfers between devices with their start and end apart: 14, of which 7 were waited for; matrix products, arithmetic and copies ran while one was open for 4% of the time, Pallas kernels for 0%

commit v1 on v0

v1 whole, which is shorter than its diff:
```python
import jax
import jax.numpy as jnp
from jax import lax
from jax.experimental import pallas as pl
from jax.experimental.pallas import tpu as pltpu
from jax.sharding import PartitionSpec as P

VMEM = pl.BlockSpec(memory_space=pltpu.VMEM)
SMEM = pl.BlockSpec(memory_space=pltpu.SMEM)
NT = (((1,), (1,)), ((), ()))
NN = (((1,), (0,)), ((), ()))
BF = jnp.bfloat16
F32 = jnp.float32


def pair_of(i, n):
    return i + 1 - 2 * (i % 2)


def cross_of(i, n):
    return (i - 1 + 2 * (i % 2) + n) % n


def far_of(i, n):
    return (i + n // 2) % n


def swap(value, axis, partner):
    n = lax.axis_size(axis)
    return lax.ppermute(value, axis, [(i, partner(i, n)) for i in range(n)])


def far_groups(n):
    half = n // 2
    return [[i, i + 1, i + half, i + half + 1] for i in range(0, half, 2)]


def gather_far(value, axis):
    return lax.all_gather(value, axis, axis_index_groups=far_groups(lax.axis_size(axis)))


def group_place(i, n):
    return i % 2 + 2 * (i // (n // 2))


def call(body, out_shape, in_specs, args, flops, moved, scratch=(), name=None, aliases=None, out_specs=None):
    return pl.pallas_call(
        body,
        out_shape=out_shape,
        in_specs=in_specs,
        out_specs=out_specs if out_specs is not None else jax.tree.map(lambda _: VMEM, out_shape),
        scratch_shapes=list(scratch),
        input_output_aliases=aliases or {},
        compiler_params=pltpu.CompilerParams(vmem_limit_bytes=16 * 2**20),
        cost_estimate=pl.CostEstimate(flops=flops, bytes_accessed=moved, transcendentals=0),
        name=name,
    )(*args)


def f32_like(x):
    return jax.ShapeDtypeStruct(x.shape, F32)


def bf_like(x):
    return jax.ShapeDtypeStruct(x.shape, BF)


def masked_sum(products, keys, key):
    total = None
    for s, k in enumerate(keys):
        term = jnp.where(k == key, products[s], 0.0)
        total = term if total is None else total + term
    return total


def product_body(kind, pair_idx, n_row, n_col, slots, add, finish):
    def body(*refs):
        targets, sources, blocks, *rest = refs
        count = 2 if kind == "fwd" else 4
        panels, rest = rest[:count], rest[count:]
        if add:
            base, rest = rest[0], rest[1:]
        outs, held, products = rest[:-2], rest[-2], rest[-1]
        r = lax.axis_index("row")
        c = lax.axis_index("col")
        if kind == "fwd":
            held[0:4] = panels[0][...]
            held[4] = panels[1][...]
        else:
            for i in range(4):
                held[i] = panels[i][...]
        keys = []
        for s in range(slots):
            t = targets[pair_idx, 0, s]
            e = sources[pair_idx, 0, s]
            if kind == "fwd":
                place = jnp.where(e == cross_of(c, n_col), 4, group_place(e, n_col))
                keys.append(t)
            else:
                place = jnp.where(
                    t == r, 0, jnp.where(t == pair_of(r, n_row), 1, jnp.where(t == far_of(r, n_row), 3, 2))
                )
                keys.append(e)
            products[s] = lax.dot_general(
                held[place], blocks[pair_idx, 0, s], NT if kind == "fwd" else NN, preferred_element_type=F32
            )
        me, n = (r, n_row) if kind == "fwd" else (c, n_col)
        for i, key in enumerate((me, pair_of(me, n), cross_of(me, n), far_of(me, n))):
            total = masked_sum(products, keys, key)
            if add:
                total = total + base[i]
            if finish:
                if kind == "fwd" or i in (0, 2):
                    outs[i if kind == "fwd" else i // 2][...] = total.astype(BF)
                else:
                    outs[2][i // 2] = total.astype(BF)
            else:
                outs[0][i] = total

    return body


def products(kind, pair_idx, tables, blocks, panels, base, finish):
    n_row, n_col = lax.axis_size("row"), lax.axis_size("col")
    slots, size = blocks.shape[2], blocks.shape[3]
    shape = panels[-1].shape
    panel = jax.ShapeDtypeStruct(shape, BF)
    if not finish:
        out = [jax.ShapeDtypeStruct((4, *shape), F32)]
    elif kind == "fwd":
        out = [panel] * 4
    else:
        out = [panel, panel, jax.ShapeDtypeStruct((2, *shape), BF)]
    args = [*tables, blocks, *panels] + ([base] if base is not None else [])
    return call(
        product_body(kind, pair_idx, n_row, n_col, slots, base is not None, finish),
        out,
        [SMEM, SMEM] + [VMEM] * (len(args) - 2),
        args,
        2 * slots * shape[0] * size * size,
        2 * slots * size * size,
        [pltpu.VMEM((5, *shape), BF), pltpu.VMEM((slots, *shape), F32)],
        f"{kind}{pair_idx}",
    )


def first_body(rhs, inverse, y_out, send_out):
    y = lax.dot_general(rhs[0, 0, 0].astype(BF), inverse[0, 0, 0], NT, preferred_element_type=F32)
    y_out[...] = y
    send_out[...] = y.astype(BF)


def forward_body(level, last):
    def body(rhs, inverse, own, pair, cross, far, *outs):
        total = own[...].astype(F32) + pair[...].astype(F32) + cross[...].astype(F32) + far[...].astype(F32)
        y = lax.dot_general(
            (rhs[level, 0, 0] - total).astype(BF), inverse[level, 0, 0], NT, preferred_element_type=F32
        )
        if last:
            y = lax.dot_general(y.astype(BF), inverse[level, 0, 0], NN, preferred_element_type=F32)
        outs[0][...] = y
        outs[1][...] = y.astype(BF)

    return body


def backward_body(level, n_col):
    def body(y, inverse, own, cross, group, *outs):
        c = lax.axis_index("col")
        total = (
            own[...].astype(F32)
            + cross[...].astype(F32)
            + group[group_place(pair_of(c, n_col), n_col), 0].astype(F32)
            + group[group_place(far_of(c, n_col), n_col), 1].astype(F32)
        )
        z = lax.dot_general((y[...] - total).astype(BF), inverse[level, 0, 0], NN, preferred_element_type=F32)
        outs[0][...] = z
        if level > 0:
            outs[1][...] = z.astype(BF)

    return body


def shards(rhs, inverse, blocks, targets, sources):
    n_col = lax.axis_size("col")
    tables = (targets, sources)
    panel = jax.ShapeDtypeStruct(rhs.shape[3:], F32)
    solve_flops = 2 * panel.shape[0] * panel.shape[1] ** 2

    def gather_cols(value):
        cross = swap(value, "col", cross_of)
        return [gather_far(value, "col"), cross]

    def gather_rows(value):
        far = swap(value, "row", far_of)
        pair = swap(value, "row", pair_of)
        cross = swap(value, "row", cross_of)
        return [value, pair, cross, far]

    def scatter_rows(parts):
        own, pair, cross, far = parts
        far = swap(far, "row", far_of)
        pair = swap(pair, "row", pair_of)
        cross = swap(cross, "row", cross_of)
        return [own, pair, cross, far]

    def scatter_cols(parts):
        own, cross, group = parts
        cross = swap(cross, "col", cross_of)
        return [own, cross, gather_far(group, "col")]

    y0, s0 = call(first_body, [panel, bf_like(panel)], [VMEM] * 2, (rhs, inverse), solve_flops, 2**18, name="y0")
    g0 = gather_cols(s0)
    parts = scatter_rows(products("fwd", 0, tables, blocks, g0, None, True))
    base2 = products("fwd", 1, tables, blocks, g0, None, False)[0]
    y1, s1 = call(
        forward_body(1, False), [panel, bf_like(panel)], [VMEM] * 6, (rhs, inverse, *parts), solve_flops, 2**18, name="y1"
    )
    g1 = gather_cols(s1)
    parts = scatter_rows(products("fwd", 2, tables, blocks, g1, base2, True))
    z2, b2 = call(
        forward_body(2, True), [panel, bf_like(panel)], [VMEM] * 6, (rhs, inverse, *parts), 2 * solve_flops, 2**18, name="z2"
    )
    h2 = gather_rows(b2)
    parts = scatter_cols(products("bwd", 2, tables, blocks, h2, None, True))
    base0 = products("bwd", 1, tables, blocks, h2, None, False)[0]
    z1, b1 = call(
        backward_body(1, n_col), [panel, bf_like(panel)], [VMEM] * 5, (y1, inverse, *parts), solve_flops, 2**18, name="z1"
    )
    h1 = gather_rows(b1)
    parts = scatter_cols(products("bwd", 0, tables, blocks, h1, base0, True))
    z0 = call(backward_body(0, n_col), [panel], [VMEM] * 5, (y0, inverse, *parts), solve_flops, 2**18, name="z0")[0]
    return jnp.stack([z0, z1, z2])[:, None, None]


def solution(mesh):
    placed = (
        P(None, "row", "col", None, None),
        P(None, "row", "col", None, None),
        P(None, "row", "col", None, None),
        P(None, "row", "col"),
        P(None, "row", "col"),
    )
    return jax.shard_map(
        shards,
        mesh=mesh,
        in_specs=placed,
        out_specs=P(None, "row", "col", None, None),
        check_vma=False,
    )
```

time: 199 us -> 150 us (0.75)
  the two profiles are of different devices: /device:TPU:32 before, /device:TPU:1 now
where the time goes in v1:
time: 150 us
  starting transfers between devices  71.1 us (47%)
  blocking collectives  38.9 us (26%)
  waiting for transfers between devices  25.9 us (17%)
  Pallas kernels  7.24 us (5%)
  local copies, waits for them, and re-layouts  5.41 us (4%)
    ppermute x16, starting transfers between devices, swap(): return lax.ppermute(value, axis, [(i, partner(i, n)) for i in range(n)])  71.1 us
    all_gather x4, blocking collectives, gather_far(): lax.all_gather(value, axis, axis_index_groups=far_groups(lax.axis_size(ax...  38.9 us
    ppermute x16, waiting for transfers between devices, swap(): return lax.ppermute(value, axis, [(i, partner(i, n)) for i in range(n)])  25.9 us
    pallas_call x11, Pallas kernels, call(): pl.pallas_call(body, out_shape=out_shape, in_specs=in_specs, out_specs=ou...  7.24 us
    unnamed x16, local copies, waits for them, and re-layouts  5.41 us
  transfers between devices with their start and end apart: 16, of which 4 were waited for; matrix products, arithmetic and copies ran while one was open for 0% of the time, Pallas kernels for 1%

profile of v1, /device:TPU:1, one launch (start us, length us, event | category | flops | bytes accessed | tf_op | source)
XLA Modules:
  0.0 149.5 jit_solution(11405884083635211233)
XLA Ops:
  0.0 0.0 copy-start.2
  0.0 1.0 copy-done.2
  1.0 0.0 copy-start.4
  1.0 0.9 copy-done.4
  1.9 0.2 y0.1
  2.1 4.6 %collective-permute-start = (bf16[64,256]{1,0:T(8,128)(2,1)S(1)}, bf16[64,256]{1,0:T(8,128)(2,1)S(1)}, u32[]{:S(2)}, u32[]{:S(2)}) collective-permute-start(bf16[64,256]{1,0:T(8,128)(2,1)S(1)} %get-tuple-element.28), channel_id=1, source_target_pairs={{0,31},{1,2},{2,1},{3,4},{4,3},{5,6},{6,5},{7,8},{8,7},{9,10},{10,... | collective-permute-start | bytes 98312 | tf_op jit(solution)/shard_map/ppermute | solution.py:30
  6.7 10.9 %all-gather = bf16[256,256]{1,0:T(8,128)(2,1)S(1)} all-gather(bf16[64,256]{1,0:T(8,128)(2,1)S(1)} %get-tuple-element.28), channel_id=2, replica_groups={{0,1,16,17},{2,3,18,19},{4,5,20,21},{6,7,22,23},{8,9,24,25},{10,11,26,2..., dimensions={0}, use_global_device_ids=true | all-gather | bytes 163840 | tf_op jit(solution)/shard_map/all_gather | solution.py:39
  17.6 0.0 collective-permute-done.refs_4_
  17.6 0.0 copy-start
  17.6 2.1 %copy-done = bf16[3,1,10,256,256]{4,3,2,1,0:T(8,128)(2,1)S(1)} copy-done((bf16[3,1,10,256,256]{4,3,2,1,0:T(8,128)(2,1)S(1)}, bf16[3,1,10,256,256]{4,3,2,1,0:T(8,128)(2,1)}, u32[]{:S(2)}) %copy-start) | copy-done | bytes 3932184
  19.7 0.0 copy-start.6
  19.7 0.7 copy-done.6
  20.4 0.0 copy-start.7
  20.4 0.7 copy-done.7
  21.1 0.0 copy-start.3
  21.1 0.0 copy-start.5
  21.1 0.0 copy-start.1
  21.1 1.1 fwd0.1
  22.2 3.0 %collective-permute-start.1 = (bf16[64,256]{1,0:T(8,128)(2,1)S(1)}, bf16[64,256]{1,0:T(8,128)(2,1)S(1)}, u32[]{:S(2)}, u32[]{:S(2)}) collective-permute-start(bf16[64,256]{1,0:T(8,128)(2,1)S(1)} %get-tuple-element.30), channel_id=1, source_target_pairs={{0,32},{32,0},{64,96},{96,64},{128,160},{160,128},{192,224},{224,1... | collective-permute-start | bytes 98312 | tf_op jit(solution)/shard_map/ppermute | solution.py:30
  25.2 10.2 %collective-permute-start.2 = (bf16[64,256]{1,0:T(8,128)(2,1)S(1)}, bf16[64,256]{1,0:T(8,128)(2,1)S(1)}, u32[]{:S(2)}, u32[]{:S(2)}) collective-permute-start(bf16[64,256]{1,0:T(8,128)(2,1)S(1)} %get-tuple-element.31), channel_id=1, source_target_pairs={{0,480},{32,64},{64,32},{96,128},{128,96},{160,192},{192,160},{224... | collective-permute-start | bytes 98312 | tf_op jit(solution)/shard_map/ppermute | solution.py:30
  35.4 6.3 %collective-permute-start.3 = (bf16[64,256]{1,0:T(8,128)(2,1)S(1)}, bf16[64,256]{1,0:T(8,128)(2,1)S(1)}, u32[]{:S(2)}, u32[]{:S(2)}) collective-permute-start(bf16[64,256]{1,0:T(8,128)(2,1)S(1)} %get-tuple-element.32), channel_id=1, source_target_pairs={{0,256},{32,288},{64,320},{96,352},{128,384},{160,416},{192,448},{... | collective-permute-start | bytes 98312 | tf_op jit(solution)/shard_map/ppermute | solution.py:30
  41.7 1.1 fwd1.1.refs_5_
  42.8 0.0 collective-permute-done.1.pair
  42.8 0.0 collective-permute-done.2.cross
  42.9 6.0 %collective-permute-done.3.far = bf16[64,256]{1,0:T(8,128)(2,1)S(1)} collective-permute-done((bf16[64,256]{1,0:T(8,128)(2,1)S(1)}, bf16[64,256]{1,0:T(8,128)(2,1)S(1)}, u32[]{:S(2)}, u32[]{:S(2)}) %collective-permute-start.3) | collective-permute-done | bytes 32800 | tf_op jit(solution)/shard_map/ppermute | solution.py:30
  48.8 0.0 copy-done.3
  48.8 0.0 copy-done.5
  48.8 0.2 y1.1
  49.0 1.9 %collective-permute-start.4 = (bf16[64,256]{1,0:T(8,128)(2,1)S(1)}, bf16[64,256]{1,0:T(8,128)(2,1)S(1)}, u32[]{:S(2)}, u32[]{:S(2)}) collective-permute-start(bf16[64,256]{1,0:T(8,128)(2,1)S(1)} %get-tuple-element.34), channel_id=1, source_target_pairs={{0,31},{1,2},{2,1},{3,4},{4,3},{5,6},{6,5},{7,8},{8,7},{9,10},{10,... | collective-permute-start | bytes 98312 | tf_op jit(solution)/shard_map/ppermute | solution.py:30
  50.9 8.7 %all-gather.1 = bf16[256,256]{1,0:T(8,128)(2,1)S(1)} all-gather(bf16[64,256]{1,0:T(8,128)(2,1)S(1)} %get-tuple-element.34), channel_id=3, replica_groups={{0,1,16,17},{2,3,18,19},{4,5,20,21},{6,7,22,23},{8,9,24,25},{10,11,26,2..., dimensions={0}, use_global_device_ids=true | all-gather | bytes 163840 | tf_op jit(solution)/shard_map/all_gather | solution.py:39
  59.6 0.0 collective-permute-done.4.refs_4_
  59.6 0.0 copy-done.1
  59.6 1.1 fwd2.1
  60.8 1.9 %collective-permute-start.5 = (bf16[64,256]{1,0:T(8,128)(2,1)S(1)}, bf16[64,256]{1,0:T(8,128)(2,1)S(1)}, u32[]{:S(2)}, u32[]{:S(2)}) collective-permute-start(bf16[64,256]{1,0:T(8,128)(2,1)S(1)} %get-tuple-element.36), channel_id=1, source_target_pairs={{0,32},{32,0},{64,96},{96,64},{128,160},{160,128},{192,224},{224,1... | collective-permute-start | bytes 98312 | tf_op jit(solution)/shard_map/ppermute | solution.py:30
  62.7 3.3 %collective-permute-start.6 = (bf16[64,256]{1,0:T(8,128)(2,1)S(1)}, bf16[64,256]{1,0:T(8,128)(2,1)S(1)}, u32[]{:S(2)}, u32[]{:S(2)}) collective-permute-start(bf16[64,256]{1,0:T(8,128)(2,1)S(1)} %get-tuple-element.37), channel_id=1, source_target_pairs={{0,480},{32,64},{64,32},{96,128},{128,96},{160,192},{192,160},{224... | collective-permute-start | bytes 98312 | tf_op jit(solution)/shard_map/ppermute | solution.py:30
  66.0 7.6 %collective-permute-start.7 = (bf16[64,256]{1,0:T(8,128)(2,1)S(1)}, bf16[64,256]{1,0:T(8,128)(2,1)S(1)}, u32[]{:S(2)}, u32[]{:S(2)}) collective-permute-start(bf16[64,256]{1,0:T(8,128)(2,1)S(1)} %get-tuple-element.38), channel_id=1, source_target_pairs={{0,256},{32,288},{64,320},{96,352},{128,384},{160,416},{192,448},{... | collective-permute-start | bytes 98312 | tf_op jit(solution)/shard_map/ppermute | solution.py:30
  73.6 0.0 collective-permute-done.5.pair
  73.6 0.0 collective-permute-done.6.cross
  73.6 5.8 %collective-permute-done.7.far = bf16[64,256]{1,0:T(8,128)(2,1)S(1)} collective-permute-done((bf16[64,256]{1,0:T(8,128)(2,1)S(1)}, bf16[64,256]{1,0:T(8,128)(2,1)S(1)}, u32[]{:S(2)}, u32[]{:S(2)}) %collective-permute-start.7) | collective-permute-done | bytes 32800 | tf_op jit(solution)/shard_map/ppermute | solution.py:30
  79.4 0.3 z2.1
  79.7 2.0 %collective-permute-start.8 = (bf16[64,256]{1,0:T(8,128)(2,1)S(1)}, bf16[64,256]{1,0:T(8,128)(2,1)S(1)}, u32[]{:S(2)}, u32[]{:S(2)}) collective-permute-start(bf16[64,256]{1,0:T(8,128)(2,1)S(1)} %get-tuple-element.39.refs_3_), channel_id=1, source_target_pairs={{0,32},{32,0},{64,96},{96,64},{128,160},{160,128},{192,224},{224,1... | collective-permute-start | bytes 98312 | tf_op jit(solution)/shard_map/ppermute | solution.py:30
  81.7 4.7 %collective-permute-start.9 = (bf16[64,256]{1,0:T(8,128)(2,1)S(1)}, bf16[64,256]{1,0:T(8,128)(2,1)S(1)}, u32[]{:S(2)}, u32[]{:S(2)}) collective-permute-start(bf16[64,256]{1,0:T(8,128)(2,1)S(1)} %get-tuple-element.39.refs_3_), channel_id=1, source_target_pairs={{0,480},{32,64},{64,32},{96,128},{128,96},{160,192},{192,160},{224... | collective-permute-start | bytes 98312 | tf_op jit(solution)/shard_map/ppermute | solution.py:30
  86.5 6.4 %collective-permute-start.10 = (bf16[64,256]{1,0:T(8,128)(2,1)S(1)}, bf16[64,256]{1,0:T(8,128)(2,1)S(1)}, u32[]{:S(2)}, u32[]{:S(2)}) collective-permute-start(bf16[64,256]{1,0:T(8,128)(2,1)S(1)} %get-tuple-element.39.refs_3_), channel_id=1, source_target_pairs={{0,256},{32,288},{64,320},{96,352},{128,384},{160,416},{192,448},{... | collective-permute-start | bytes 98312 | tf_op jit(solution)/shard_map/ppermute | solution.py:30
  92.9 0.0 collective-permute-done.8.refs_4_
  92.9 0.0 collective-permute-done.9.refs_5_
  92.9 6.9 %collective-permute-done.10.refs_6_ = bf16[64,256]{1,0:T(8,128)(2,1)S(1)} collective-permute-done((bf16[64,256]{1,0:T(8,128)(2,1)S(1)}, bf16[64,256]{1,0:T(8,128)(2,1)S(1)}, u32[]{:S(2)}, u32[]{:S(2)}) %collective-permute-start.10) | collective-permute-done | bytes 32800 | tf_op jit(solution)/shard_map/ppermute | solution.py:30
  99.9 1.0 bwd2.1
  100.8 5.4 %collective-permute-start.11 = (bf16[64,256]{1,0:T(8,128)(2,1)S(1)}, bf16[64,256]{1,0:T(8,128)(2,1)S(1)}, u32[]{:S(2)}, u32[]{:S(2)}) collective-permute-start(bf16[64,256]{1,0:T(8,128)(2,1)S(1)} %get-tuple-element.41), channel_id=1, source_target_pairs={{0,31},{1,2},{2,1},{3,4},{4,3},{5,6},{6,5},{7,8},{8,7},{9,10},{10,... | collective-permute-start | bytes 98312 | tf_op jit(solution)/shard_map/ppermute | solution.py:30
  106.2 8.3 %all-gather.2 = bf16[8,64,256]{2,1,0:T(8,128)(2,1)S(1)} all-gather(bf16[2,64,256]{2,1,0:T(8,128)(2,1)S(1)} %get-tuple-element.42), channel_id=4, replica_groups={{0,1,16,17},{2,3,18,19},{4,5,20,21},{6,7,22,23},{8,9,24,25},{10,11,26,2..., dimensions={0}, use_global_device_ids=true | all-gather | bytes 327680 | tf_op jit(solution)/shard_map/all_gather | solution.py:39
  114.5 0.0 collective-permute-done.11.cross
  114.5 0.2 z1.1
  114.7 1.9 %collective-permute-start.12 = (bf16[64,256]{1,0:T(8,128)(2,1)S(1)}, bf16[64,256]{1,0:T(8,128)(2,1)S(1)}, u32[]{:S(2)}, u32[]{:S(2)}) collective-permute-start(bf16[64,256]{1,0:T(8,128)(2,1)S(1)} %get-tuple-element.43.refs_3_), channel_id=1, source_target_pairs={{0,32},{32,0},{64,96},{96,64},{128,160},{160,128},{192,224},{224,1... | collective-permute-start | bytes 98312 | tf_op jit(solution)/shard_map/ppermute | solution.py:30
  116.6 4.1 %collective-permute-start.13 = (bf16[64,256]{1,0:T(8,128)(2,1)S(1)}, bf16[64,256]{1,0:T(8,128)(2,1)S(1)}, u32[]{:S(2)}, u32[]{:S(2)}) collective-permute-start(bf16[64,256]{1,0:T(8,128)(2,1)S(1)} %get-tuple-element.43.refs_3_), channel_id=1, source_target_pairs={{0,480},{32,64},{64,32},{96,128},{128,96},{160,192},{192,160},{224... | collective-permute-start | bytes 98312 | tf_op jit(solution)/shard_map/ppermute | solution.py:30
  120.7 5.2 %collective-permute-start.14 = (bf16[64,256]{1,0:T(8,128)(2,1)S(1)}, bf16[64,256]{1,0:T(8,128)(2,1)S(1)}, u32[]{:S(2)}, u32[]{:S(2)}) collective-permute-start(bf16[64,256]{1,0:T(8,128)(2,1)S(1)} %get-tuple-element.43.refs_3_), channel_id=1, source_target_pairs={{0,256},{32,288},{64,320},{96,352},{128,384},{160,416},{192,448},{... | collective-permute-start | bytes 98312 | tf_op jit(solution)/shard_map/ppermute | solution.py:30
  125.8 1.0 bwd1.1.refs_7_
  126.8 0.0 collective-permute-done.12.refs_4_
  126.8 0.0 collective-permute-done.13.refs_5_
  126.8 7.2 %collective-permute-done.14.refs_6_ = bf16[64,256]{1,0:T(8,128)(2,1)S(1)} collective-permute-done((bf16[64,256]{1,0:T(8,128)(2,1)S(1)}, bf16[64,256]{1,0:T(8,128)(2,1)S(1)}, u32[]{:S(2)}, u32[]{:S(2)}) %collective-permute-start.14) | collective-permute-done | bytes 32800 | tf_op jit(solution)/shard_map/ppermute | solution.py:30
  134.0 1.0 bwd0.1
  135.0 2.6 %collective-permute-start.15 = (bf16[64,256]{1,0:T(8,128)(2,1)S(1)}, bf16[64,256]{1,0:T(8,128)(2,1)S(1)}, u32[]{:S(2)}, u32[]{:S(2)}) collective-permute-start(bf16[64,256]{1,0:T(8,128)(2,1)S(1)} %get-tuple-element.45), channel_id=1, source_target_pairs={{0,31},{1,2},{2,1},{3,4},{4,3},{5,6},{6,5},{7,8},{8,7},{9,10},{10,... | collective-permute-start | bytes 98312 | tf_op jit(solution)/shard_map/ppermute | solution.py:30
  137.7 11.0 %all-gather.3 = bf16[8,64,256]{2,1,0:T(8,128)(2,1)S(1)} all-gather(bf16[2,64,256]{2,1,0:T(8,128)(2,1)S(1)} %get-tuple-element.46), channel_id=5, replica_groups={{0,1,16,17},{2,3,18,19},{4,5,20,21},{6,7,22,23},{8,9,24,25},{10,11,26,2..., dimensions={0}, use_global_device_ids=true | all-gather | bytes 327680 | tf_op jit(solution)/shard_map/all_gather | solution.py:39
  148.7 0.0 collective-permute-done.15.cross
  148.7 0.2 z0.1
  148.8 0.7 maximum_bitcast_fusion
Async XLA Ops:
  0.0 1.0 copy-start.2
  1.0 0.9 copy-start.4
  2.1 15.6 %collective-permute-start = (bf16[64,256]{1,0:T(8,128)(2,1)S(1)}, bf16[64,256]{1,0:T(8,128)(2,1)S(1)}, u32[]{:S(2)}, u32[]{:S(2)}) collective-permute-start(bf16[64,256]{1,0:T(8,128)(2,1)S(1)} %get-tuple-element.28), channel_id=1, source_target_pairs={{0,31},{1,2},{2,1},{3,4},{4,3},{5,6},{6,5},{7,8},{8,7},{9,10},{10,... | collective-permute-start | bytes 98312 | tf_op jit(solution)/shard_map/ppermute | solution.py:30
  17.6 2.1 %copy-start = (bf16[3,1,10,256,256]{4,3,2,1,0:T(8,128)(2,1)S(1)}, bf16[3,1,10,256,256]{4,3,2,1,0:T(8,128)(2,1)}, u32[]{:S(2)}) copy-start(bf16[3,1,10,256,256]{4,3,2,1,0:T(8,128)(2,1)} %refs_2_.11) | copy-start | bytes 11796484
  19.7 0.7 copy-start.6
  20.4 0.7 copy-start.7
  21.1 27.7 %copy-start.3 = (bf16[3,1,1,256,256]{4,3,2,1,0:T(8,128)(2,1)S(1)}, bf16[3,1,1,256,256]{4,3,2,1,0:T(8,128)(2,1)}, u32[]{:S(2)}) copy-start(bf16[3,1,1,256,256]{4,3,2,1,0:T(8,128)(2,1)} %inverse.9) | copy-start | bytes 1179652
  21.1 27.7 %copy-start.5 = (f32[3,1,1,64,256]{4,3,2,1,0:T(8,128)S(1)}, f32[3,1,1,64,256]{4,3,2,1,0:T(8,128)}, u32[]{:S(2)}) copy-start(f32[3,1,1,64,256]{4,3,2,1,0:T(8,128)} %rhs.5) | copy-start | bytes 589828
  21.1 38.5 %copy-start.1 = (bf16[3,1,10,256,256]{4,3,2,1,0:T(8,128)(2,1)S(1)}, bf16[3,1,10,256,256]{4,3,2,1,0:T(8,128)(2,1)}, u32[]{:S(2)}) copy-start(bf16[3,1,10,256,256]{4,3,2,1,0:T(8,128)(2,1)} %refs_2_.11) | copy-start | bytes 11796484
  22.2 20.6 %collective-permute-start.1 = (bf16[64,256]{1,0:T(8,128)(2,1)S(1)}, bf16[64,256]{1,0:T(8,128)(2,1)S(1)}, u32[]{:S(2)}, u32[]{:S(2)}) collective-permute-start(bf16[64,256]{1,0:T(8,128)(2,1)S(1)} %get-tuple-element.30), channel_id=1, source_target_pairs={{0,32},{32,0},{64,96},{96,64},{128,160},{160,128},{192,224},{224,1... | collective-permute-start | bytes 98312 | tf_op jit(solution)/shard_map/ppermute | solution.py:30
  25.2 17.6 %collective-permute-start.2 = (bf16[64,256]{1,0:T(8,128)(2,1)S(1)}, bf16[64,256]{1,0:T(8,128)(2,1)S(1)}, u32[]{:S(2)}, u32[]{:S(2)}) collective-permute-start(bf16[64,256]{1,0:T(8,128)(2,1)S(1)} %get-tuple-element.31), channel_id=1, source_target_pairs={{0,480},{32,64},{64,32},{96,128},{128,96},{160,192},{192,160},{224... | collective-permute-start | bytes 98312 | tf_op jit(solution)/shard_map/ppermute | solution.py:30
  35.4 13.4 %collective-permute-start.3 = (bf16[64,256]{1,0:T(8,128)(2,1)S(1)}, bf16[64,256]{1,0:T(8,128)(2,1)S(1)}, u32[]{:S(2)}, u32[]{:S(2)}) collective-permute-start(bf16[64,256]{1,0:T(8,128)(2,1)S(1)} %get-tuple-element.32), channel_id=1, source_target_pairs={{0,256},{32,288},{64,320},{96,352},{128,384},{160,416},{192,448},{... | collective-permute-start | bytes 98312 | tf_op jit(solution)/shard_map/ppermute | solution.py:30
  49.0 10.6 %collective-permute-start.4 = (bf16[64,256]{1,0:T(8,128)(2,1)S(1)}, bf16[64,256]{1,0:T(8,128)(2,1)S(1)}, u32[]{:S(2)}, u32[]{:S(2)}) collective-permute-start(bf16[64,256]{1,0:T(8,128)(2,1)S(1)} %get-tuple-element.34), channel_id=1, source_target_pairs={{0,31},{1,2},{2,1},{3,4},{4,3},{5,6},{6,5},{7,8},{8,7},{9,10},{10,... | collective-permute-start | bytes 98312 | tf_op jit(solution)/shard_map/ppermute | solution.py:30
  60.8 12.8 %collective-permute-start.5 = (bf16[64,256]{1,0:T(8,128)(2,1)S(1)}, bf16[64,256]{1,0:T(8,128)(2,1)S(1)}, u32[]{:S(2)}, u32[]{:S(2)}) collective-permute-start(bf16[64,256]{1,0:T(8,128)(2,1)S(1)} %get-tuple-element.36), channel_id=1, source_target_pairs={{0,32},{32,0},{64,96},{96,64},{128,160},{160,128},{192,224},{224,1... | collective-permute-start | bytes 98312 | tf_op jit(solution)/shard_map/ppermute | solution.py:30
  62.7 10.9 %collective-permute-start.6 = (bf16[64,256]{1,0:T(8,128)(2,1)S(1)}, bf16[64,256]{1,0:T(8,128)(2,1)S(1)}, u32[]{:S(2)}, u32[]{:S(2)}) collective-permute-start(bf16[64,256]{1,0:T(8,128)(2,1)S(1)} %get-tuple-element.37), channel_id=1, source_target_pairs={{0,480},{32,64},{64,32},{96,128},{128,96},{160,192},{192,160},{224... | collective-permute-start | bytes 98312 | tf_op jit(solution)/shard_map/ppermute | solution.py:30
  66.0 13.4 %collective-permute-start.7 = (bf16[64,256]{1,0:T(8,128)(2,1)S(1)}, bf16[64,256]{1,0:T(8,128)(2,1)S(1)}, u32[]{:S(2)}, u32[]{:S(2)}) collective-permute-start(bf16[64,256]{1,0:T(8,128)(2,1)S(1)} %get-tuple-element.38), channel_id=1, source_target_pairs={{0,256},{32,288},{64,320},{96,352},{128,384},{160,416},{192,448},{... | collective-permute-start | bytes 98312 | tf_op jit(solution)/shard_map/ppermute | solution.py:30
  79.7 13.2 %collective-permute-start.8 = (bf16[64,256]{1,0:T(8,128)(2,1)S(1)}, bf16[64,256]{1,0:T(8,128)(2,1)S(1)}, u32[]{:S(2)}, u32[]{:S(2)}) collective-permute-start(bf16[64,256]{1,0:T(8,128)(2,1)S(1)} %get-tuple-element.39.refs_3_), channel_id=1, source_target_pairs={{0,32},{32,0},{64,96},{96,64},{128,160},{160,128},{192,224},{224,1... | collective-permute-start | bytes 98312 | tf_op jit(solution)/shard_map/ppermute | solution.py:30
  81.7 11.2 %collective-permute-start.9 = (bf16[64,256]{1,0:T(8,128)(2,1)S(1)}, bf16[64,256]{1,0:T(8,128)(2,1)S(1)}, u32[]{:S(2)}, u32[]{:S(2)}) collective-permute-start(bf16[64,256]{1,0:T(8,128)(2,1)S(1)} %get-tuple-element.39.refs_3_), channel_id=1, source_target_pairs={{0,480},{32,64},{64,32},{96,128},{128,96},{160,192},{192,160},{224... | collective-permute-start | bytes 98312 | tf_op jit(solution)/shard_map/ppermute | solution.py:30
  86.5 13.4 %collective-permute-start.10 = (bf16[64,256]{1,0:T(8,128)(2,1)S(1)}, bf16[64,256]{1,0:T(8,128)(2,1)S(1)}, u32[]{:S(2)}, u32[]{:S(2)}) collective-permute-start(bf16[64,256]{1,0:T(8,128)(2,1)S(1)} %get-tuple-element.39.refs_3_), channel_id=1, source_target_pairs={{0,256},{32,288},{64,320},{96,352},{128,384},{160,416},{192,448},{... | collective-permute-start | bytes 98312 | tf_op jit(solution)/shard_map/ppermute | solution.py:30
  100.8 13.7 %collective-permute-start.11 = (bf16[64,256]{1,0:T(8,128)(2,1)S(1)}, bf16[64,256]{1,0:T(8,128)(2,1)S(1)}, u32[]{:S(2)}, u32[]{:S(2)}) collective-permute-start(bf16[64,256]{1,0:T(8,128)(2,1)S(1)} %get-tuple-element.41), channel_id=1, source_target_pairs={{0,31},{1,2},{2,1},{3,4},{4,3},{5,6},{6,5},{7,8},{8,7},{9,10},{10,... | collective-permute-start | bytes 98312 | tf_op jit(solution)/shard_map/ppermute | solution.py:30
  114.7 12.2 %collective-permute-start.12 = (bf16[64,256]{1,0:T(8,128)(2,1)S(1)}, bf16[64,256]{1,0:T(8,128)(2,1)S(1)}, u32[]{:S(2)}, u32[]{:S(2)}) collective-permute-start(bf16[64,256]{1,0:T(8,128)(2,1)S(1)} %get-tuple-element.43.refs_3_), channel_id=1, source_target_pairs={{0,32},{32,0},{64,96},{96,64},{128,160},{160,128},{192,224},{224,1... | collective-permute-start | bytes 98312 | tf_op jit(solution)/shard_map/ppermute | solution.py:30
  116.6 10.2 %collective-permute-start.13 = (bf16[64,256]{1,0:T(8,128)(2,1)S(1)}, bf16[64,256]{1,0:T(8,128)(2,1)S(1)}, u32[]{:S(2)}, u32[]{:S(2)}) collective-permute-start(bf16[64,256]{1,0:T(8,128)(2,1)S(1)} %get-tuple-element.43.refs_3_), channel_id=1, source_target_pairs={{0,480},{32,64},{64,32},{96,128},{128,96},{160,192},{192,160},{224... | collective-permute-start | bytes 98312 | tf_op jit(solution)/shard_map/ppermute | solution.py:30
  120.7 13.4 %collective-permute-start.14 = (bf16[64,256]{1,0:T(8,128)(2,1)S(1)}, bf16[64,256]{1,0:T(8,128)(2,1)S(1)}, u32[]{:S(2)}, u32[]{:S(2)}) collective-permute-start(bf16[64,256]{1,0:T(8,128)(2,1)S(1)} %get-tuple-element.43.refs_3_), channel_id=1, source_target_pairs={{0,256},{32,288},{64,320},{96,352},{128,384},{160,416},{192,448},{... | collective-permute-start | bytes 98312 | tf_op jit(solution)/shard_map/ppermute | solution.py:30
  135.0 13.6 %collective-permute-start.15 = (bf16[64,256]{1,0:T(8,128)(2,1)S(1)}, bf16[64,256]{1,0:T(8,128)(2,1)S(1)}, u32[]{:S(2)}, u32[]{:S(2)}) collective-permute-start(bf16[64,256]{1,0:T(8,128)(2,1)S(1)} %get-tuple-element.45), channel_id=1, source_target_pairs={{0,31},{1,2},{2,1},{3,4},{4,3},{5,6},{6,5},{7,8},{8,7},{9,10},{10,... | collective-permute-start | bytes 98312 | tf_op jit(solution)/shard_map/ppermute | solution.py:30

commit v2 on v1

--- a/solution.py
+++ b/solution.py
@@ -7,6 +7,9 @@
 
 VMEM = pl.BlockSpec(memory_space=pltpu.VMEM)
 SMEM = pl.BlockSpec(memory_space=pltpu.SMEM)
+ANY = pl.BlockSpec(memory_space=pl.ANY)
+HBM = pl.BlockSpec(memory_space=pltpu.HBM)
+FIRST_FLOPS = 6 * 10**9
 NT = (((1,), (1,)), ((), ()))
 NN = (((1,), (0,)), ((), ()))
 BF = jnp.bfloat16
@@ -84,8 +87,8 @@
         r = lax.axis_index("row")
         c = lax.axis_index("col")
         if kind == "fwd":
-            held[0:4] = panels[0][...]
-            held[4] = panels[1][...]
+            held[4] = panels[0][...]
+            held[0:4] = panels[1][...]
         else:
             for i in range(4):
                 held[i] = panels[i][...]
@@ -98,7 +101,7 @@
                 keys.append(t)
             else:
                 place = jnp.where(
-                    t == r, 0, jnp.where(t == pair_of(r, n_row), 1, jnp.where(t == far_of(r, n_row), 3, 2))
+                    t == far_of(r, n_row), 0, jnp.where(t == pair_of(r, n_row), 1, jnp.where(t == r, 3, 2))
                 )
                 keys.append(e)
             products[s] = lax.dot_general(
@@ -123,7 +126,7 @@
 def products(kind, pair_idx, tables, blocks, panels, base, finish):
     n_row, n_col = lax.axis_size("row"), lax.axis_size("col")
     slots, size = blocks.shape[2], blocks.shape[3]
-    shape = panels[-1].shape
+    shape = panels[0].shape
     panel = jax.ShapeDtypeStruct(shape, BF)
     if not finish:
         out = [jax.ShapeDtypeStruct((4, *shape), F32)]
@@ -144,14 +147,22 @@
     )
 
 
-def first_body(rhs, inverse, y_out, send_out):
-    y = lax.dot_general(rhs[0, 0, 0].astype(BF), inverse[0, 0, 0], NT, preferred_element_type=F32)
+def first_body(rhs, inverse, y_out, send_out, rhs_held, inverse_held, sems):
+    copies = [
+        pltpu.make_async_copy(rhs.at[0, 0, 0], rhs_held, sems.at[0]),
+        pltpu.make_async_copy(inverse.at[0, 0, 0], inverse_held, sems.at[1]),
+    ]
+    for copy in copies:
+        copy.start()
+    for copy in copies:
+        copy.wait()
+    y = lax.dot_general(rhs_held[...].astype(BF), inverse_held[...], NT, preferred_element_type=F32)
     y_out[...] = y
     send_out[...] = y.astype(BF)
 
 
 def forward_body(level, last):
-    def body(rhs, inverse, own, pair, cross, far, *outs):
+    def body(rhs, inverse, far, pair, cross, own, *outs):
         total = own[...].astype(F32) + pair[...].astype(F32) + cross[...].astype(F32) + far[...].astype(F32)
         y = lax.dot_general(
             (rhs[level, 0, 0] - total).astype(BF), inverse[level, 0, 0], NT, preferred_element_type=F32
@@ -166,6 +177,14 @@
 
 def backward_body(level, n_col):
     def body(y, inverse, own, cross, group, *outs):
+        if level == 0:
+            z1, z2, out, z0, sems = outs
+            copies = [
+                pltpu.make_async_copy(held, out.at[i, 0, 0], sems.at[i]) for i, held in enumerate((z0, z1, z2))
+            ]
+            copies[1].start()
+            copies[2].start()
+            outs = (z0,)
         c = lax.axis_index("col")
         total = (
             own[...].astype(F32)
@@ -177,6 +196,10 @@
         outs[0][...] = z
         if level > 0:
             outs[1][...] = z.astype(BF)
+        else:
+            copies[0].start()
+            for copy in copies:
+                copy.wait()
 
     return body
 
@@ -189,27 +212,36 @@
 
     def gather_cols(value):
         cross = swap(value, "col", cross_of)
-        return [gather_far(value, "col"), cross]
+        return [cross, gather_far(value, "col")]
 
     def gather_rows(value):
         far = swap(value, "row", far_of)
         pair = swap(value, "row", pair_of)
         cross = swap(value, "row", cross_of)
-        return [value, pair, cross, far]
+        return [far, pair, cross, value]
 
     def scatter_rows(parts):
         own, pair, cross, far = parts
         far = swap(far, "row", far_of)
         pair = swap(pair, "row", pair_of)
         cross = swap(cross, "row", cross_of)
-        return [own, pair, cross, far]
+        return [far, pair, cross, own]
 
     def scatter_cols(parts):
         own, cross, group = parts
         cross = swap(cross, "col", cross_of)
         return [own, cross, gather_far(group, "col")]
 
-    y0, s0 = call(first_body, [panel, bf_like(panel)], [VMEM] * 2, (rhs, inverse), solve_flops, 2**18, name="y0")
+    y0, s0 = call(
+        first_body,
+        [panel, bf_like(panel)],
+        [HBM] * 2,
+        (rhs, inverse),
+        FIRST_FLOPS,
+        2**18,
+        [pltpu.VMEM(panel.shape, F32), pltpu.VMEM(inverse.shape[3:], BF), pltpu.SemaphoreType.DMA((2,))],
+        "y0",
+    )
     g0 = gather_cols(s0)
     parts = scatter_rows(products("fwd", 0, tables, blocks, g0, None, True))
     base2 = products("fwd", 1, tables, blocks, g0, None, False)[0]
@@ -229,8 +261,17 @@
     )
     h1 = gather_rows(b1)
     parts = scatter_cols(products("bwd", 0, tables, blocks, h1, base0, True))
-    z0 = call(backward_body(0, n_col), [panel], [VMEM] * 5, (y0, inverse, *parts), solve_flops, 2**18, name="z0")[0]
-    return jnp.stack([z0, z1, z2])[:, None, None]
+    return call(
+        backward_body(0, n_col),
+        f32_like(rhs),
+        [VMEM] * 7,
+        (y0, inverse, *parts, z1, z2),
+        solve_flops,
+        2**18,
+        [pltpu.VMEM(panel.shape, F32), pltpu.SemaphoreType.DMA((3,))],
+        "z0",
+        out_specs=ANY,
+    )
 
 
 def solution(mesh):

time: 150 us -> 129 us (0.86)
  waiting for transfers between devices: 25.9 us -> 10.8 us
  local copies, waits for them, and re-layouts: 5.41 us -> 1.94 us
  starting transfers between devices: 71.1 us -> 69 us
    ppermute x16, waiting for transfers between devices: 25.9 us -> 10.8 us  [swap(): return lax.ppermute(value, axis, [(i, partner(i, n)) for i in range(n)])]
    unnamed x16 -> x14, local copies, waits for them, and re-layouts: 5.41 us -> 1.94 us
    ppermute x16, starting transfers between devices: 71.1 us -> 69 us  [swap(): return lax.ppermute(value, axis, [(i, partner(i, n)) for i in range(n)])]
  transfers between devices with their start and end apart: 16 -> 16, of which waited for: 4 -> 7; matrix products, arithmetic and copies ran while one was open for 0% -> 0% of each run, Pallas kernels for 1% -> 2%
where the time goes in v2:
time: 129 us; the launch traced here: 128 us
  starting transfers between devices  69 us (53%)
  blocking collectives  38.3 us (30%)
  waiting for transfers between devices  10.8 us (8%)
  Pallas kernels  8.21 us (6%)
  local copies, waits for them, and re-layouts  1.94 us (2%)
    ppermute x16, starting transfers between devices, swap(): return lax.ppermute(value, axis, [(i, partner(i, n)) for i in range(n)])  69 us
    all_gather x4, blocking collectives, gather_far(): lax.all_gather(value, axis, axis_index_groups=far_groups(lax.axis_size(ax...  38.3 us
    ppermute x16, waiting for transfers between devices, swap(): return lax.ppermute(value, axis, [(i, partner(i, n)) for i in range(n)])  10.8 us
    pallas_call x11, Pallas kernels, call(): pl.pallas_call(body, out_shape=out_shape, in_specs=in_specs, out_specs=ou...  8.21 us
  transfers between devices with their start and end apart: 16, of which 7 were waited for; matrix products, arithmetic and copies ran while one was open for 0% of the time, Pallas kernels for 2%

profile of v2, /device:TPU:1, one launch (start us, length us, event | category | flops | bytes accessed | tf_op | source)
XLA Modules:
  0.0 128.4 jit_solution(5463653735672132896)
XLA Ops:
  0.0 0.0 copy-start.1
  0.0 1.0 copy-done.1
  1.0 0.0 copy-start.3
  1.0 0.9 copy-done.3
  1.9 0.0 copy-start
  1.9 0.0 copy-start.5
  1.9 0.0 copy-start.6
  1.9 0.5 y0.1
  2.4 4.7 %collective-permute-start = (bf16[64,256]{1,0:T(8,128)(2,1)S(1)}, bf16[64,256]{1,0:T(8,128)(2,1)S(1)}, u32[]{:S(2)}, u32[]{:S(2)}) collective-permute-start(bf16[64,256]{1,0:T(8,128)(2,1)S(1)} %get-tuple-element.28), channel_id=1, source_target_pairs={{0,31},{1,2},{2,1},{3,4},{4,3},{5,6},{6,5},{7,8},{8,7},{9,10},{10,... | collective-permute-start | bytes 98312 | tf_op jit(solution)/shard_map/ppermute | solution.py:33
  7.1 10.9 %all-gather = bf16[256,256]{1,0:T(8,128)(2,1)S(1)} all-gather(bf16[64,256]{1,0:T(8,128)(2,1)S(1)} %get-tuple-element.28), channel_id=2, replica_groups={{0,1,16,17},{2,3,18,19},{4,5,20,21},{6,7,22,23},{8,9,24,25},{10,11,26,2..., dimensions={0}, use_global_device_ids=true | all-gather | bytes 163840 | tf_op jit(solution)/shard_map/all_gather | solution.py:42
  18.0 0.0 collective-permute-done.refs_3_
  18.0 0.0 copy-done
  18.1 0.0 copy-done.5
  18.1 0.0 copy-done.6
  18.1 0.0 copy-start.4
  18.1 1.1 fwd0.1
  19.2 14.7 %collective-permute-start.1 = (bf16[64,256]{1,0:T(8,128)(2,1)S(1)}, bf16[64,256]{1,0:T(8,128)(2,1)S(1)}, u32[]{:S(2)}, u32[]{:S(2)}) collective-permute-start(bf16[64,256]{1,0:T(8,128)(2,1)S(1)} %get-tuple-element.29), channel_id=1, source_target_pairs={{0,256},{32,288},{64,320},{96,352},{128,384},{160,416},{192,448},{... | collective-permute-start | bytes 98312 | tf_op jit(solution)/shard_map/ppermute | solution.py:33
  34.0 2.6 %collective-permute-start.2 = (bf16[64,256]{1,0:T(8,128)(2,1)S(1)}, bf16[64,256]{1,0:T(8,128)(2,1)S(1)}, u32[]{:S(2)}, u32[]{:S(2)}) collective-permute-start(bf16[64,256]{1,0:T(8,128)(2,1)S(1)} %get-tuple-element.30), channel_id=1, source_target_pairs={{0,32},{32,0},{64,96},{96,64},{128,160},{160,128},{192,224},{224,1... | collective-permute-start | bytes 98312 | tf_op jit(solution)/shard_map/ppermute | solution.py:33
  36.6 1.9 %collective-permute-start.3 = (bf16[64,256]{1,0:T(8,128)(2,1)S(1)}, bf16[64,256]{1,0:T(8,128)(2,1)S(1)}, u32[]{:S(2)}, u32[]{:S(2)}) collective-permute-start(bf16[64,256]{1,0:T(8,128)(2,1)S(1)} %get-tuple-element.31), channel_id=1, source_target_pairs={{0,480},{32,64},{64,32},{96,128},{128,96},{160,192},{192,160},{224... | collective-permute-start | bytes 98312 | tf_op jit(solution)/shard_map/ppermute | solution.py:33
  38.5 1.1 fwd1.1.refs_5_
  39.7 0.0 collective-permute-done.1.far
  39.7 0.2 collective-permute-done.2.pair
  39.9 2.6 %collective-permute-done.3.cross = bf16[64,256]{1,0:T(8,128)(2,1)S(1)} collective-permute-done((bf16[64,256]{1,0:T(8,128)(2,1)S(1)}, bf16[64,256]{1,0:T(8,128)(2,1)S(1)}, u32[]{:S(2)}, u32[]{:S(2)}) %collective-permute-start.3) | collective-permute-done | bytes 32800 | tf_op jit(solution)/shard_map/ppermute | solution.py:33
  42.5 0.0 copy-done.4
  42.5 0.2 y1.1
  42.6 1.9 %collective-permute-start.4 = (bf16[64,256]{1,0:T(8,128)(2,1)S(1)}, bf16[64,256]{1,0:T(8,128)(2,1)S(1)}, u32[]{:S(2)}, u32[]{:S(2)}) collective-permute-start(bf16[64,256]{1,0:T(8,128)(2,1)S(1)} %get-tuple-element.34), channel_id=1, source_target_pairs={{0,31},{1,2},{2,1},{3,4},{4,3},{5,6},{6,5},{7,8},{8,7},{9,10},{10,... | collective-permute-start | bytes 98312 | tf_op jit(solution)/shard_map/ppermute | solution.py:33
  44.6 8.6 %all-gather.1 = bf16[256,256]{1,0:T(8,128)(2,1)S(1)} all-gather(bf16[64,256]{1,0:T(8,128)(2,1)S(1)} %get-tuple-element.34), channel_id=3, replica_groups={{0,1,16,17},{2,3,18,19},{4,5,20,21},{6,7,22,23},{8,9,24,25},{10,11,26,2..., dimensions={0}, use_global_device_ids=true | all-gather | bytes 163840 | tf_op jit(solution)/shard_map/all_gather | solution.py:42
  53.2 0.0 collective-permute-done.4.refs_3_
  53.2 0.0 copy-start.2
  53.2 1.1 fwd2.1
  54.4 5.1 %collective-permute-start.5 = (bf16[64,256]{1,0:T(8,128)(2,1)S(1)}, bf16[64,256]{1,0:T(8,128)(2,1)S(1)}, u32[]{:S(2)}, u32[]{:S(2)}) collective-permute-start(bf16[64,256]{1,0:T(8,128)(2,1)S(1)} %get-tuple-element.35), channel_id=1, source_target_pairs={{0,256},{32,288},{64,320},{96,352},{128,384},{160,416},{192,448},{... | collective-permute-start | bytes 98312 | tf_op jit(solution)/shard_map/ppermute | solution.py:33
  59.5 1.9 %collective-permute-start.6 = (bf16[64,256]{1,0:T(8,128)(2,1)S(1)}, bf16[64,256]{1,0:T(8,128)(2,1)S(1)}, u32[]{:S(2)}, u32[]{:S(2)}) collective-permute-start(bf16[64,256]{1,0:T(8,128)(2,1)S(1)} %get-tuple-element.36), channel_id=1, source_target_pairs={{0,32},{32,0},{64,96},{96,64},{128,160},{160,128},{192,224},{224,1... | collective-permute-start | bytes 98312 | tf_op jit(solution)/shard_map/ppermute | solution.py:33
  61.4 4.6 %collective-permute-start.7 = (bf16[64,256]{1,0:T(8,128)(2,1)S(1)}, bf16[64,256]{1,0:T(8,128)(2,1)S(1)}, u32[]{:S(2)}, u32[]{:S(2)}) collective-permute-start(bf16[64,256]{1,0:T(8,128)(2,1)S(1)} %get-tuple-element.37), channel_id=1, source_target_pairs={{0,480},{32,64},{64,32},{96,128},{128,96},{160,192},{192,160},{224... | collective-permute-start | bytes 98312 | tf_op jit(solution)/shard_map/ppermute | solution.py:33
  66.0 2.4 %collective-permute-done.5.far = bf16[64,256]{1,0:T(8,128)(2,1)S(1)} collective-permute-done((bf16[64,256]{1,0:T(8,128)(2,1)S(1)}, bf16[64,256]{1,0:T(8,128)(2,1)S(1)}, u32[]{:S(2)}, u32[]{:S(2)}) %collective-permute-start.5) | collective-permute-done | bytes 32800 | tf_op jit(solution)/shard_map/ppermute | solution.py:33
  68.4 0.0 collective-permute-done.6.pair
  68.4 0.0 collective-permute-done.7.cross
  68.4 0.3 z2.1
  68.7 7.8 %collective-permute-start.8 = (bf16[64,256]{1,0:T(8,128)(2,1)S(1)}, bf16[64,256]{1,0:T(8,128)(2,1)S(1)}, u32[]{:S(2)}, u32[]{:S(2)}) collective-permute-start(bf16[64,256]{1,0:T(8,128)(2,1)S(1)} %get-tuple-element.39.refs_6_), channel_id=1, source_target_pairs={{0,256},{32,288},{64,320},{96,352},{128,384},{160,416},{192,448},{... | collective-permute-start | bytes 98312 | tf_op jit(solution)/shard_map/ppermute | solution.py:33
  76.5 2.2 %collective-permute-start.9 = (bf16[64,256]{1,0:T(8,128)(2,1)S(1)}, bf16[64,256]{1,0:T(8,128)(2,1)S(1)}, u32[]{:S(2)}, u32[]{:S(2)}) collective-permute-start(bf16[64,256]{1,0:T(8,128)(2,1)S(1)} %get-tuple-element.39.refs_6_), channel_id=1, source_target_pairs={{0,32},{32,0},{64,96},{96,64},{128,160},{160,128},{192,224},{224,1... | collective-permute-start | bytes 98312 | tf_op jit(solution)/shard_map/ppermute | solution.py:33
  78.7 2.0 %collective-permute-start.10 = (bf16[64,256]{1,0:T(8,128)(2,1)S(1)}, bf16[64,256]{1,0:T(8,128)(2,1)S(1)}, u32[]{:S(2)}, u32[]{:S(2)}) collective-permute-start(bf16[64,256]{1,0:T(8,128)(2,1)S(1)} %get-tuple-element.39.refs_6_), channel_id=1, source_target_pairs={{0,480},{32,64},{64,32},{96,128},{128,96},{160,192},{192,160},{224... | collective-permute-start | bytes 98312 | tf_op jit(solution)/shard_map/ppermute | solution.py:33
  80.6 1.5 %collective-permute-done.8.refs_3_ = bf16[64,256]{1,0:T(8,128)(2,1)S(1)} collective-permute-done((bf16[64,256]{1,0:T(8,128)(2,1)S(1)}, bf16[64,256]{1,0:T(8,128)(2,1)S(1)}, u32[]{:S(2)}, u32[]{:S(2)}) %collective-permute-start.8) | collective-permute-done | bytes 32800 | tf_op jit(solution)/shard_map/ppermute | solution.py:33
  82.2 0.0 collective-permute-done.9.refs_4_
  82.2 2.4 %collective-permute-done.10.refs_5_ = bf16[64,256]{1,0:T(8,128)(2,1)S(1)} collective-permute-done((bf16[64,256]{1,0:T(8,128)(2,1)S(1)}, bf16[64,256]{1,0:T(8,128)(2,1)S(1)}, u32[]{:S(2)}, u32[]{:S(2)}) %collective-permute-start.10) | collective-permute-done | bytes 32800 | tf_op jit(solution)/shard_map/ppermute | solution.py:33
  84.5 1.0 bwd2.1
  85.5 5.3 %collective-permute-start.11 = (bf16[64,256]{1,0:T(8,128)(2,1)S(1)}, bf16[64,256]{1,0:T(8,128)(2,1)S(1)}, u32[]{:S(2)}, u32[]{:S(2)}) collective-permute-start(bf16[64,256]{1,0:T(8,128)(2,1)S(1)} %get-tuple-element.41), channel_id=1, source_target_pairs={{0,31},{1,2},{2,1},{3,4},{4,3},{5,6},{6,5},{7,8},{8,7},{9,10},{10,... | collective-permute-start | bytes 98312 | tf_op jit(solution)/shard_map/ppermute | solution.py:33
  90.9 7.7 %all-gather.2 = bf16[8,64,256]{2,1,0:T(8,128)(2,1)S(1)} all-gather(bf16[2,64,256]{2,1,0:T(8,128)(2,1)S(1)} %get-tuple-element.42), channel_id=4, replica_groups={{0,1,16,17},{2,3,18,19},{4,5,20,21},{6,7,22,23},{8,9,24,25},{10,11,26,2..., dimensions={0}, use_global_device_ids=true | all-gather | bytes 327680 | tf_op jit(solution)/shard_map/all_gather | solution.py:42
  98.6 0.0 collective-permute-done.11.cross
  98.6 0.0 copy-done.2
  98.6 0.2 z1.1
  98.8 6.5 %collective-permute-start.12 = (bf16[64,256]{1,0:T(8,128)(2,1)S(1)}, bf16[64,256]{1,0:T(8,128)(2,1)S(1)}, u32[]{:S(2)}, u32[]{:S(2)}) collective-permute-start(bf16[64,256]{1,0:T(8,128)(2,1)S(1)} %get-tuple-element.43.refs_6_), channel_id=1, source_target_pairs={{0,256},{32,288},{64,320},{96,352},{128,384},{160,416},{192,448},{... | collective-permute-start | bytes 98312 | tf_op jit(solution)/shard_map/ppermute | solution.py:33
  105.3 2.3 %collective-permute-start.13 = (bf16[64,256]{1,0:T(8,128)(2,1)S(1)}, bf16[64,256]{1,0:T(8,128)(2,1)S(1)}, u32[]{:S(2)}, u32[]{:S(2)}) collective-permute-start(bf16[64,256]{1,0:T(8,128)(2,1)S(1)} %get-tuple-element.43.refs_6_), channel_id=1, source_target_pairs={{0,32},{32,0},{64,96},{96,64},{128,160},{160,128},{192,224},{224,1... | collective-permute-start | bytes 98312 | tf_op jit(solution)/shard_map/ppermute | solution.py:33
  107.5 3.4 %collective-permute-start.14 = (bf16[64,256]{1,0:T(8,128)(2,1)S(1)}, bf16[64,256]{1,0:T(8,128)(2,1)S(1)}, u32[]{:S(2)}, u32[]{:S(2)}) collective-permute-start(bf16[64,256]{1,0:T(8,128)(2,1)S(1)} %get-tuple-element.43.refs_6_), channel_id=1, source_target_pairs={{0,480},{32,64},{64,32},{96,128},{128,96},{160,192},{192,160},{224... | collective-permute-start | bytes 98312 | tf_op jit(solution)/shard_map/ppermute | solution.py:33
  111.0 1.0 bwd1.1.refs_7_
  112.0 0.5 collective-permute-done.12.refs_3_
  112.5 0.0 collective-permute-done.13.refs_4_
  112.5 1.1 collective-permute-done.14.refs_5_
  113.6 1.0 bwd0.1
  114.6 2.0 %collective-permute-start.15 = (bf16[64,256]{1,0:T(8,128)(2,1)S(1)}, bf16[64,256]{1,0:T(8,128)(2,1)S(1)}, u32[]{:S(2)}, u32[]{:S(2)}) collective-permute-start(bf16[64,256]{1,0:T(8,128)(2,1)S(1)} %get-tuple-element.45), channel_id=1, source_target_pairs={{0,31},{1,2},{2,1},{3,4},{4,3},{5,6},{6,5},{7,8},{8,7},{9,10},{10,... | collective-permute-start | bytes 98312 | tf_op jit(solution)/shard_map/ppermute | solution.py:33
  116.6 11.0 %all-gather.3 = bf16[8,64,256]{2,1,0:T(8,128)(2,1)S(1)} all-gather(bf16[2,64,256]{2,1,0:T(8,128)(2,1)S(1)} %get-tuple-element.46), channel_id=5, replica_groups={{0,1,16,17},{2,3,18,19},{4,5,20,21},{6,7,22,23},{8,9,24,25},{10,11,26,2..., dimensions={0}, use_global_device_ids=true | all-gather | bytes 327680 | tf_op jit(solution)/shard_map/all_gather | solution.py:42
  127.6 0.0 collective-permute-done.15.cross
  127.6 0.8 z0.1
Async XLA Ops:
  0.0 1.0 copy-start.1
  1.0 0.9 copy-start.3
  1.9 16.1 %copy-start = (bf16[3,1,10,256,256]{4,3,2,1,0:T(8,128)(2,1)S(1)}, bf16[3,1,10,256,256]{4,3,2,1,0:T(8,128)(2,1)}, u32[]{:S(2)}) copy-start(bf16[3,1,10,256,256]{4,3,2,1,0:T(8,128)(2,1)} %refs_2_.11) | copy-start | bytes 11796484
  1.9 16.1 %copy-start.5 = (s32[3,1,10]{2,1,0:T(1,128)S(1)}, s32[3,1,10]{2,1,0:T(1,128)}, u32[]{:S(2)}) copy-start(s32[3,1,10]{2,1,0:T(1,128)} %refs_0_.11) | copy-start | bytes 364
  1.9 16.1 %copy-start.6 = (s32[3,1,10]{2,1,0:T(1,128)S(1)}, s32[3,1,10]{2,1,0:T(1,128)}, u32[]{:S(2)}) copy-start(s32[3,1,10]{2,1,0:T(1,128)} %refs_1_.11) | copy-start | bytes 364
  2.4 15.7 %collective-permute-start = (bf16[64,256]{1,0:T(8,128)(2,1)S(1)}, bf16[64,256]{1,0:T(8,128)(2,1)S(1)}, u32[]{:S(2)}, u32[]{:S(2)}) collective-permute-start(bf16[64,256]{1,0:T(8,128)(2,1)S(1)} %get-tuple-element.28), channel_id=1, source_target_pairs={{0,31},{1,2},{2,1},{3,4},{4,3},{5,6},{6,5},{7,8},{8,7},{9,10},{10,... | collective-permute-start | bytes 98312 | tf_op jit(solution)/shard_map/ppermute | solution.py:33
  18.1 24.4 %copy-start.4 = (f32[3,1,1,64,256]{4,3,2,1,0:T(8,128)S(1)}, f32[3,1,1,64,256]{4,3,2,1,0:T(8,128)}, u32[]{:S(2)}) copy-start(f32[3,1,1,64,256]{4,3,2,1,0:T(8,128)} %rhs.5) | copy-start | bytes 589828
  19.2 20.5 %collective-permute-start.1 = (bf16[64,256]{1,0:T(8,128)(2,1)S(1)}, bf16[64,256]{1,0:T(8,128)(2,1)S(1)}, u32[]{:S(2)}, u32[]{:S(2)}) collective-permute-start(bf16[64,256]{1,0:T(8,128)(2,1)S(1)} %get-tuple-element.29), channel_id=1, source_target_pairs={{0,256},{32,288},{64,320},{96,352},{128,384},{160,416},{192,448},{... | collective-permute-start | bytes 98312 | tf_op jit(solution)/shard_map/ppermute | solution.py:33
  34.0 5.9 %collective-permute-start.2 = (bf16[64,256]{1,0:T(8,128)(2,1)S(1)}, bf16[64,256]{1,0:T(8,128)(2,1)S(1)}, u32[]{:S(2)}, u32[]{:S(2)}) collective-permute-start(bf16[64,256]{1,0:T(8,128)(2,1)S(1)} %get-tuple-element.30), channel_id=1, source_target_pairs={{0,32},{32,0},{64,96},{96,64},{128,160},{160,128},{192,224},{224,1... | collective-permute-start | bytes 98312 | tf_op jit(solution)/shard_map/ppermute | solution.py:33
  36.6 5.9 %collective-permute-start.3 = (bf16[64,256]{1,0:T(8,128)(2,1)S(1)}, bf16[64,256]{1,0:T(8,128)(2,1)S(1)}, u32[]{:S(2)}, u32[]{:S(2)}) collective-permute-start(bf16[64,256]{1,0:T(8,128)(2,1)S(1)} %get-tuple-element.31), channel_id=1, source_target_pairs={{0,480},{32,64},{64,32},{96,128},{128,96},{160,192},{192,160},{224... | collective-permute-start | bytes 98312 | tf_op jit(solution)/shard_map/ppermute | solution.py:33
  42.6 10.6 %collective-permute-start.4 = (bf16[64,256]{1,0:T(8,128)(2,1)S(1)}, bf16[64,256]{1,0:T(8,128)(2,1)S(1)}, u32[]{:S(2)}, u32[]{:S(2)}) collective-permute-start(bf16[64,256]{1,0:T(8,128)(2,1)S(1)} %get-tuple-element.34), channel_id=1, source_target_pairs={{0,31},{1,2},{2,1},{3,4},{4,3},{5,6},{6,5},{7,8},{8,7},{9,10},{10,... | collective-permute-start | bytes 98312 | tf_op jit(solution)/shard_map/ppermute | solution.py:33
  53.2 45.4 %copy-start.2 = (bf16[3,1,1,256,256]{4,3,2,1,0:T(8,128)(2,1)S(1)}, bf16[3,1,1,256,256]{4,3,2,1,0:T(8,128)(2,1)}, u32[]{:S(2)}) copy-start(bf16[3,1,1,256,256]{4,3,2,1,0:T(8,128)(2,1)} %inverse.9) | copy-start | bytes 1179652
  54.4 14.0 %collective-permute-start.5 = (bf16[64,256]{1,0:T(8,128)(2,1)S(1)}, bf16[64,256]{1,0:T(8,128)(2,1)S(1)}, u32[]{:S(2)}, u32[]{:S(2)}) collective-permute-start(bf16[64,256]{1,0:T(8,128)(2,1)S(1)} %get-tuple-element.35), channel_id=1, source_target_pairs={{0,256},{32,288},{64,320},{96,352},{128,384},{160,416},{192,448},{... | collective-permute-start | bytes 98312 | tf_op jit(solution)/shard_map/ppermute | solution.py:33
  59.5 8.9 %collective-permute-start.6 = (bf16[64,256]{1,0:T(8,128)(2,1)S(1)}, bf16[64,256]{1,0:T(8,128)(2,1)S(1)}, u32[]{:S(2)}, u32[]{:S(2)}) collective-permute-start(bf16[64,256]{1,0:T(8,128)(2,1)S(1)} %get-tuple-element.36), channel_id=1, source_target_pairs={{0,32},{32,0},{64,96},{96,64},{128,160},{160,128},{192,224},{224,1... | collective-permute-start | bytes 98312 | tf_op jit(solution)/shard_map/ppermute | solution.py:33
  61.4 6.9 %collective-permute-start.7 = (bf16[64,256]{1,0:T(8,128)(2,1)S(1)}, bf16[64,256]{1,0:T(8,128)(2,1)S(1)}, u32[]{:S(2)}, u32[]{:S(2)}) collective-permute-start(bf16[64,256]{1,0:T(8,128)(2,1)S(1)} %get-tuple-element.37), channel_id=1, source_target_pairs={{0,480},{32,64},{64,32},{96,128},{128,96},{160,192},{192,160},{224... | collective-permute-start | bytes 98312 | tf_op jit(solution)/shard_map/ppermute | solution.py:33
  68.7 13.5 %collective-permute-start.8 = (bf16[64,256]{1,0:T(8,128)(2,1)S(1)}, bf16[64,256]{1,0:T(8,128)(2,1)S(1)}, u32[]{:S(2)}, u32[]{:S(2)}) collective-permute-start(bf16[64,256]{1,0:T(8,128)(2,1)S(1)} %get-tuple-element.39.refs_6_), channel_id=1, source_target_pairs={{0,256},{32,288},{64,320},{96,352},{128,384},{160,416},{192,448},{... | collective-permute-start | bytes 98312 | tf_op jit(solution)/shard_map/ppermute | solution.py:33
  76.5 5.7 %collective-permute-start.9 = (bf16[64,256]{1,0:T(8,128)(2,1)S(1)}, bf16[64,256]{1,0:T(8,128)(2,1)S(1)}, u32[]{:S(2)}, u32[]{:S(2)}) collective-permute-start(bf16[64,256]{1,0:T(8,128)(2,1)S(1)} %get-tuple-element.39.refs_6_), channel_id=1, source_target_pairs={{0,32},{32,0},{64,96},{96,64},{128,160},{160,128},{192,224},{224,1... | collective-permute-start | bytes 98312 | tf_op jit(solution)/shard_map/ppermute | solution.py:33
  78.7 5.9 %collective-permute-start.10 = (bf16[64,256]{1,0:T(8,128)(2,1)S(1)}, bf16[64,256]{1,0:T(8,128)(2,1)S(1)}, u32[]{:S(2)}, u32[]{:S(2)}) collective-permute-start(bf16[64,256]{1,0:T(8,128)(2,1)S(1)} %get-tuple-element.39.refs_6_), channel_id=1, source_target_pairs={{0,480},{32,64},{64,32},{96,128},{128,96},{160,192},{192,160},{224... | collective-permute-start | bytes 98312 | tf_op jit(solution)/shard_map/ppermute | solution.py:33
  85.5 13.1 %collective-permute-start.11 = (bf16[64,256]{1,0:T(8,128)(2,1)S(1)}, bf16[64,256]{1,0:T(8,128)(2,1)S(1)}, u32[]{:S(2)}, u32[]{:S(2)}) collective-permute-start(bf16[64,256]{1,0:T(8,128)(2,1)S(1)} %get-tuple-element.41), channel_id=1, source_target_pairs={{0,31},{1,2},{2,1},{3,4},{4,3},{5,6},{6,5},{7,8},{8,7},{9,10},{10,... | collective-permute-start | bytes 98312 | tf_op jit(solution)/shard_map/ppermute | solution.py:33
  98.8 13.8 %collective-permute-start.12 = (bf16[64,256]{1,0:T(8,128)(2,1)S(1)}, bf16[64,256]{1,0:T(8,128)(2,1)S(1)}, u32[]{:S(2)}, u32[]{:S(2)}) collective-permute-start(bf16[64,256]{1,0:T(8,128)(2,1)S(1)} %get-tuple-element.43.refs_6_), channel_id=1, source_target_pairs={{0,256},{32,288},{64,320},{96,352},{128,384},{160,416},{192,448},{... | collective-permute-start | bytes 98312 | tf_op jit(solution)/shard_map/ppermute | solution.py:33
  105.3 7.3 %collective-permute-start.13 = (bf16[64,256]{1,0:T(8,128)(2,1)S(1)}, bf16[64,256]{1,0:T(8,128)(2,1)S(1)}, u32[]{:S(2)}, u32[]{:S(2)}) collective-permute-start(bf16[64,256]{1,0:T(8,128)(2,1)S(1)} %get-tuple-element.43.refs_6_), channel_id=1, source_target_pairs={{0,32},{32,0},{64,96},{96,64},{128,160},{160,128},{192,224},{224,1... | collective-permute-start | bytes 98312 | tf_op jit(solution)/shard_map/ppermute | solution.py:33
  107.5 6.1 %collective-permute-start.14 = (bf16[64,256]{1,0:T(8,128)(2,1)S(1)}, bf16[64,256]{1,0:T(8,128)(2,1)S(1)}, u32[]{:S(2)}, u32[]{:S(2)}) collective-permute-start(bf16[64,256]{1,0:T(8,128)(2,1)S(1)} %get-tuple-element.43.refs_6_), channel_id=1, source_target_pairs={{0,480},{32,64},{64,32},{96,128},{128,96},{160,192},{192,160},{224... | collective-permute-start | bytes 98312 | tf_op jit(solution)/shard_map/ppermute | solution.py:33
  114.6 13.0 %collective-permute-start.15 = (bf16[64,256]{1,0:T(8,128)(2,1)S(1)}, bf16[64,256]{1,0:T(8,128)(2,1)S(1)}, u32[]{:S(2)}, u32[]{:S(2)}) collective-permute-start(bf16[64,256]{1,0:T(8,128)(2,1)S(1)} %get-tuple-element.45), channel_id=1, source_target_pairs={{0,31},{1,2},{2,1},{3,4},{4,3},{5,6},{6,5},{7,8},{8,7},{9,10},{10,... | collective-permute-start | bytes 98312 | tf_op jit(solution)/shard_map/ppermute | solution.py:33

commit v3 on v2

v3 whole, which is shorter than its diff:
```python
import jax
import jax.numpy as jnp
from jax import lax
from jax.experimental import pallas as pl
from jax.experimental.pallas import tpu as pltpu
from jax.sharding import PartitionSpec as P

VMEM = pl.BlockSpec(memory_space=pltpu.VMEM)
SMEM = pl.BlockSpec(memory_space=pltpu.SMEM)
ANY = pl.BlockSpec(memory_space=pl.ANY)
HBM = pl.BlockSpec(memory_space=pltpu.HBM)
EXCHANGE_FLOPS = 6 * 10**9
NT = (((1,), (1,)), ((), ()))
NN = (((1,), (0,)), ((), ()))
BF = jnp.bfloat16
F32 = jnp.float32


def pair_of(i, n):
    return i + 1 - 2 * (i % 2)


def cross_of(i, n):
    return (i - 1 + 2 * (i % 2) + n) % n


def far_of(i, n):
    return (i + n // 2) % n


def swap(value, axis, partner):
    n = lax.axis_size(axis)
    return lax.ppermute(value, axis, [(i, partner(i, n)) for i in range(n)])


def far_groups(n):
    half = n // 2
    return [[i, i + 1, i + half, i + half + 1] for i in range(0, half, 2)]


def gather_far(value, axis):
    return lax.all_gather(value, axis, axis_index_groups=far_groups(lax.axis_size(axis)))


def gather_pair(value, axis):
    pairs = [[i, i + 1] for i in range(0, lax.axis_size(axis), 2)]
    return lax.all_gather(value, axis, axis_index_groups=pairs)


def group_place(i, n):
    return i % 2 + 2 * (i // (n // 2))


def call(body, out_shape, in_specs, args, flops, moved, scratch=(), name=None, out_specs=None, vmem=16 * 2**20):
    return pl.pallas_call(
        body,
        out_shape=out_shape,
        in_specs=in_specs,
        out_specs=out_specs if out_specs is not None else jax.tree.map(lambda _: VMEM, out_shape),
        scratch_shapes=list(scratch),
        compiler_params=pltpu.CompilerParams(vmem_limit_bytes=vmem),
        cost_estimate=pl.CostEstimate(flops=flops, bytes_accessed=moved, transcendentals=0),
        name=name,
    )(*args)


def f32_like(x):
    return jax.ShapeDtypeStruct(x.shape, F32)


def bf_like(x):
    return jax.ShapeDtypeStruct(x.shape, BF)


def product_body(kind, index, pair_idx, n_row, n_col, slots, add, finish):
    def body(*refs):
        targets, sources, blocks, *rest = refs
        count = 2 if kind == "fwd" else 3
        panels, rest = rest[:count], rest[count:]
        if add:
            base, rest = rest[0], rest[1:]
        outs, held = rest[:-1], rest[-1]
        r = lax.axis_index("row")
        c = lax.axis_index("col")
        place = 0
        for panel in panels:
            if len(panel.shape) == 2:
                held[place] = panel[...]
                place += 1
            else:
                held[place : place + panel.shape[0]] = panel[...]
                place += panel.shape[0]
        me, n = (r, n_row) if kind == "fwd" else (c, n_col)
        kinds = (me, pair_of(me, n), cross_of(me, n), far_of(me, n))
        total = None
        for s in range(slots):
            t = targets[pair_idx, 0, s]
            e = sources[pair_idx, 0, s]
            if kind == "fwd":
                key = t
                place = jnp.where(e == cross_of(c, n_col), 0, 1 + group_place(e, n_col))
            else:
                key = e
                place = jnp.where(
                    t == far_of(r, n_row), 0, jnp.where(t == cross_of(r, n_row), 1, 2 + t % 2)
                )
            panel = held[place]
            zero = jnp.zeros_like(panel)
            stacked = jnp.concatenate([jnp.where(key == k, panel, zero) for k in kinds], axis=0)
            term = lax.dot_general(
                stacked, blocks[index, 0, s], NT if kind == "fwd" else NN, preferred_element_type=F32
            )
            total = term if total is None else total + term
        rows = held.shape[1]
        if add:
            total = total + base[...]
        if not finish:
            outs[0][...] = total
            return
        parts = [total[i * rows : (i + 1) * rows].astype(BF) for i in range(4)]
        if kind == "fwd":
            for out, part in zip(outs, parts):
                out[...] = part
        else:
            outs[0][...] = parts[0]
            outs[1][...] = parts[2]
            outs[2][0] = parts[1]
            outs[2][1] = parts[3]

    return body


def products(kind, index, pair_idx, tables, blocks, panels, base, finish):
    n_row, n_col = lax.axis_size("row"), lax.axis_size("col")
    slots, size = blocks.shape[2], blocks.shape[3]
    shape = panels[0].shape
    panel = jax.ShapeDtypeStruct(shape, BF)
    if not finish:
        out = [jax.ShapeDtypeStruct((4 * shape[0], shape[1]), F32)]
    elif kind == "fwd":
        out = [panel] * 4
    else:
        out = [panel, panel, jax.ShapeDtypeStruct((2, *shape), BF)]
    args = [*tables, blocks, *panels] + ([base] if base is not None else [])
    return call(
        product_body(kind, index, pair_idx, n_row, n_col, slots, base is not None, finish),
        out,
        [SMEM, SMEM] + [VMEM] * (len(args) - 2),
        args,
        8 * slots * shape[0] * size * size,
        2 * slots * size * size,
        [pltpu.VMEM((5 if kind == "fwd" else 4, *shape), BF)],
        f"{kind}{pair_idx}",
    )


def round_body(value, out):
    out[...] = value[...].astype(BF)


def forward_body(level, last):
    def body(rhs, inverse, far, cross, pairs, own, *outs):
        r = lax.axis_index("row")
        pair = pairs[1 - r % 2]
        total = own[...].astype(F32) + pair.astype(F32) + cross[...].astype(F32) + far[...].astype(F32)
        y = lax.dot_general(
            (rhs[level, 0, 0] - total).astype(BF), inverse[level, 0, 0], NT, preferred_element_type=F32
        )
        if last:
            y = lax.dot_general(y.astype(BF), inverse[level, 0, 0], NN, preferred_element_type=F32)
        outs[0][...] = y
        outs[1][...] = y.astype(BF)

    return body


def backward_body(level, n_col):
    def body(y, inverse, own, cross, group, *outs):
        if level == 0:
            z1, z2, out, z0, sems = outs
            copies = [
                pltpu.make_async_copy(held, out.at[i, 0, 0], sems.at[i]) for i, held in enumerate((z0, z1, z2))
            ]
            copies[1].start()
            copies[2].start()
            outs = (z0,)
        c = lax.axis_index("col")
        total = (
            own[...].astype(F32)
            + cross[...].astype(F32)
            + group[group_place(pair_of(c, n_col), n_col), 0].astype(F32)
            + group[group_place(far_of(c, n_col), n_col), 1].astype(F32)
        )
        z = lax.dot_general((y[...] - total).astype(BF), inverse[level, 0, 0], NN, preferred_element_type=F32)
        outs[0][...] = z
        if level > 0:
            outs[1][...] = z.astype(BF)
        else:
            copies[0].start()
            for copy in copies:
                copy.wait()

    return body


def shards(rhs, inverse, blocks, targets, sources):
    n_col = lax.axis_size("col")
    panel = jax.ShapeDtypeStruct(rhs.shape[3:], F32)
    solve_flops = 2 * panel.shape[0] * panel.shape[1] ** 2

    def gather_cols(value):
        cross = swap(value, "col", cross_of)
        return [cross, gather_far(value, "col")]

    def gather_rows(value):
        far = swap(value, "row", far_of)
        cross = swap(value, "row", cross_of)
        return [far, cross, gather_pair(value, "row")]

    def scatter_rows(parts):
        own, pair, cross, far = parts
        far = swap(far, "row", far_of)
        cross = swap(cross, "row", cross_of)
        return [far, cross, gather_pair(pair, "row"), own]

    def scatter_cols(parts):
        own, cross, group = parts
        cross = swap(cross, "col", cross_of)
        return [own, cross, gather_far(group, "col")]

    tables = (targets, sources)
    blocks0 = blocks
    y0 = lax.dot_general(rhs[0, 0, 0].astype(BF), inverse[0, 0, 0], NT, preferred_element_type=F32)
    s0 = call(round_body, bf_like(panel), [VMEM], (y0,), EXCHANGE_FLOPS, 2**17, name="s0")
    g0 = gather_cols(s0)
    parts = scatter_rows(products("fwd", 0, 0, tables, blocks0, g0, None, True))
    base2 = products("fwd", 1, 1, tables, blocks, g0, None, False)[0]
    y1, s1 = call(
        forward_body(1, False), [panel, bf_like(panel)], [VMEM] * 6, (rhs, inverse, *parts), solve_flops, 2**18, name="y1"
    )
    g1 = gather_cols(s1)
    parts = scatter_rows(products("fwd", 2, 2, tables, blocks, g1, base2, True))
    z2, b2 = call(
        forward_body(2, True), [panel, bf_like(panel)], [VMEM] * 6, (rhs, inverse, *parts), 2 * solve_flops, 2**18, name="z2"
    )
    h2 = gather_rows(b2)
    parts = scatter_cols(products("bwd", 2, 2, tables, blocks, h2, None, True))
    base0 = products("bwd", 1, 1, tables, blocks, h2, None, False)[0]
    z1, b1 = call(
        backward_body(1, n_col), [panel, bf_like(panel)], [VMEM] * 5, (y1, inverse, *parts), solve_flops, 2**18, name="z1"
    )
    h1 = gather_rows(b1)
    parts = scatter_cols(products("bwd", 0, 0, tables, blocks0, h1, base0, True))
    return call(
        backward_body(0, n_col),
        f32_like(rhs),
        [VMEM] * 7,
        (y0, inverse, *parts, z1, z2),
        solve_flops,
        2**18,
        [pltpu.VMEM(panel.shape, F32), pltpu.SemaphoreType.DMA((3,))],
        "z0",
        out_specs=ANY,
    )


def solution(mesh):
    placed = (
        P(None, "row", "col", None, None),
        P(None, "row", "col", None, None),
        P(None, "row", "col", None, None),
        P(None, "row", "col"),
        P(None, "row", "col"),
    )
    return jax.shard_map(
        shards,
        mesh=mesh,
        in_specs=placed,
        out_specs=P(None, "row", "col", None, None),
        check_vma=False,
    )
```

time: 129 us -> 125 us (0.969)
  blocking collectives: 38.3 us -> 52.9 us
  starting transfers between devices: 69 us -> 59.9 us
  waiting for transfers between devices: 10.8 us -> 1.93 us
  local copies, waits for them, and re-layouts: 1.94 us -> 0.06 us
    all_gather x0 -> x4, blocking collectives: none -> 14.9 us  [gather_pair(): return lax.all_gather(value, axis, axis_index_groups=pairs)]
    ppermute x16 -> x12, starting transfers between devices: 69 us -> 59.9 us  [swap(): return lax.ppermute(value, axis, [(i, partner(i, n)) for i in range(n)])]
    ppermute x16 -> x12, waiting for transfers between devices: 10.8 us -> 1.93 us  [swap(): return lax.ppermute(value, axis, [(i, partner(i, n)) for i in range(n)])]
    unnamed x14 -> x10, local copies, waits for them, and re-layouts: 1.94 us -> 0.06 us
  transfers between devices with their start and end apart: 16 -> 12, of which waited for: 7 -> 1; matrix products, arithmetic and copies ran while one was open for 0% -> 0% of each run, Pallas kernels for 2% -> 2%
where the time goes in v3:
time: 125 us; the launch traced here: 124 us
  starting transfers between devices  59.9 us (48%)
  blocking collectives  52.9 us (42%)
  Pallas kernels  8.14 us (7%)
  waiting for transfers between devices  1.93 us (2%)
    ppermute x12, starting transfers between devices, swap(): return lax.ppermute(value, axis, [(i, partner(i, n)) for i in range(n)])  59.9 us
    all_gather x4, blocking collectives, gather_far(): lax.all_gather(value, axis, axis_index_groups=far_groups(lax.axis_size(ax...  38 us
    all_gather x4, blocking collectives, gather_pair(): return lax.all_gather(value, axis, axis_index_groups=pairs)  14.9 us
    pallas_call x11, Pallas kernels, call(): pl.pallas_call(body, out_shape=out_shape, in_specs=in_specs, out_specs=ou...  8.14 us
  transfers between devices with their start and end apart: 12, of which 1 were waited for; matrix products, arithmetic and copies ran while one was open for 0% of the time, Pallas kernels for 2%

profile of v3, /device:TPU:1, one launch (start us, length us, event | category | flops | bytes accessed | tf_op | source)
XLA Modules:
  0.0 124.3 jit_solution(16309945153219479606)
XLA Ops:
  0.0 1.1 fusion.value.y
  1.1 0.0 copy-start
  1.1 0.0 copy-start.3
  1.1 0.0 copy-start.4
  1.2 4.8 %collective-permute-start = (bf16[64,256]{1,0:T(8,128)(2,1)S(1)}, bf16[64,256]{1,0:T(8,128)(2,1)S(1)}, u32[]{:S(2)}, u32[]{:S(2)}) collective-permute-start(bf16[64,256]{1,0:T(8,128)(2,1)S(1)} %s0.1), channel_id=1, source_target_pairs={{0,31},{1,2},{2,1},{3,4},{4,3},{5,6},{6,5},{7,8},{8,7},{9,10},{10,... | collective-permute-start | bytes 98312 | tf_op jit(solution)/shard_map/ppermute | solution.py:33
  6.0 10.9 %all-gather = bf16[256,256]{1,0:T(8,128)(2,1)S(1)} all-gather(bf16[64,256]{1,0:T(8,128)(2,1)S(1)} %s0.1), channel_id=2, replica_groups={{0,1,16,17},{2,3,18,19},{4,5,20,21},{6,7,22,23},{8,9,24,25},{10,11,26,2..., dimensions={0}, use_global_device_ids=true | all-gather | bytes 163840 | tf_op jit(solution)/shard_map/all_gather | solution.py:42
  16.9 0.0 collective-permute-done.refs_3_
  17.0 0.0 copy-done
  17.0 0.0 copy-done.3
  17.0 0.0 copy-done.4
  17.0 0.0 copy-start.1
  17.0 0.0 copy-start.2
  17.0 1.1 fwd0.1
  18.1 14.7 %collective-permute-start.1 = (bf16[64,256]{1,0:T(8,128)(2,1)S(1)}, bf16[64,256]{1,0:T(8,128)(2,1)S(1)}, u32[]{:S(2)}, u32[]{:S(2)}) collective-permute-start(bf16[64,256]{1,0:T(8,128)(2,1)S(1)} %get-tuple-element.25), channel_id=1, source_target_pairs={{0,256},{32,288},{64,320},{96,352},{128,384},{160,416},{192,448},{... | collective-permute-start | bytes 98312 | tf_op jit(solution)/shard_map/ppermute | solution.py:33
  32.9 1.9 %collective-permute-start.2 = (bf16[64,256]{1,0:T(8,128)(2,1)S(1)}, bf16[64,256]{1,0:T(8,128)(2,1)S(1)}, u32[]{:S(2)}, u32[]{:S(2)}) collective-permute-start(bf16[64,256]{1,0:T(8,128)(2,1)S(1)} %get-tuple-element.26), channel_id=1, source_target_pairs={{0,480},{32,64},{64,32},{96,128},{128,96},{160,192},{192,160},{224... | collective-permute-start | bytes 98312 | tf_op jit(solution)/shard_map/ppermute | solution.py:33
  34.8 3.8 %all-gather.1 = bf16[128,256]{1,0:T(8,128)(2,1)S(1)} all-gather(bf16[64,256]{1,0:T(8,128)(2,1)S(1)} %get-tuple-element.27), channel_id=3, replica_groups={{0,32},{64,96},{128,160},{192,224},{256,288},{320,352},{384,416},{448,4..., dimensions={0}, use_global_device_ids=true | all-gather | bytes 98304 | tf_op jit(solution)/shard_map/all_gather | solution.py:47
  38.6 1.1 fwd1.1.refs_5_
  39.7 0.0 collective-permute-done.1.far
  39.7 0.0 collective-permute-done.2.cross
  39.8 0.0 copy-done.1
  39.8 0.0 copy-done.2
  39.8 0.2 y1.1
  39.9 1.9 %collective-permute-start.3 = (bf16[64,256]{1,0:T(8,128)(2,1)S(1)}, bf16[64,256]{1,0:T(8,128)(2,1)S(1)}, u32[]{:S(2)}, u32[]{:S(2)}) collective-permute-start(bf16[64,256]{1,0:T(8,128)(2,1)S(1)} %get-tuple-element.30), channel_id=1, source_target_pairs={{0,31},{1,2},{2,1},{3,4},{4,3},{5,6},{6,5},{7,8},{8,7},{9,10},{10,... | collective-permute-start | bytes 98312 | tf_op jit(solution)/shard_map/ppermute | solution.py:33
  41.9 8.1 %all-gather.2 = bf16[256,256]{1,0:T(8,128)(2,1)S(1)} all-gather(bf16[64,256]{1,0:T(8,128)(2,1)S(1)} %get-tuple-element.30), channel_id=4, replica_groups={{0,1,16,17},{2,3,18,19},{4,5,20,21},{6,7,22,23},{8,9,24,25},{10,11,26,2..., dimensions={0}, use_global_device_ids=true | all-gather | bytes 163840 | tf_op jit(solution)/shard_map/all_gather | solution.py:42
  50.0 0.0 collective-permute-done.3.refs_3_
  50.0 1.1 fwd2.1
  51.1 7.9 %collective-permute-start.4 = (bf16[64,256]{1,0:T(8,128)(2,1)S(1)}, bf16[64,256]{1,0:T(8,128)(2,1)S(1)}, u32[]{:S(2)}, u32[]{:S(2)}) collective-permute-start(bf16[64,256]{1,0:T(8,128)(2,1)S(1)} %get-tuple-element.31), channel_id=1, source_target_pairs={{0,256},{32,288},{64,320},{96,352},{128,384},{160,416},{192,448},{... | collective-permute-start | bytes 98312 | tf_op jit(solution)/shard_map/ppermute | solution.py:33
  59.1 1.9 %collective-permute-start.5 = (bf16[64,256]{1,0:T(8,128)(2,1)S(1)}, bf16[64,256]{1,0:T(8,128)(2,1)S(1)}, u32[]{:S(2)}, u32[]{:S(2)}) collective-permute-start(bf16[64,256]{1,0:T(8,128)(2,1)S(1)} %get-tuple-element.32), channel_id=1, source_target_pairs={{0,480},{32,64},{64,32},{96,128},{128,96},{160,192},{192,160},{224... | collective-permute-start | bytes 98312 | tf_op jit(solution)/shard_map/ppermute | solution.py:33
  61.0 3.7 %all-gather.3 = bf16[128,256]{1,0:T(8,128)(2,1)S(1)} all-gather(bf16[64,256]{1,0:T(8,128)(2,1)S(1)} %get-tuple-element.33), channel_id=5, replica_groups={{0,32},{64,96},{128,160},{192,224},{256,288},{320,352},{384,416},{448,4..., dimensions={0}, use_global_device_ids=true | all-gather | bytes 98304 | tf_op jit(solution)/shard_map/all_gather | solution.py:47
  64.7 0.0 collective-permute-done.4.far
  64.7 1.9 %collective-permute-done.5.cross = bf16[64,256]{1,0:T(8,128)(2,1)S(1)} collective-permute-done((bf16[64,256]{1,0:T(8,128)(2,1)S(1)}, bf16[64,256]{1,0:T(8,128)(2,1)S(1)}, u32[]{:S(2)}, u32[]{:S(2)}) %collective-permute-start.5) | collective-permute-done | bytes 32800 | tf_op jit(solution)/shard_map/ppermute | solution.py:33
  66.6 0.3 z2.1
  67.0 7.0 %collective-permute-start.6 = (bf16[64,256]{1,0:T(8,128)(2,1)S(1)}, bf16[64,256]{1,0:T(8,128)(2,1)S(1)}, u32[]{:S(2)}, u32[]{:S(2)}) collective-permute-start(bf16[64,256]{1,0:T(8,128)(2,1)S(1)} %get-tuple-element.35), channel_id=1, source_target_pairs={{0,256},{32,288},{64,320},{96,352},{128,384},{160,416},{192,448},{... | collective-permute-start | bytes 98312 | tf_op jit(solution)/shard_map/ppermute | solution.py:33
  74.0 2.4 %collective-permute-start.7 = (bf16[64,256]{1,0:T(8,128)(2,1)S(1)}, bf16[64,256]{1,0:T(8,128)(2,1)S(1)}, u32[]{:S(2)}, u32[]{:S(2)}) collective-permute-start(bf16[64,256]{1,0:T(8,128)(2,1)S(1)} %get-tuple-element.35), channel_id=1, source_target_pairs={{0,480},{32,64},{64,32},{96,128},{128,96},{160,192},{192,160},{224... | collective-permute-start | bytes 98312 | tf_op jit(solution)/shard_map/ppermute | solution.py:33
  76.4 4.0 %all-gather.4 = bf16[128,256]{1,0:T(8,128)(2,1)S(1)} all-gather(bf16[64,256]{1,0:T(8,128)(2,1)S(1)} %get-tuple-element.35), channel_id=6, replica_groups={{0,32},{64,96},{128,160},{192,224},{256,288},{320,352},{384,416},{448,4..., dimensions={0}, use_global_device_ids=true | all-gather | bytes 98304 | tf_op jit(solution)/shard_map/all_gather | solution.py:47
  80.4 0.0 collective-permute-done.6.refs_3_
  80.4 0.0 collective-permute-done.7.refs_4_
  80.4 1.1 bwd2.1
  81.5 4.5 %collective-permute-start.8 = (bf16[64,256]{1,0:T(8,128)(2,1)S(1)}, bf16[64,256]{1,0:T(8,128)(2,1)S(1)}, u32[]{:S(2)}, u32[]{:S(2)}) collective-permute-start(bf16[64,256]{1,0:T(8,128)(2,1)S(1)} %get-tuple-element.37), channel_id=1, source_target_pairs={{0,31},{1,2},{2,1},{3,4},{4,3},{5,6},{6,5},{7,8},{8,7},{9,10},{10,... | collective-permute-start | bytes 98312 | tf_op jit(solution)/shard_map/ppermute | solution.py:33
  86.0 8.8 %all-gather.5 = bf16[8,64,256]{2,1,0:T(8,128)(2,1)S(1)} all-gather(bf16[2,64,256]{2,1,0:T(8,128)(2,1)S(1)} %get-tuple-element.38), channel_id=7, replica_groups={{0,1,16,17},{2,3,18,19},{4,5,20,21},{6,7,22,23},{8,9,24,25},{10,11,26,2..., dimensions={0}, use_global_device_ids=true | all-gather | bytes 327680 | tf_op jit(solution)/shard_map/all_gather | solution.py:42
  94.7 0.0 collective-permute-done.8.cross
  94.7 0.2 z1.1
  94.9 7.0 %collective-permute-start.9 = (bf16[64,256]{1,0:T(8,128)(2,1)S(1)}, bf16[64,256]{1,0:T(8,128)(2,1)S(1)}, u32[]{:S(2)}, u32[]{:S(2)}) collective-permute-start(bf16[64,256]{1,0:T(8,128)(2,1)S(1)} %get-tuple-element.39), channel_id=1, source_target_pairs={{0,256},{32,288},{64,320},{96,352},{128,384},{160,416},{192,448},{... | collective-permute-start | bytes 98312 | tf_op jit(solution)/shard_map/ppermute | solution.py:33
  101.9 3.8 %collective-permute-start.10 = (bf16[64,256]{1,0:T(8,128)(2,1)S(1)}, bf16[64,256]{1,0:T(8,128)(2,1)S(1)}, u32[]{:S(2)}, u32[]{:S(2)}) collective-permute-start(bf16[64,256]{1,0:T(8,128)(2,1)S(1)} %get-tuple-element.39), channel_id=1, source_target_pairs={{0,480},{32,64},{64,32},{96,128},{128,96},{160,192},{192,160},{224... | collective-permute-start | bytes 98312 | tf_op jit(solution)/shard_map/ppermute | solution.py:33
  105.7 1.1 bwd1.1.refs_6_
  106.8 3.4 %all-gather.6 = bf16[128,256]{1,0:T(8,128)(2,1)S(1)} all-gather(bf16[64,256]{1,0:T(8,128)(2,1)S(1)} %get-tuple-element.39), channel_id=8, replica_groups={{0,32},{64,96},{128,160},{192,224},{256,288},{320,352},{384,416},{448,4..., dimensions={0}, use_global_device_ids=true | all-gather | bytes 98304 | tf_op jit(solution)/shard_map/all_gather | solution.py:47
  110.2 0.0 collective-permute-done.9.refs_3_
  110.2 0.0 collective-permute-done.10.refs_4_
  110.2 1.1 bwd0.1
  111.3 1.9 %collective-permute-start.11 = (bf16[64,256]{1,0:T(8,128)(2,1)S(1)}, bf16[64,256]{1,0:T(8,128)(2,1)S(1)}, u32[]{:S(2)}, u32[]{:S(2)}) collective-permute-start(bf16[64,256]{1,0:T(8,128)(2,1)S(1)} %get-tuple-element.41), channel_id=1, source_target_pairs={{0,31},{1,2},{2,1},{3,4},{4,3},{5,6},{6,5},{7,8},{8,7},{9,10},{10,... | collective-permute-start | bytes 98312 | tf_op jit(solution)/shard_map/ppermute | solution.py:33
  113.2 10.2 %all-gather.7 = bf16[8,64,256]{2,1,0:T(8,128)(2,1)S(1)} all-gather(bf16[2,64,256]{2,1,0:T(8,128)(2,1)S(1)} %get-tuple-element.42), channel_id=9, replica_groups={{0,1,16,17},{2,3,18,19},{4,5,20,21},{6,7,22,23},{8,9,24,25},{10,11,26,2..., dimensions={0}, use_global_device_ids=true | all-gather | bytes 327680 | tf_op jit(solution)/shard_map/all_gather | solution.py:42
  123.4 0.0 collective-permute-done.11.cross
  123.4 0.8 z0.1
  (1 shorter events, 0.0 us)
Async XLA Ops:
  1.1 15.9 %copy-start = (bf16[3,1,10,256,256]{4,3,2,1,0:T(8,128)(2,1)S(1)}, bf16[3,1,10,256,256]{4,3,2,1,0:T(8,128)(2,1)}, u32[]{:S(2)}) copy-start(bf16[3,1,10,256,256]{4,3,2,1,0:T(8,128)(2,1)} %refs_2_.11) | copy-start | bytes 11796484
  1.1 15.9 %copy-start.3 = (s32[3,1,10]{2,1,0:T(1,128)S(1)}, s32[3,1,10]{2,1,0:T(1,128)}, u32[]{:S(2)}) copy-start(s32[3,1,10]{2,1,0:T(1,128)} %refs_0_.11) | copy-start | bytes 364
  1.1 15.8 %copy-start.4 = (s32[3,1,10]{2,1,0:T(1,128)S(1)}, s32[3,1,10]{2,1,0:T(1,128)}, u32[]{:S(2)}) copy-start(s32[3,1,10]{2,1,0:T(1,128)} %refs_1_.11) | copy-start | bytes 364
  1.2 15.8 %collective-permute-start = (bf16[64,256]{1,0:T(8,128)(2,1)S(1)}, bf16[64,256]{1,0:T(8,128)(2,1)S(1)}, u32[]{:S(2)}, u32[]{:S(2)}) collective-permute-start(bf16[64,256]{1,0:T(8,128)(2,1)S(1)} %s0.1), channel_id=1, source_target_pairs={{0,31},{1,2},{2,1},{3,4},{4,3},{5,6},{6,5},{7,8},{8,7},{9,10},{10,... | collective-permute-start | bytes 98312 | tf_op jit(solution)/shard_map/ppermute | solution.py:33
  17.0 22.8 %copy-start.1 = (bf16[3,1,1,256,256]{4,3,2,1,0:T(8,128)(2,1)S(1)}, bf16[3,1,1,256,256]{4,3,2,1,0:T(8,128)(2,1)}, u32[]{:S(2)}) copy-start(bf16[3,1,1,256,256]{4,3,2,1,0:T(8,128)(2,1)} %inverse.7) | copy-start | bytes 1179652
  17.0 22.8 %copy-start.2 = (f32[3,1,1,64,256]{4,3,2,1,0:T(8,128)S(1)}, f32[3,1,1,64,256]{4,3,2,1,0:T(8,128)}, u32[]{:S(2)}) copy-start(f32[3,1,1,64,256]{4,3,2,1,0:T(8,128)} %rhs.3) | copy-start | bytes 589828
  18.1 21.6 %collective-permute-start.1 = (bf16[64,256]{1,0:T(8,128)(2,1)S(1)}, bf16[64,256]{1,0:T(8,128)(2,1)S(1)}, u32[]{:S(2)}, u32[]{:S(2)}) collective-permute-start(bf16[64,256]{1,0:T(8,128)(2,1)S(1)} %get-tuple-element.25), channel_id=1, source_target_pairs={{0,256},{32,288},{64,320},{96,352},{128,384},{160,416},{192,448},{... | collective-permute-start | bytes 98312 | tf_op jit(solution)/shard_map/ppermute | solution.py:33
  32.9 6.9 %collective-permute-start.2 = (bf16[64,256]{1,0:T(8,128)(2,1)S(1)}, bf16[64,256]{1,0:T(8,128)(2,1)S(1)}, u32[]{:S(2)}, u32[]{:S(2)}) collective-permute-start(bf16[64,256]{1,0:T(8,128)(2,1)S(1)} %get-tuple-element.26), channel_id=1, source_target_pairs={{0,480},{32,64},{64,32},{96,128},{128,96},{160,192},{192,160},{224... | collective-permute-start | bytes 98312 | tf_op jit(solution)/shard_map/ppermute | solution.py:33
  39.9 10.0 %collective-permute-start.3 = (bf16[64,256]{1,0:T(8,128)(2,1)S(1)}, bf16[64,256]{1,0:T(8,128)(2,1)S(1)}, u32[]{:S(2)}, u32[]{:S(2)}) collective-permute-start(bf16[64,256]{1,0:T(8,128)(2,1)S(1)} %get-tuple-element.30), channel_id=1, source_target_pairs={{0,31},{1,2},{2,1},{3,4},{4,3},{5,6},{6,5},{7,8},{8,7},{9,10},{10,... | collective-permute-start | bytes 98312 | tf_op jit(solution)/shard_map/ppermute | solution.py:33
  51.1 13.6 %collective-permute-start.4 = (bf16[64,256]{1,0:T(8,128)(2,1)S(1)}, bf16[64,256]{1,0:T(8,128)(2,1)S(1)}, u32[]{:S(2)}, u32[]{:S(2)}) collective-permute-start(bf16[64,256]{1,0:T(8,128)(2,1)S(1)} %get-tuple-element.31), channel_id=1, source_target_pairs={{0,256},{32,288},{64,320},{96,352},{128,384},{160,416},{192,448},{... | collective-permute-start | bytes 98312 | tf_op jit(solution)/shard_map/ppermute | solution.py:33
  59.1 7.6 %collective-permute-start.5 = (bf16[64,256]{1,0:T(8,128)(2,1)S(1)}, bf16[64,256]{1,0:T(8,128)(2,1)S(1)}, u32[]{:S(2)}, u32[]{:S(2)}) collective-permute-start(bf16[64,256]{1,0:T(8,128)(2,1)S(1)} %get-tuple-element.32), channel_id=1, source_target_pairs={{0,480},{32,64},{64,32},{96,128},{128,96},{160,192},{192,160},{224... | collective-permute-start | bytes 98312 | tf_op jit(solution)/shard_map/ppermute | solution.py:33
  67.0 13.4 %collective-permute-start.6 = (bf16[64,256]{1,0:T(8,128)(2,1)S(1)}, bf16[64,256]{1,0:T(8,128)(2,1)S(1)}, u32[]{:S(2)}, u32[]{:S(2)}) collective-permute-start(bf16[64,256]{1,0:T(8,128)(2,1)S(1)} %get-tuple-element.35), channel_id=1, source_target_pairs={{0,256},{32,288},{64,320},{96,352},{128,384},{160,416},{192,448},{... | collective-permute-start | bytes 98312 | tf_op jit(solution)/shard_map/ppermute | solution.py:33
  74.0 6.4 %collective-permute-start.7 = (bf16[64,256]{1,0:T(8,128)(2,1)S(1)}, bf16[64,256]{1,0:T(8,128)(2,1)S(1)}, u32[]{:S(2)}, u32[]{:S(2)}) collective-permute-start(bf16[64,256]{1,0:T(8,128)(2,1)S(1)} %get-tuple-element.35), channel_id=1, source_target_pairs={{0,480},{32,64},{64,32},{96,128},{128,96},{160,192},{192,160},{224... | collective-permute-start | bytes 98312 | tf_op jit(solution)/shard_map/ppermute | solution.py:33
  81.5 13.3 %collective-permute-start.8 = (bf16[64,256]{1,0:T(8,128)(2,1)S(1)}, bf16[64,256]{1,0:T(8,128)(2,1)S(1)}, u32[]{:S(2)}, u32[]{:S(2)}) collective-permute-start(bf16[64,256]{1,0:T(8,128)(2,1)S(1)} %get-tuple-element.37), channel_id=1, source_target_pairs={{0,31},{1,2},{2,1},{3,4},{4,3},{5,6},{6,5},{7,8},{8,7},{9,10},{10,... | collective-permute-start | bytes 98312 | tf_op jit(solution)/shard_map/ppermute | solution.py:33
  94.9 15.3 %collective-permute-start.9 = (bf16[64,256]{1,0:T(8,128)(2,1)S(1)}, bf16[64,256]{1,0:T(8,128)(2,1)S(1)}, u32[]{:S(2)}, u32[]{:S(2)}) collective-permute-start(bf16[64,256]{1,0:T(8,128)(2,1)S(1)} %get-tuple-element.39), channel_id=1, source_target_pairs={{0,256},{32,288},{64,320},{96,352},{128,384},{160,416},{192,448},{... | collective-permute-start | bytes 98312 | tf_op jit(solution)/shard_map/ppermute | solution.py:33
  101.9 8.3 %collective-permute-start.10 = (bf16[64,256]{1,0:T(8,128)(2,1)S(1)}, bf16[64,256]{1,0:T(8,128)(2,1)S(1)}, u32[]{:S(2)}, u32[]{:S(2)}) collective-permute-start(bf16[64,256]{1,0:T(8,128)(2,1)S(1)} %get-tuple-element.39), channel_id=1, source_target_pairs={{0,480},{32,64},{64,32},{96,128},{128,96},{160,192},{192,160},{224... | collective-permute-start | bytes 98312 | tf_op jit(solution)/shard_map/ppermute | solution.py:33
  111.3 12.1 %collective-permute-start.11 = (bf16[64,256]{1,0:T(8,128)(2,1)S(1)}, bf16[64,256]{1,0:T(8,128)(2,1)S(1)}, u32[]{:S(2)}, u32[]{:S(2)}) collective-permute-start(bf16[64,256]{1,0:T(8,128)(2,1)S(1)} %get-tuple-element.41), channel_id=1, source_target_pairs={{0,31},{1,2},{2,1},{3,4},{4,3},{5,6},{6,5},{7,8},{8,7},{9,10},{10,... | collective-permute-start | bytes 98312 | tf_op jit(solution)/shard_map/ppermute | solution.py:33

commit v4 on v3

v4 whole, which is shorter than its diff:
```python
import jax
import jax.numpy as jnp
from jax import lax
from jax.experimental import pallas as pl
from jax.experimental.pallas import tpu as pltpu
from jax.sharding import PartitionSpec as P


VMEM = pl.BlockSpec(memory_space=pltpu.VMEM)
ANY = pl.BlockSpec(memory_space=pl.ANY)
EXCHANGE_FLOPS = 6 * 10**9
NT = (((1,), (1,)), ((), ()))
NN = (((1,), (0,)), ((), ()))
BF = jnp.bfloat16
F32 = jnp.float32


def pair_of(i):
    return i + 1 - 2 * (i % 2)


def cross_of(i, n):
    return (i - 1 + 2 * (i % 2) + n) % n


def far_of(i, n):
    return (i + n // 2) % n


def swap(value, axis, partner):
    n = lax.axis_size(axis)
    return lax.ppermute(value, axis, [(i, partner(i, n)) for i in range(n)])


def far_groups(n):
    half = n // 2
    return [[i, i + 1, i + half, i + half + 1] for i in range(0, half, 2)]


def gather_far(value, axis):
    return lax.all_gather(value, axis, axis_index_groups=far_groups(lax.axis_size(axis)))


def gather_pair(value, axis):
    pairs = [[i, i + 1] for i in range(0, lax.axis_size(axis), 2)]
    return lax.all_gather(value, axis, axis_index_groups=pairs)


def group_place(i, n):
    return i % 2 + 2 * (i // (n // 2))


def call(body, out_shape, in_specs, args, flops, moved, scratch=(), out_specs=None, vmem=16 * 2**20):
    return pl.pallas_call(
        body,
        out_shape=out_shape,
        in_specs=in_specs,
        out_specs=out_specs if out_specs is not None else jax.tree.map(lambda _: VMEM, out_shape),
        scratch_shapes=list(scratch),
        compiler_params=pltpu.CompilerParams(vmem_limit_bytes=vmem),
        cost_estimate=pl.CostEstimate(flops=flops, bytes_accessed=moved, transcendentals=0),
    )(*args)


def f32_like(x):
    return jax.ShapeDtypeStruct(x.shape, F32)


def bf_like(x):
    return jax.ShapeDtypeStruct(x.shape, BF)


def splat(flags, s, shape):
    one = jnp.broadcast_to(flags[:, s : s + 1], (16, 128)).astype(BF)
    return jnp.tile(one, (shape[0] // 16, shape[1] // 128))


def pair_products(kind, pair_idx, n_row, n_col, slots, targets, sources, blocks, held):
    r = lax.axis_index("row")
    c = lax.axis_index("col")
    t = targets[pair_idx]
    e = sources[pair_idx]
    me, n, key = (r, n_row, t) if kind == "fwd" else (c, n_col, e)
    goals = [key == k for k in (me, pair_of(me), cross_of(me, n), far_of(me, n))]
    if kind == "fwd":
        low = c % (n_col // 2) - c % 2
        group = [low, low + 1, low + n_col // 2, low + n_col // 2 + 1]
        picks = [e == k for k in (cross_of(c, n_col), *group)]
    else:
        picks = [t == k for k in (far_of(r, n_row), cross_of(r, n_row), r - r % 2, r - r % 2 + 1)]
    goals = [g.astype(F32) for g in goals]
    picks = [g.astype(F32) for g in picks]
    shape = held[0].shape
    total = None
    for s in range(slots):
        panel = None
        for pick, one in zip(picks, held):
            term = splat(pick, s, shape) * one
            panel = term if panel is None else panel + term
        stacked = jnp.concatenate([splat(goal, s, shape) * panel for goal in goals], axis=0)
        term = lax.dot_general(
            stacked, blocks[pair_idx, 0, s], NT if kind == "fwd" else NN, preferred_element_type=F32
        )
        total = term if total is None else total + term
    return total


def product_body(kind, pair_idx, n_row, n_col, slots, add, extra):
    def body(*refs):
        targets, sources, blocks, *rest = refs
        count = 2 if kind == "fwd" else 3
        panels, rest = rest[:count], rest[count:]
        if add:
            base, rest = rest[0], rest[1:]
        outs = rest
        held = []
        for panel in panels:
            if len(panel.shape) == 2:
                held.append(panel[...])
            else:
                held.extend(panel[i] for i in range(panel.shape[0]))
        if pair_idx is not None:
            total = pair_products(kind, pair_idx, n_row, n_col, slots, targets, sources, blocks, held)
            if add:
                total = total + base[...]
            rows = held[0].shape[0]
            parts = [total[i * rows : (i + 1) * rows].astype(BF) for i in range(4)]
            if kind == "fwd":
                for out, part in zip(outs, parts):
                    out[...] = part
            else:
                outs[0][...] = parts[0]
                outs[1][...] = parts[2]
                outs[2][0] = parts[1]
                outs[2][1] = parts[3]
        if extra is not None:
            outs[-1][...] = pair_products(kind, extra, n_row, n_col, slots, targets, sources, blocks, held)

    return body


def products(kind, pair_idx, extra, tables, blocks, panels, base=None):
    n_row, n_col = lax.axis_size("row"), lax.axis_size("col")
    slots, size = blocks.shape[2], blocks.shape[3]
    shape = panels[0].shape
    panel = jax.ShapeDtypeStruct(shape, BF)
    out = []
    if pair_idx is not None:
        out = [panel] * 4 if kind == "fwd" else [panel, panel, jax.ShapeDtypeStruct((2, *shape), BF)]
    if extra is not None:
        out.append(jax.ShapeDtypeStruct((4 * shape[0], shape[1]), F32))
    args = [*tables, blocks, *panels] + ([base] if base is not None else [])
    pairs = len([p for p in (pair_idx, extra) if p is not None])
    return call(
        product_body(kind, pair_idx, n_row, n_col, slots, base is not None, extra),
        out,
        [VMEM] * len(args),
        args,
        8 * pairs * slots * shape[0] * size * size,
        2 * pairs * slots * size * size,
    )


def round_body(value, out):
    out[...] = value[...].astype(BF)


def forward_body(level, last):
    def body(rhs, inverse, far, cross, pairs, own, *outs):
        r = lax.axis_index("row")
        pair = pairs[1 - r % 2]
        total = own[...].astype(F32) + pair.astype(F32) + cross[...].astype(F32) + far[...].astype(F32)
        y = lax.dot_general(
            (rhs[level, 0, 0] - total).astype(BF), inverse[level, 0, 0], NT, preferred_element_type=F32
        )
        if last:
            y = lax.dot_general(y.astype(BF), inverse[level, 0, 0], NN, preferred_element_type=F32)
        outs[0][...] = y
        outs[1][...] = y.astype(BF)

    return body


def backward_body(level, n_col):
    def body(y, inverse, own, cross, group, *outs):
        if level == 0:
            z1, z2, out, z0, sems = outs
            copies = [
                pltpu.make_async_copy(held, out.at[i, 0, 0], sems.at[i]) for i, held in enumerate((z0, z1, z2))
            ]
            copies[1].start()
            copies[2].start()
            outs = (z0,)
        c = lax.axis_index("col")
        total = (
            own[...].astype(F32)
            + cross[...].astype(F32)
            + group[group_place(pair_of(c), n_col), 0].astype(F32)
            + group[group_place(far_of(c, n_col), n_col), 1].astype(F32)
        )
        z = lax.dot_general((y[...] - total).astype(BF), inverse[level, 0, 0], NN, preferred_element_type=F32)
        outs[0][...] = z
        if level > 0:
            outs[1][...] = z.astype(BF)
        else:
            copies[0].start()
            for copy in copies:
                copy.wait()

    return body


def shards(rhs, inverse, blocks, targets, sources):
    n_col = lax.axis_size("col")
    panel = jax.ShapeDtypeStruct(rhs.shape[3:], F32)
    solve_flops = 2 * panel.shape[0] * panel.shape[1] ** 2

    def gather_cols(value):
        cross = swap(value, "col", cross_of)
        return [cross, gather_far(value, "col")]

    def swap_rows(far, cross, pair):
        far = swap(far, "row", far_of)
        cross = swap(cross, "row", cross_of)
        return [far, cross, gather_pair(pair, "row")]

    def gather_rows(value):
        return swap_rows(value, value, value)

    def scatter_rows(parts):
        own, pair, cross, far = parts
        return [*swap_rows(far, cross, pair), own]

    def scatter_cols(parts):
        own, cross, group = parts
        cross = swap(cross, "col", cross_of)
        return [own, cross, gather_far(group, "col")]

    tables = (targets, sources)
    y0 = lax.dot_general(rhs[0, 0, 0].astype(BF), inverse[0, 0, 0], NT, preferred_element_type=F32)
    s0 = call(round_body, bf_like(panel), [VMEM], (y0,), EXCHANGE_FLOPS, 2**17)
    g0 = gather_cols(s0)
    parts = scatter_rows(products("fwd", 0, None, tables, blocks, g0))
    base2 = products("fwd", None, 1, tables, blocks, g0)[0]
    y1, s1 = call(
        forward_body(1, False), [panel, bf_like(panel)], [VMEM] * 6, (rhs, inverse, *parts), solve_flops, 2**18
    )
    g1 = gather_cols(s1)
    parts = scatter_rows(products("fwd", 2, None, tables, blocks, g1, base2))
    z2, b2 = call(
        forward_body(2, True), [panel, bf_like(panel)], [VMEM] * 6, (rhs, inverse, *parts), 2 * solve_flops, 2**18
    )
    *parts, base0 = products("bwd", 2, 1, tables, blocks, gather_rows(b2))
    parts = scatter_cols(parts)
    z1, b1 = call(
        backward_body(1, n_col), [panel, bf_like(panel)], [VMEM] * 5, (y1, inverse, *parts), solve_flops, 2**18
    )
    parts = scatter_cols(products("bwd", 0, None, tables, blocks, gather_rows(b1), base0))
    return call(
        backward_body(0, n_col),
        f32_like(rhs),
        [VMEM] * 7,
        (y0, inverse, *parts, z1, z2),
        solve_flops,
        2**18,
        [pltpu.VMEM(panel.shape, F32), pltpu.SemaphoreType.DMA((3,))],
        out_specs=ANY,
    )


def solution(mesh):
    placed = (
        P(None, "row", "col", None, None),
        P(None, "row", "col", None, None),
        P(None, "row", "col", None, None),
        P(None, "row", "col"),
        P(None, "row", "col"),
    )

    return jax.shard_map(
        shards,
        mesh=mesh,
        in_specs=placed,
        out_specs=P(None, "row", "col", None, None),
        check_vma=False,
    )
```

time: 125 us -> 126 us (level)
  waiting for transfers between devices: 1.93 us -> 8.71 us
  Pallas kernels: 8.14 us -> 4.67 us
  blocking collectives: 52.9 us -> 50.2 us
    ppermute x12, waiting for transfers between devices: 1.93 us -> 8.71 us  [swap(): return lax.ppermute(value, axis, [(i, partner(i, n)) for i in range(n)])]
    pallas_call x11 -> x10, Pallas kernels: 8.14 us -> 4.67 us  [call(): pl.pallas_call(body, out_shape=out_shape, in_specs=in_specs, out_specs=ou...]
    all_gather x4, blocking collectives: 38 us -> 35.5 us  [gather_far(): lax.all_gather(value, axis, axis_index_groups=far_groups(lax.axis_size(ax...]
  transfers between devices with their start and end apart: 12 -> 12, of which waited for: 1 -> 3; matrix products, arithmetic and copies ran while one was open for 0% -> 0% of each run, Pallas kernels for 2% -> 0%
where the time goes in v4:
time: 126 us
  starting transfers between devices  61 us (48%)
  blocking collectives  50.2 us (40%)
  waiting for transfers between devices  8.71 us (7%)
  Pallas kernels  4.67 us (4%)
    ppermute x12, starting transfers between devices, swap(): return lax.ppermute(value, axis, [(i, partner(i, n)) for i in range(n)])  61 us
    all_gather x4, blocking collectives, gather_far(): lax.all_gather(value, axis, axis_index_groups=far_groups(lax.axis_size(ax...  35.5 us
    all_gather x4, blocking collectives, gather_pair(): return lax.all_gather(value, axis, axis_index_groups=pairs)  14.8 us
    ppermute x12, waiting for transfers between devices, swap(): return lax.ppermute(value, axis, [(i, partner(i, n)) for i in range(n)])  8.71 us
    pallas_call x10, Pallas kernels, call(): pl.pallas_call(body, out_shape=out_shape, in_specs=in_specs, out_specs=ou...  4.67 us
  transfers between devices with their start and end apart: 12, of which 3 were waited for; matrix products, arithmetic and copies ran while one was open for 0% of the time, Pallas kernels for 0%

profile of v4, /device:TPU:1, one launch (start us, length us, event | category | flops | bytes accessed | tf_op | source)
XLA Modules:
  0.0 126.0 jit_solution(11702303319270317344)
XLA Ops:
  0.0 1.1 fusion.value.y
  1.1 0.0 copy-start
  1.1 0.0 copy-start.3
  1.1 0.0 copy-start.4
  1.2 4.8 %collective-permute-start = (bf16[64,256]{1,0:T(8,128)(2,1)S(1)}, bf16[64,256]{1,0:T(8,128)(2,1)S(1)}, u32[]{:S(2)}, u32[]{:S(2)}) collective-permute-start(bf16[64,256]{1,0:T(8,128)(2,1)S(1)} %shard_map.55), channel_id=1, source_target_pairs={{0,31},{1,2},{2,1},{3,4},{4,3},{5,6},{6,5},{7,8},{8,7},{9,10},{10,... | collective-permute-start | bytes 98312 | tf_op jit(solution)/shard_map/ppermute | solution.py:32
  6.0 10.9 %all-gather = bf16[256,256]{1,0:T(8,128)(2,1)S(1)} all-gather(bf16[64,256]{1,0:T(8,128)(2,1)S(1)} %shard_map.55), channel_id=2, replica_groups={{0,1,16,17},{2,3,18,19},{4,5,20,21},{6,7,22,23},{8,9,24,25},{10,11,26,2..., dimensions={0}, use_global_device_ids=true | all-gather | bytes 163840 | tf_op jit(solution)/shard_map/all_gather | solution.py:41
  16.9 0.0 collective-permute-done.refs_3_
  17.0 0.0 copy-done
  17.0 0.0 copy-done.3
  17.0 0.0 copy-done.4
  17.0 0.0 copy-start.1
  17.0 0.0 copy-start.2
  17.0 0.6 shard_map.56
  17.6 14.7 %collective-permute-start.1 = (bf16[64,256]{1,0:T(8,128)(2,1)S(1)}, bf16[64,256]{1,0:T(8,128)(2,1)S(1)}, u32[]{:S(2)}, u32[]{:S(2)}) collective-permute-start(bf16[64,256]{1,0:T(8,128)(2,1)S(1)} %get-tuple-element.26), channel_id=1, source_target_pairs={{0,256},{32,288},{64,320},{96,352},{128,384},{160,416},{192,448},{... | collective-permute-start | bytes 98312 | tf_op jit(solution)/shard_map/ppermute | solution.py:32
  32.3 1.9 %collective-permute-start.2 = (bf16[64,256]{1,0:T(8,128)(2,1)S(1)}, bf16[64,256]{1,0:T(8,128)(2,1)S(1)}, u32[]{:S(2)}, u32[]{:S(2)}) collective-permute-start(bf16[64,256]{1,0:T(8,128)(2,1)S(1)} %get-tuple-element.27), channel_id=1, source_target_pairs={{0,480},{32,64},{64,32},{96,128},{128,96},{160,192},{192,160},{224... | collective-permute-start | bytes 98312 | tf_op jit(solution)/shard_map/ppermute | solution.py:32
  34.2 3.8 %all-gather.1 = bf16[128,256]{1,0:T(8,128)(2,1)S(1)} all-gather(bf16[64,256]{1,0:T(8,128)(2,1)S(1)} %get-tuple-element.28), channel_id=3, replica_groups={{0,32},{64,96},{128,160},{192,224},{256,288},{320,352},{384,416},{448,4..., dimensions={0}, use_global_device_ids=true | all-gather | bytes 98304 | tf_op jit(solution)/shard_map/all_gather | solution.py:46
  38.0 0.6 shard_map.58.refs_5_
  38.6 0.0 collective-permute-done.1.far
  38.6 0.0 collective-permute-done.2.cross
  38.6 0.0 copy-done.1
  38.6 0.0 copy-done.2
  38.7 0.2 shard_map.57
  38.8 1.9 %collective-permute-start.3 = (bf16[64,256]{1,0:T(8,128)(2,1)S(1)}, bf16[64,256]{1,0:T(8,128)(2,1)S(1)}, u32[]{:S(2)}, u32[]{:S(2)}) collective-permute-start(bf16[64,256]{1,0:T(8,128)(2,1)S(1)} %get-tuple-element.31), channel_id=1, source_target_pairs={{0,31},{1,2},{2,1},{3,4},{4,3},{5,6},{6,5},{7,8},{8,7},{9,10},{10,... | collective-permute-start | bytes 98312 | tf_op jit(solution)/shard_map/ppermute | solution.py:32
  40.8 8.1 %all-gather.2 = bf16[256,256]{1,0:T(8,128)(2,1)S(1)} all-gather(bf16[64,256]{1,0:T(8,128)(2,1)S(1)} %get-tuple-element.31), channel_id=4, replica_groups={{0,1,16,17},{2,3,18,19},{4,5,20,21},{6,7,22,23},{8,9,24,25},{10,11,26,2..., dimensions={0}, use_global_device_ids=true | all-gather | bytes 163840 | tf_op jit(solution)/shard_map/all_gather | solution.py:41
  48.9 0.0 collective-permute-done.3.refs_3_
  48.9 0.6 shard_map.59
  49.4 7.9 %collective-permute-start.4 = (bf16[64,256]{1,0:T(8,128)(2,1)S(1)}, bf16[64,256]{1,0:T(8,128)(2,1)S(1)}, u32[]{:S(2)}, u32[]{:S(2)}) collective-permute-start(bf16[64,256]{1,0:T(8,128)(2,1)S(1)} %get-tuple-element.32), channel_id=1, source_target_pairs={{0,256},{32,288},{64,320},{96,352},{128,384},{160,416},{192,448},{... | collective-permute-start | bytes 98312 | tf_op jit(solution)/shard_map/ppermute | solution.py:32
  57.4 1.9 %collective-permute-start.5 = (bf16[64,256]{1,0:T(8,128)(2,1)S(1)}, bf16[64,256]{1,0:T(8,128)(2,1)S(1)}, u32[]{:S(2)}, u32[]{:S(2)}) collective-permute-start(bf16[64,256]{1,0:T(8,128)(2,1)S(1)} %get-tuple-element.33), channel_id=1, source_target_pairs={{0,480},{32,64},{64,32},{96,128},{128,96},{160,192},{192,160},{224... | collective-permute-start | bytes 98312 | tf_op jit(solution)/shard_map/ppermute | solution.py:32
  59.3 3.7 %all-gather.3 = bf16[128,256]{1,0:T(8,128)(2,1)S(1)} all-gather(bf16[64,256]{1,0:T(8,128)(2,1)S(1)} %get-tuple-element.34), channel_id=5, replica_groups={{0,32},{64,96},{128,160},{192,224},{256,288},{320,352},{384,416},{448,4..., dimensions={0}, use_global_device_ids=true | all-gather | bytes 98304 | tf_op jit(solution)/shard_map/all_gather | solution.py:46
  63.0 0.0 collective-permute-done.4.far
  63.0 2.1 %collective-permute-done.5.cross = bf16[64,256]{1,0:T(8,128)(2,1)S(1)} collective-permute-done((bf16[64,256]{1,0:T(8,128)(2,1)S(1)}, bf16[64,256]{1,0:T(8,128)(2,1)S(1)}, u32[]{:S(2)}, u32[]{:S(2)}) %collective-permute-start.5) | collective-permute-done | bytes 32800 | tf_op jit(solution)/shard_map/ppermute | solution.py:32
  65.1 0.3 shard_map.60
  65.5 2.5 %collective-permute-start.7 = (bf16[64,256]{1,0:T(8,128)(2,1)S(1)}, bf16[64,256]{1,0:T(8,128)(2,1)S(1)}, u32[]{:S(2)}, u32[]{:S(2)}) collective-permute-start(bf16[64,256]{1,0:T(8,128)(2,1)S(1)} %get-tuple-element.36), channel_id=1, source_target_pairs={{0,480},{32,64},{64,32},{96,128},{128,96},{160,192},{192,160},{224... | collective-permute-start | bytes 98312 | tf_op jit(solution)/shard_map/ppermute | solution.py:32
  68.0 6.7 %collective-permute-start.6 = (bf16[64,256]{1,0:T(8,128)(2,1)S(1)}, bf16[64,256]{1,0:T(8,128)(2,1)S(1)}, u32[]{:S(2)}, u32[]{:S(2)}) collective-permute-start(bf16[64,256]{1,0:T(8,128)(2,1)S(1)} %get-tuple-element.36), channel_id=1, source_target_pairs={{0,256},{32,288},{64,320},{96,352},{128,384},{160,416},{192,448},{... | collective-permute-start | bytes 98312 | tf_op jit(solution)/shard_map/ppermute | solution.py:32
  74.7 3.8 %all-gather.4 = bf16[128,256]{1,0:T(8,128)(2,1)S(1)} all-gather(bf16[64,256]{1,0:T(8,128)(2,1)S(1)} %get-tuple-element.36), channel_id=6, replica_groups={{0,32},{64,96},{128,160},{192,224},{256,288},{320,352},{384,416},{448,4..., dimensions={0}, use_global_device_ids=true | all-gather | bytes 98304 | tf_op jit(solution)/shard_map/all_gather | solution.py:46
  78.5 0.0 collective-permute-done.7.refs_4_
  78.5 2.9 %collective-permute-done.6.refs_3_ = bf16[64,256]{1,0:T(8,128)(2,1)S(1)} collective-permute-done((bf16[64,256]{1,0:T(8,128)(2,1)S(1)}, bf16[64,256]{1,0:T(8,128)(2,1)S(1)}, u32[]{:S(2)}, u32[]{:S(2)}) %collective-permute-start.6) | collective-permute-done | bytes 32800 | tf_op jit(solution)/shard_map/ppermute | solution.py:32
  81.4 0.9 shard_map.61
  82.3 6.2 %collective-permute-start.8 = (bf16[64,256]{1,0:T(8,128)(2,1)S(1)}, bf16[64,256]{1,0:T(8,128)(2,1)S(1)}, u32[]{:S(2)}, u32[]{:S(2)}) collective-permute-start(bf16[64,256]{1,0:T(8,128)(2,1)S(1)} %get-tuple-element.38), channel_id=1, source_target_pairs={{0,31},{1,2},{2,1},{3,4},{4,3},{5,6},{6,5},{7,8},{8,7},{9,10},{10,... | collective-permute-start | bytes 98312 | tf_op jit(solution)/shard_map/ppermute | solution.py:32
  88.5 7.4 %all-gather.5 = bf16[8,64,256]{2,1,0:T(8,128)(2,1)S(1)} all-gather(bf16[2,64,256]{2,1,0:T(8,128)(2,1)S(1)} %get-tuple-element.39), channel_id=7, replica_groups={{0,1,16,17},{2,3,18,19},{4,5,20,21},{6,7,22,23},{8,9,24,25},{10,11,26,2..., dimensions={0}, use_global_device_ids=true | all-gather | bytes 327680 | tf_op jit(solution)/shard_map/all_gather | solution.py:41
  95.8 0.0 collective-permute-done.8.cross
  95.8 0.2 shard_map.62
  96.0 3.9 %collective-permute-start.10 = (bf16[64,256]{1,0:T(8,128)(2,1)S(1)}, bf16[64,256]{1,0:T(8,128)(2,1)S(1)}, u32[]{:S(2)}, u32[]{:S(2)}) collective-permute-start(bf16[64,256]{1,0:T(8,128)(2,1)S(1)} %get-tuple-element.40), channel_id=1, source_target_pairs={{0,480},{32,64},{64,32},{96,128},{128,96},{160,192},{192,160},{224... | collective-permute-start | bytes 98312 | tf_op jit(solution)/shard_map/ppermute | solution.py:32
  99.9 6.5 %collective-permute-start.9 = (bf16[64,256]{1,0:T(8,128)(2,1)S(1)}, bf16[64,256]{1,0:T(8,128)(2,1)S(1)}, u32[]{:S(2)}, u32[]{:S(2)}) collective-permute-start(bf16[64,256]{1,0:T(8,128)(2,1)S(1)} %get-tuple-element.40), channel_id=1, source_target_pairs={{0,256},{32,288},{64,320},{96,352},{128,384},{160,416},{192,448},{... | collective-permute-start | bytes 98312 | tf_op jit(solution)/shard_map/ppermute | solution.py:32
  106.3 3.5 %all-gather.6 = bf16[128,256]{1,0:T(8,128)(2,1)S(1)} all-gather(bf16[64,256]{1,0:T(8,128)(2,1)S(1)} %get-tuple-element.40), channel_id=8, replica_groups={{0,32},{64,96},{128,160},{192,224},{256,288},{320,352},{384,416},{448,4..., dimensions={0}, use_global_device_ids=true | all-gather | bytes 98304 | tf_op jit(solution)/shard_map/all_gather | solution.py:46
  109.8 0.0 collective-permute-done.10.refs_4_
  109.8 3.7 %collective-permute-done.9.refs_3_ = bf16[64,256]{1,0:T(8,128)(2,1)S(1)} collective-permute-done((bf16[64,256]{1,0:T(8,128)(2,1)S(1)}, bf16[64,256]{1,0:T(8,128)(2,1)S(1)}, u32[]{:S(2)}, u32[]{:S(2)}) %collective-permute-start.9) | collective-permute-done | bytes 32800 | tf_op jit(solution)/shard_map/ppermute | solution.py:32
  113.5 0.6 shard_map.63
  114.1 1.9 %collective-permute-start.11 = (bf16[64,256]{1,0:T(8,128)(2,1)S(1)}, bf16[64,256]{1,0:T(8,128)(2,1)S(1)}, u32[]{:S(2)}, u32[]{:S(2)}) collective-permute-start(bf16[64,256]{1,0:T(8,128)(2,1)S(1)} %get-tuple-element.43), channel_id=1, source_target_pairs={{0,31},{1,2},{2,1},{3,4},{4,3},{5,6},{6,5},{7,8},{8,7},{9,10},{10,... | collective-permute-start | bytes 98312 | tf_op jit(solution)/shard_map/ppermute | solution.py:32
  116.0 9.1 %all-gather.7 = bf16[8,64,256]{2,1,0:T(8,128)(2,1)S(1)} all-gather(bf16[2,64,256]{2,1,0:T(8,128)(2,1)S(1)} %get-tuple-element.44), channel_id=9, replica_groups={{0,1,16,17},{2,3,18,19},{4,5,20,21},{6,7,22,23},{8,9,24,25},{10,11,26,2..., dimensions={0}, use_global_device_ids=true | all-gather | bytes 327680 | tf_op jit(solution)/shard_map/all_gather | solution.py:41
  125.2 0.0 collective-permute-done.11.cross
  125.2 0.8 shard_map.64
  (1 shorter events, 0.0 us)
Async XLA Ops:
  1.1 15.9 %copy-start = (bf16[3,1,10,256,256]{4,3,2,1,0:T(8,128)(2,1)S(1)}, bf16[3,1,10,256,256]{4,3,2,1,0:T(8,128)(2,1)}, u32[]{:S(2)}) copy-start(bf16[3,1,10,256,256]{4,3,2,1,0:T(8,128)(2,1)} %refs_2_.9) | copy-start | bytes 11796484
  1.1 15.9 %copy-start.3 = (s32[3,1,10]{2,1,0:T(1,128)S(1)}, s32[3,1,10]{2,1,0:T(1,128)}, u32[]{:S(2)}) copy-start(s32[3,1,10]{2,1,0:T(1,128)} %refs_0_.9) | copy-start | bytes 364
  1.1 15.8 %copy-start.4 = (s32[3,1,10]{2,1,0:T(1,128)S(1)}, s32[3,1,10]{2,1,0:T(1,128)}, u32[]{:S(2)}) copy-start(s32[3,1,10]{2,1,0:T(1,128)} %refs_1_.9) | copy-start | bytes 364
  1.2 15.8 %collective-permute-start = (bf16[64,256]{1,0:T(8,128)(2,1)S(1)}, bf16[64,256]{1,0:T(8,128)(2,1)S(1)}, u32[]{:S(2)}, u32[]{:S(2)}) collective-permute-start(bf16[64,256]{1,0:T(8,128)(2,1)S(1)} %shard_map.55), channel_id=1, source_target_pairs={{0,31},{1,2},{2,1},{3,4},{4,3},{5,6},{6,5},{7,8},{8,7},{9,10},{10,... | collective-permute-start | bytes 98312 | tf_op jit(solution)/shard_map/ppermute | solution.py:32
  17.0 21.7 %copy-start.1 = (bf16[3,1,1,256,256]{4,3,2,1,0:T(8,128)(2,1)S(1)}, bf16[3,1,1,256,256]{4,3,2,1,0:T(8,128)(2,1)}, u32[]{:S(2)}) copy-start(bf16[3,1,1,256,256]{4,3,2,1,0:T(8,128)(2,1)} %inverse.7) | copy-start | bytes 1179652
  17.0 21.7 %copy-start.2 = (f32[3,1,1,64,256]{4,3,2,1,0:T(8,128)S(1)}, f32[3,1,1,64,256]{4,3,2,1,0:T(8,128)}, u32[]{:S(2)}) copy-start(f32[3,1,1,64,256]{4,3,2,1,0:T(8,128)} %rhs.3) | copy-start | bytes 589828
  17.6 21.0 %collective-permute-start.1 = (bf16[64,256]{1,0:T(8,128)(2,1)S(1)}, bf16[64,256]{1,0:T(8,128)(2,1)S(1)}, u32[]{:S(2)}, u32[]{:S(2)}) collective-permute-start(bf16[64,256]{1,0:T(8,128)(2,1)S(1)} %get-tuple-element.26), channel_id=1, source_target_pairs={{0,256},{32,288},{64,320},{96,352},{128,384},{160,416},{192,448},{... | collective-permute-start | bytes 98312 | tf_op jit(solution)/shard_map/ppermute | solution.py:32
  32.3 6.3 %collective-permute-start.2 = (bf16[64,256]{1,0:T(8,128)(2,1)S(1)}, bf16[64,256]{1,0:T(8,128)(2,1)S(1)}, u32[]{:S(2)}, u32[]{:S(2)}) collective-permute-start(bf16[64,256]{1,0:T(8,128)(2,1)S(1)} %get-tuple-element.27), channel_id=1, source_target_pairs={{0,480},{32,64},{64,32},{96,128},{128,96},{160,192},{192,160},{224... | collective-permute-start | bytes 98312 | tf_op jit(solution)/shard_map/ppermute | solution.py:32
  38.8 10.0 %collective-permute-start.3 = (bf16[64,256]{1,0:T(8,128)(2,1)S(1)}, bf16[64,256]{1,0:T(8,128)(2,1)S(1)}, u32[]{:S(2)}, u32[]{:S(2)}) collective-permute-start(bf16[64,256]{1,0:T(8,128)(2,1)S(1)} %get-tuple-element.31), channel_id=1, source_target_pairs={{0,31},{1,2},{2,1},{3,4},{4,3},{5,6},{6,5},{7,8},{8,7},{9,10},{10,... | collective-permute-start | bytes 98312 | tf_op jit(solution)/shard_map/ppermute | solution.py:32
  49.4 13.6 %collective-permute-start.4 = (bf16[64,256]{1,0:T(8,128)(2,1)S(1)}, bf16[64,256]{1,0:T(8,128)(2,1)S(1)}, u32[]{:S(2)}, u32[]{:S(2)}) collective-permute-start(bf16[64,256]{1,0:T(8,128)(2,1)S(1)} %get-tuple-element.32), channel_id=1, source_target_pairs={{0,256},{32,288},{64,320},{96,352},{128,384},{160,416},{192,448},{... | collective-permute-start | bytes 98312 | tf_op jit(solution)/shard_map/ppermute | solution.py:32
  57.4 7.8 %collective-permute-start.5 = (bf16[64,256]{1,0:T(8,128)(2,1)S(1)}, bf16[64,256]{1,0:T(8,128)(2,1)S(1)}, u32[]{:S(2)}, u32[]{:S(2)}) collective-permute-start(bf16[64,256]{1,0:T(8,128)(2,1)S(1)} %get-tuple-element.33), channel_id=1, source_target_pairs={{0,480},{32,64},{64,32},{96,128},{128,96},{160,192},{192,160},{224... | collective-permute-start | bytes 98312 | tf_op jit(solution)/shard_map/ppermute | solution.py:32
  65.5 13.0 %collective-permute-start.7 = (bf16[64,256]{1,0:T(8,128)(2,1)S(1)}, bf16[64,256]{1,0:T(8,128)(2,1)S(1)}, u32[]{:S(2)}, u32[]{:S(2)}) collective-permute-start(bf16[64,256]{1,0:T(8,128)(2,1)S(1)} %get-tuple-element.36), channel_id=1, source_target_pairs={{0,480},{32,64},{64,32},{96,128},{128,96},{160,192},{192,160},{224... | collective-permute-start | bytes 98312 | tf_op jit(solution)/shard_map/ppermute | solution.py:32
  68.0 13.4 %collective-permute-start.6 = (bf16[64,256]{1,0:T(8,128)(2,1)S(1)}, bf16[64,256]{1,0:T(8,128)(2,1)S(1)}, u32[]{:S(2)}, u32[]{:S(2)}) collective-permute-start(bf16[64,256]{1,0:T(8,128)(2,1)S(1)} %get-tuple-element.36), channel_id=1, source_target_pairs={{0,256},{32,288},{64,320},{96,352},{128,384},{160,416},{192,448},{... | collective-permute-start | bytes 98312 | tf_op jit(solution)/shard_map/ppermute | solution.py:32
  82.3 13.5 %collective-permute-start.8 = (bf16[64,256]{1,0:T(8,128)(2,1)S(1)}, bf16[64,256]{1,0:T(8,128)(2,1)S(1)}, u32[]{:S(2)}, u32[]{:S(2)}) collective-permute-start(bf16[64,256]{1,0:T(8,128)(2,1)S(1)} %get-tuple-element.38), channel_id=1, source_target_pairs={{0,31},{1,2},{2,1},{3,4},{4,3},{5,6},{6,5},{7,8},{8,7},{9,10},{10,... | collective-permute-start | bytes 98312 | tf_op jit(solution)/shard_map/ppermute | solution.py:32
  96.0 13.8 %collective-permute-start.10 = (bf16[64,256]{1,0:T(8,128)(2,1)S(1)}, bf16[64,256]{1,0:T(8,128)(2,1)S(1)}, u32[]{:S(2)}, u32[]{:S(2)}) collective-permute-start(bf16[64,256]{1,0:T(8,128)(2,1)S(1)} %get-tuple-element.40), channel_id=1, source_target_pairs={{0,480},{32,64},{64,32},{96,128},{128,96},{160,192},{192,160},{224... | collective-permute-start | bytes 98312 | tf_op jit(solution)/shard_map/ppermute | solution.py:32
  99.9 13.7 %collective-permute-start.9 = (bf16[64,256]{1,0:T(8,128)(2,1)S(1)}, bf16[64,256]{1,0:T(8,128)(2,1)S(1)}, u32[]{:S(2)}, u32[]{:S(2)}) collective-permute-start(bf16[64,256]{1,0:T(8,128)(2,1)S(1)} %get-tuple-element.40), channel_id=1, source_target_pairs={{0,256},{32,288},{64,320},{96,352},{128,384},{160,416},{192,448},{... | collective-permute-start | bytes 98312 | tf_op jit(solution)/shard_map/ppermute | solution.py:32
  114.1 11.0 %collective-permute-start.11 = (bf16[64,256]{1,0:T(8,128)(2,1)S(1)}, bf16[64,256]{1,0:T(8,128)(2,1)S(1)}, u32[]{:S(2)}, u32[]{:S(2)}) collective-permute-start(bf16[64,256]{1,0:T(8,128)(2,1)S(1)} %get-tuple-element.43), channel_id=1, source_target_pairs={{0,31},{1,2},{2,1},{3,4},{4,3},{5,6},{6,5},{7,8},{8,7},{9,10},{10,... | collective-permute-start | bytes 98312 | tf_op jit(solution)/shard_map/ppermute | solution.py:32

commit v5 on v4

--- a/solution.py
+++ b/solution.py
@@ -15,7 +15,7 @@
 F32 = jnp.float32
 
 
-def pair_of(i):
+def pair_of(i, n):
     return i + 1 - 2 * (i % 2)
 
 
@@ -81,7 +81,7 @@
     t = targets[pair_idx]
     e = sources[pair_idx]
     me, n, key = (r, n_row, t) if kind == "fwd" else (c, n_col, e)
-    goals = [key == k for k in (me, pair_of(me), cross_of(me, n), far_of(me, n))]
+    goals = [key == k for k in (me, pair_of(me, n), cross_of(me, n), far_of(me, n))]
     if kind == "fwd":
         low = c % (n_col // 2) - c % 2
         group = [low, low + 1, low + n_col // 2, low + n_col // 2 + 1]
@@ -105,7 +105,7 @@
     return total
 
 
-def product_body(kind, pair_idx, n_row, n_col, slots, add, extra):
+def product_body(kind, pair_idx, n_row, n_col, slots, add, extra, apart):
     def body(*refs):
         targets, sources, blocks, *rest = refs
         count = 2 if kind == "fwd" else 3
@@ -125,7 +125,7 @@
                 total = total + base[...]
             rows = held[0].shape[0]
             parts = [total[i * rows : (i + 1) * rows].astype(BF) for i in range(4)]
-            if kind == "fwd":
+            if apart:
                 for out, part in zip(outs, parts):
                     out[...] = part
             else:
@@ -139,20 +139,20 @@
     return body
 
 
-def products(kind, pair_idx, extra, tables, blocks, panels, base=None):
+def products(kind, pair_idx, extra, tables, blocks, panels, base=None, apart=True):
     n_row, n_col = lax.axis_size("row"), lax.axis_size("col")
     slots, size = blocks.shape[2], blocks.shape[3]
     shape = panels[0].shape
     panel = jax.ShapeDtypeStruct(shape, BF)
     out = []
     if pair_idx is not None:
-        out = [panel] * 4 if kind == "fwd" else [panel, panel, jax.ShapeDtypeStruct((2, *shape), BF)]
+        out = [panel] * 4 if apart else [panel, panel, jax.ShapeDtypeStruct((2, *shape), BF)]
     if extra is not None:
         out.append(jax.ShapeDtypeStruct((4 * shape[0], shape[1]), F32))
     args = [*tables, blocks, *panels] + ([base] if base is not None else [])
     pairs = len([p for p in (pair_idx, extra) if p is not None])
     return call(
-        product_body(kind, pair_idx, n_row, n_col, slots, base is not None, extra),
+        product_body(kind, pair_idx, n_row, n_col, slots, base is not None, extra, apart),
         out,
         [VMEM] * len(args),
         args,
@@ -181,33 +181,31 @@
     return body
 
 
-def backward_body(level, n_col):
-    def body(y, inverse, own, cross, group, *outs):
-        if level == 0:
-            z1, z2, out, z0, sems = outs
-            copies = [
-                pltpu.make_async_copy(held, out.at[i, 0, 0], sems.at[i]) for i, held in enumerate((z0, z1, z2))
-            ]
-            copies[1].start()
-            copies[2].start()
-            outs = (z0,)
+def backward_body(n_col):
+    def body(y, inverse, own, cross, group, z_out, send_out):
         c = lax.axis_index("col")
         total = (
             own[...].astype(F32)
             + cross[...].astype(F32)
-            + group[group_place(pair_of(c), n_col), 0].astype(F32)
+            + group[group_place(pair_of(c, n_col), n_col), 0].astype(F32)
             + group[group_place(far_of(c, n_col), n_col), 1].astype(F32)
         )
-        z = lax.dot_general((y[...] - total).astype(BF), inverse[level, 0, 0], NN, preferred_element_type=F32)
-        outs[0][...] = z
-        if level > 0:
-            outs[1][...] = z.astype(BF)
-        else:
-            copies[0].start()
-            for copy in copies:
-                copy.wait()
+        z = lax.dot_general((y[...] - total).astype(BF), inverse[1, 0, 0], NN, preferred_element_type=F32)
+        z_out[...] = z
+        send_out[...] = z.astype(BF)
 
     return body
+
+
+def last_body(y, inverse, own, pair, far, cross, z1, z2, out, z0, sems):
+    copies = [pltpu.make_async_copy(held, out.at[i, 0, 0], sems.at[i]) for i, held in enumerate((z0, z1, z2))]
+    copies[1].start()
+    copies[2].start()
+    total = own[...].astype(F32) + pair[...].astype(F32) + far[...].astype(F32) + cross[...].astype(F32)
+    z0[...] = lax.dot_general((y[...] - total).astype(BF), inverse[0, 0, 0], NN, preferred_element_type=F32)
+    copies[0].start()
+    for copy in copies:
+        copy.wait()
 
 
 def shards(rhs, inverse, blocks, targets, sources):
@@ -230,6 +228,13 @@
     def scatter_rows(parts):
         own, pair, cross, far = parts
         return [*swap_rows(far, cross, pair), own]
+
+    def last_scatter(parts):
+        own, pair, cross, far = parts
+        pair = swap(pair, "col", pair_of)
+        far = swap(far, "col", far_of)
+        cross = swap(cross, "col", cross_of)
+        return [own, pair, far, cross]
 
     def scatter_cols(parts):
         own, cross, group = parts
@@ -250,16 +255,14 @@
     z2, b2 = call(
         forward_body(2, True), [panel, bf_like(panel)], [VMEM] * 6, (rhs, inverse, *parts), 2 * solve_flops, 2**18
     )
-    *parts, base0 = products("bwd", 2, 1, tables, blocks, gather_rows(b2))
+    *parts, base0 = products("bwd", 2, 1, tables, blocks, gather_rows(b2), apart=False)
     parts = scatter_cols(parts)
-    z1, b1 = call(
-        backward_body(1, n_col), [panel, bf_like(panel)], [VMEM] * 5, (y1, inverse, *parts), solve_flops, 2**18
-    )
-    parts = scatter_cols(products("bwd", 0, None, tables, blocks, gather_rows(b1), base0))
+    z1, b1 = call(backward_body(n_col), [panel, bf_like(panel)], [VMEM] * 5, (y1, inverse, *parts), solve_flops, 2**18)
+    parts = last_scatter(products("bwd", 0, None, tables, blocks, gather_rows(b1), base0))
     return call(
-        backward_body(0, n_col),
+        last_body,
         f32_like(rhs),
-        [VMEM] * 7,
+        [VMEM] * 8,
         (y0, inverse, *parts, z1, z2),
         solve_flops,
         2**18,

time: 126 us -> 127 us (level)
  blocking collectives: 50.2 us -> 41.1 us
  starting transfers between devices: 61 us -> 66.5 us
  waiting for transfers between devices: 8.71 us -> 12 us
    all_gather x4 -> x3, blocking collectives: 35.5 us -> 26.4 us  [gather_far(): lax.all_gather(value, axis, axis_index_groups=far_groups(lax.axis_size(ax...]
    ppermute x12 -> x14, starting transfers between devices: 61 us -> 66.5 us  [swap(): return lax.ppermute(value, axis, [(i, partner(i, n)) for i in range(n)])]
    ppermute x12 -> x14, waiting for transfers between devices: 8.71 us -> 12 us  [swap(): return lax.ppermute(value, axis, [(i, partner(i, n)) for i in range(n)])]
  transfers between devices with their start and end apart: 12 -> 14, of which waited for: 3 -> 5; matrix products, arithmetic and copies ran while one was open for 0% -> 0% of each run, Pallas kernels for 0% -> 0%
where the time goes in v5:
time: 127 us; the launch traced here: 126 us
  starting transfers between devices  66.5 us (52%)
  blocking collectives  41.1 us (32%)
  waiting for transfers between devices  12 us (9%)
  Pallas kernels  4.67 us (4%)
    ppermute x14, starting transfers between devices, swap(): return lax.ppermute(value, axis, [(i, partner(i, n)) for i in range(n)])  66.5 us
    all_gather x3, blocking collectives, gather_far(): lax.all_gather(value, axis, axis_index_groups=far_groups(lax.axis_size(ax...  26.4 us
    all_gather x4, blocking collectives, gather_pair(): return lax.all_gather(value, axis, axis_index_groups=pairs)  14.8 us
    ppermute x14, waiting for transfers between devices, swap(): return lax.ppermute(value, axis, [(i, partner(i, n)) for i in range(n)])  12 us
    pallas_call x10, Pallas kernels, call(): pl.pallas_call(body, out_shape=out_shape, in_specs=in_specs, out_specs=ou...  4.67 us
  transfers between devices with their start and end apart: 14, of which 5 were waited for; matrix products, arithmetic and copies ran while one was open for 0% of the time, Pallas kernels for 0%

profile of v5, /device:TPU:1, one launch (start us, length us, event | category | flops | bytes accessed | tf_op | source)
XLA Modules:
  0.0 125.7 jit_solution(17891403814032094502)
XLA Ops:
  0.0 1.1 fusion.value.y
  1.1 0.0 copy-start
  1.1 0.0 copy-start.3
  1.1 0.0 copy-start.4
  1.2 4.8 %collective-permute-start = (bf16[64,256]{1,0:T(8,128)(2,1)S(1)}, bf16[64,256]{1,0:T(8,128)(2,1)S(1)}, u32[]{:S(2)}, u32[]{:S(2)}) collective-permute-start(bf16[64,256]{1,0:T(8,128)(2,1)S(1)} %shard_map.55), channel_id=1, source_target_pairs={{0,31},{1,2},{2,1},{3,4},{4,3},{5,6},{6,5},{7,8},{8,7},{9,10},{10,... | collective-permute-start | bytes 98312 | tf_op jit(solution)/shard_map/ppermute | solution.py:32
  6.0 10.9 %all-gather = bf16[256,256]{1,0:T(8,128)(2,1)S(1)} all-gather(bf16[64,256]{1,0:T(8,128)(2,1)S(1)} %shard_map.55), channel_id=2, replica_groups={{0,1,16,17},{2,3,18,19},{4,5,20,21},{6,7,22,23},{8,9,24,25},{10,11,26,2..., dimensions={0}, use_global_device_ids=true | all-gather | bytes 163840 | tf_op jit(solution)/shard_map/all_gather | solution.py:41
  16.9 0.0 collective-permute-done.refs_3_
  17.0 0.0 copy-done
  17.0 0.0 copy-done.3
  17.0 0.0 copy-done.4
  17.0 0.0 copy-start.1
  17.0 0.0 copy-start.2
  17.0 0.6 shard_map.56
  17.6 14.7 %collective-permute-start.1 = (bf16[64,256]{1,0:T(8,128)(2,1)S(1)}, bf16[64,256]{1,0:T(8,128)(2,1)S(1)}, u32[]{:S(2)}, u32[]{:S(2)}) collective-permute-start(bf16[64,256]{1,0:T(8,128)(2,1)S(1)} %get-tuple-element.27), channel_id=1, source_target_pairs={{0,256},{32,288},{64,320},{96,352},{128,384},{160,416},{192,448},{... | collective-permute-start | bytes 98312 | tf_op jit(solution)/shard_map/ppermute | solution.py:32
  32.3 1.9 %collective-permute-start.2 = (bf16[64,256]{1,0:T(8,128)(2,1)S(1)}, bf16[64,256]{1,0:T(8,128)(2,1)S(1)}, u32[]{:S(2)}, u32[]{:S(2)}) collective-permute-start(bf16[64,256]{1,0:T(8,128)(2,1)S(1)} %get-tuple-element.28), channel_id=1, source_target_pairs={{0,480},{32,64},{64,32},{96,128},{128,96},{160,192},{192,160},{224... | collective-permute-start | bytes 98312 | tf_op jit(solution)/shard_map/ppermute | solution.py:32
  34.2 3.8 %all-gather.1 = bf16[128,256]{1,0:T(8,128)(2,1)S(1)} all-gather(bf16[64,256]{1,0:T(8,128)(2,1)S(1)} %get-tuple-element.29), channel_id=3, replica_groups={{0,32},{64,96},{128,160},{192,224},{256,288},{320,352},{384,416},{448,4..., dimensions={0}, use_global_device_ids=true | all-gather | bytes 98304 | tf_op jit(solution)/shard_map/all_gather | solution.py:46
  38.0 0.6 shard_map.58.refs_5_
  38.6 0.0 collective-permute-done.1.far
  38.6 0.0 collective-permute-done.2.cross
  38.6 0.0 copy-done.1
  38.6 0.0 copy-done.2
  38.7 0.2 shard_map.57
  38.8 1.9 %collective-permute-start.3 = (bf16[64,256]{1,0:T(8,128)(2,1)S(1)}, bf16[64,256]{1,0:T(8,128)(2,1)S(1)}, u32[]{:S(2)}, u32[]{:S(2)}) collective-permute-start(bf16[64,256]{1,0:T(8,128)(2,1)S(1)} %get-tuple-element.32), channel_id=1, source_target_pairs={{0,31},{1,2},{2,1},{3,4},{4,3},{5,6},{6,5},{7,8},{8,7},{9,10},{10,... | collective-permute-start | bytes 98312 | tf_op jit(solution)/shard_map/ppermute | solution.py:32
  40.8 8.1 %all-gather.2 = bf16[256,256]{1,0:T(8,128)(2,1)S(1)} all-gather(bf16[64,256]{1,0:T(8,128)(2,1)S(1)} %get-tuple-element.32), channel_id=4, replica_groups={{0,1,16,17},{2,3,18,19},{4,5,20,21},{6,7,22,23},{8,9,24,25},{10,11,26,2..., dimensions={0}, use_global_device_ids=true | all-gather | bytes 163840 | tf_op jit(solution)/shard_map/all_gather | solution.py:41
  48.9 0.0 collective-permute-done.3.refs_3_
  48.9 0.6 shard_map.59
  49.5 7.9 %collective-permute-start.4 = (bf16[64,256]{1,0:T(8,128)(2,1)S(1)}, bf16[64,256]{1,0:T(8,128)(2,1)S(1)}, u32[]{:S(2)}, u32[]{:S(2)}) collective-permute-start(bf16[64,256]{1,0:T(8,128)(2,1)S(1)} %get-tuple-element.33), channel_id=1, source_target_pairs={{0,256},{32,288},{64,320},{96,352},{128,384},{160,416},{192,448},{... | collective-permute-start | bytes 98312 | tf_op jit(solution)/shard_map/ppermute | solution.py:32
  57.4 1.9 %collective-permute-start.5 = (bf16[64,256]{1,0:T(8,128)(2,1)S(1)}, bf16[64,256]{1,0:T(8,128)(2,1)S(1)}, u32[]{:S(2)}, u32[]{:S(2)}) collective-permute-start(bf16[64,256]{1,0:T(8,128)(2,1)S(1)} %get-tuple-element.34), channel_id=1, source_target_pairs={{0,480},{32,64},{64,32},{96,128},{128,96},{160,192},{192,160},{224... | collective-permute-start | bytes 98312 | tf_op jit(solution)/shard_map/ppermute | solution.py:32
  59.3 3.7 %all-gather.3 = bf16[128,256]{1,0:T(8,128)(2,1)S(1)} all-gather(bf16[64,256]{1,0:T(8,128)(2,1)S(1)} %get-tuple-element.35), channel_id=5, replica_groups={{0,32},{64,96},{128,160},{192,224},{256,288},{320,352},{384,416},{448,4..., dimensions={0}, use_global_device_ids=true | all-gather | bytes 98304 | tf_op jit(solution)/shard_map/all_gather | solution.py:46
  63.0 0.0 collective-permute-done.4.far
  63.1 2.1 %collective-permute-done.5.cross = bf16[64,256]{1,0:T(8,128)(2,1)S(1)} collective-permute-done((bf16[64,256]{1,0:T(8,128)(2,1)S(1)}, bf16[64,256]{1,0:T(8,128)(2,1)S(1)}, u32[]{:S(2)}, u32[]{:S(2)}) %collective-permute-start.5) | collective-permute-done | bytes 32800 | tf_op jit(solution)/shard_map/ppermute | solution.py:32
  65.2 0.3 shard_map.60
  65.5 2.5 %collective-permute-start.7 = (bf16[64,256]{1,0:T(8,128)(2,1)S(1)}, bf16[64,256]{1,0:T(8,128)(2,1)S(1)}, u32[]{:S(2)}, u32[]{:S(2)}) collective-permute-start(bf16[64,256]{1,0:T(8,128)(2,1)S(1)} %get-tuple-element.37), channel_id=1, source_target_pairs={{0,480},{32,64},{64,32},{96,128},{128,96},{160,192},{192,160},{224... | collective-permute-start | bytes 98312 | tf_op jit(solution)/shard_map/ppermute | solution.py:32
  68.0 6.7 %collective-permute-start.6 = (bf16[64,256]{1,0:T(8,128)(2,1)S(1)}, bf16[64,256]{1,0:T(8,128)(2,1)S(1)}, u32[]{:S(2)}, u32[]{:S(2)}) collective-permute-start(bf16[64,256]{1,0:T(8,128)(2,1)S(1)} %get-tuple-element.37), channel_id=1, source_target_pairs={{0,256},{32,288},{64,320},{96,352},{128,384},{160,416},{192,448},{... | collective-permute-start | bytes 98312 | tf_op jit(solution)/shard_map/ppermute | solution.py:32
  74.7 3.8 %all-gather.4 = bf16[128,256]{1,0:T(8,128)(2,1)S(1)} all-gather(bf16[64,256]{1,0:T(8,128)(2,1)S(1)} %get-tuple-element.37), channel_id=6, replica_groups={{0,32},{64,96},{128,160},{192,224},{256,288},{320,352},{384,416},{448,4..., dimensions={0}, use_global_device_ids=true | all-gather | bytes 98304 | tf_op jit(solution)/shard_map/all_gather | solution.py:46
  78.5 0.0 collective-permute-done.7.refs_4_
  78.5 2.9 %collective-permute-done.6.refs_3_ = bf16[64,256]{1,0:T(8,128)(2,1)S(1)} collective-permute-done((bf16[64,256]{1,0:T(8,128)(2,1)S(1)}, bf16[64,256]{1,0:T(8,128)(2,1)S(1)}, u32[]{:S(2)}, u32[]{:S(2)}) %collective-permute-start.6) | collective-permute-done | bytes 32800 | tf_op jit(solution)/shard_map/ppermute | solution.py:32
  81.4 0.9 shard_map.61
  82.3 6.2 %collective-permute-start.8 = (bf16[64,256]{1,0:T(8,128)(2,1)S(1)}, bf16[64,256]{1,0:T(8,128)(2,1)S(1)}, u32[]{:S(2)}, u32[]{:S(2)}) collective-permute-start(bf16[64,256]{1,0:T(8,128)(2,1)S(1)} %get-tuple-element.39), channel_id=1, source_target_pairs={{0,31},{1,2},{2,1},{3,4},{4,3},{5,6},{6,5},{7,8},{8,7},{9,10},{10,... | collective-permute-start | bytes 98312 | tf_op jit(solution)/shard_map/ppermute | solution.py:32
  88.5 7.4 %all-gather.5 = bf16[8,64,256]{2,1,0:T(8,128)(2,1)S(1)} all-gather(bf16[2,64,256]{2,1,0:T(8,128)(2,1)S(1)} %get-tuple-element.40), channel_id=7, replica_groups={{0,1,16,17},{2,3,18,19},{4,5,20,21},{6,7,22,23},{8,9,24,25},{10,11,26,2..., dimensions={0}, use_global_device_ids=true | all-gather | bytes 327680 | tf_op jit(solution)/shard_map/all_gather | solution.py:41
  95.8 0.0 collective-permute-done.8.cross
  95.8 0.2 shard_map.62
  96.0 3.9 %collective-permute-start.10 = (bf16[64,256]{1,0:T(8,128)(2,1)S(1)}, bf16[64,256]{1,0:T(8,128)(2,1)S(1)}, u32[]{:S(2)}, u32[]{:S(2)}) collective-permute-start(bf16[64,256]{1,0:T(8,128)(2,1)S(1)} %get-tuple-element.41), channel_id=1, source_target_pairs={{0,480},{32,64},{64,32},{96,128},{128,96},{160,192},{192,160},{224... | collective-permute-start | bytes 98312 | tf_op jit(solution)/shard_map/ppermute | solution.py:32
  99.9 6.5 %collective-permute-start.9 = (bf16[64,256]{1,0:T(8,128)(2,1)S(1)}, bf16[64,256]{1,0:T(8,128)(2,1)S(1)}, u32[]{:S(2)}, u32[]{:S(2)}) collective-permute-start(bf16[64,256]{1,0:T(8,128)(2,1)S(1)} %get-tuple-element.41), channel_id=1, source_target_pairs={{0,256},{32,288},{64,320},{96,352},{128,384},{160,416},{192,448},{... | collective-permute-start | bytes 98312 | tf_op jit(solution)/shard_map/ppermute | solution.py:32
  106.3 3.4 %all-gather.6 = bf16[128,256]{1,0:T(8,128)(2,1)S(1)} all-gather(bf16[64,256]{1,0:T(8,128)(2,1)S(1)} %get-tuple-element.41), channel_id=8, replica_groups={{0,32},{64,96},{128,160},{192,224},{256,288},{320,352},{384,416},{448,4..., dimensions={0}, use_global_device_ids=true | all-gather | bytes 98304 | tf_op jit(solution)/shard_map/all_gather | solution.py:46
  109.8 0.0 collective-permute-done.10.refs_4_
  109.8 3.7 %collective-permute-done.9.refs_3_ = bf16[64,256]{1,0:T(8,128)(2,1)S(1)} collective-permute-done((bf16[64,256]{1,0:T(8,128)(2,1)S(1)}, bf16[64,256]{1,0:T(8,128)(2,1)S(1)}, u32[]{:S(2)}, u32[]{:S(2)}) %collective-permute-start.9) | collective-permute-done | bytes 32800 | tf_op jit(solution)/shard_map/ppermute | solution.py:32
  113.5 0.6 shard_map.63
  114.1 3.3 %collective-permute-start.11 = (bf16[64,256]{1,0:T(8,128)(2,1)S(1)}, bf16[64,256]{1,0:T(8,128)(2,1)S(1)}, u32[]{:S(2)}, u32[]{:S(2)}) collective-permute-start(bf16[64,256]{1,0:T(8,128)(2,1)S(1)} %get-tuple-element.44), channel_id=1, source_target_pairs={{0,1},{1,0},{2,3},{3,2},{4,5},{5,4},{6,7},{7,6},{8,9},{9,8},{10,11... | collective-permute-start | bytes 98312 | tf_op jit(solution)/shard_map/ppermute | solution.py:32
  117.4 2.2 %collective-permute-start.12 = (bf16[64,256]{1,0:T(8,128)(2,1)S(1)}, bf16[64,256]{1,0:T(8,128)(2,1)S(1)}, u32[]{:S(2)}, u32[]{:S(2)}) collective-permute-start(bf16[64,256]{1,0:T(8,128)(2,1)S(1)} %get-tuple-element.45), channel_id=1, source_target_pairs={{0,16},{1,17},{2,18},{3,19},{4,20},{5,21},{6,22},{7,23},{8,24},{9,... | collective-permute-start | bytes 98312 | tf_op jit(solution)/shard_map/ppermute | solution.py:32
  119.7 1.9 %collective-permute-start.13 = (bf16[64,256]{1,0:T(8,128)(2,1)S(1)}, bf16[64,256]{1,0:T(8,128)(2,1)S(1)}, u32[]{:S(2)}, u32[]{:S(2)}) collective-permute-start(bf16[64,256]{1,0:T(8,128)(2,1)S(1)} %get-tuple-element.46), channel_id=1, source_target_pairs={{0,31},{1,2},{2,1},{3,4},{4,3},{5,6},{6,5},{7,8},{8,7},{9,10},{10,... | collective-permute-start | bytes 98312 | tf_op jit(solution)/shard_map/ppermute | solution.py:32
  121.6 0.0 collective-permute-done.11.pair
  121.6 2.0 %collective-permute-done.12.far = bf16[64,256]{1,0:T(8,128)(2,1)S(1)} collective-permute-done((bf16[64,256]{1,0:T(8,128)(2,1)S(1)}, bf16[64,256]{1,0:T(8,128)(2,1)S(1)}, u32[]{:S(2)}, u32[]{:S(2)}) %collective-permute-start.12) | collective-permute-done | bytes 32800 | tf_op jit(solution)/shard_map/ppermute | solution.py:32
  123.6 1.3 %collective-permute-done.13.cross = bf16[64,256]{1,0:T(8,128)(2,1)S(1)} collective-permute-done((bf16[64,256]{1,0:T(8,128)(2,1)S(1)}, bf16[64,256]{1,0:T(8,128)(2,1)S(1)}, u32[]{:S(2)}, u32[]{:S(2)}) %collective-permute-start.13) | collective-permute-done | bytes 32800 | tf_op jit(solution)/shard_map/ppermute | solution.py:32
  124.9 0.8 shard_map.64
  (1 shorter events, 0.0 us)
Async XLA Ops:
  1.1 15.9 %copy-start = (bf16[3,1,10,256,256]{4,3,2,1,0:T(8,128)(2,1)S(1)}, bf16[3,1,10,256,256]{4,3,2,1,0:T(8,128)(2,1)}, u32[]{:S(2)}) copy-start(bf16[3,1,10,256,256]{4,3,2,1,0:T(8,128)(2,1)} %refs_2_.9) | copy-start | bytes 11796484
  1.1 15.9 %copy-start.3 = (s32[3,1,10]{2,1,0:T(1,128)S(1)}, s32[3,1,10]{2,1,0:T(1,128)}, u32[]{:S(2)}) copy-start(s32[3,1,10]{2,1,0:T(1,128)} %refs_0_.9) | copy-start | bytes 364
  1.1 15.8 %copy-start.4 = (s32[3,1,10]{2,1,0:T(1,128)S(1)}, s32[3,1,10]{2,1,0:T(1,128)}, u32[]{:S(2)}) copy-start(s32[3,1,10]{2,1,0:T(1,128)} %refs_1_.9) | copy-start | bytes 364
  1.2 15.8 %collective-permute-start = (bf16[64,256]{1,0:T(8,128)(2,1)S(1)}, bf16[64,256]{1,0:T(8,128)(2,1)S(1)}, u32[]{:S(2)}, u32[]{:S(2)}) collective-permute-start(bf16[64,256]{1,0:T(8,128)(2,1)S(1)} %shard_map.55), channel_id=1, source_target_pairs={{0,31},{1,2},{2,1},{3,4},{4,3},{5,6},{6,5},{7,8},{8,7},{9,10},{10,... | collective-permute-start | bytes 98312 | tf_op jit(solution)/shard_map/ppermute | solution.py:32
  17.0 21.7 %copy-start.1 = (bf16[3,1,1,256,256]{4,3,2,1,0:T(8,128)(2,1)S(1)}, bf16[3,1,1,256,256]{4,3,2,1,0:T(8,128)(2,1)}, u32[]{:S(2)}) copy-start(bf16[3,1,1,256,256]{4,3,2,1,0:T(8,128)(2,1)} %inverse.7) | copy-start | bytes 1179652
  17.0 21.7 %copy-start.2 = (f32[3,1,1,64,256]{4,3,2,1,0:T(8,128)S(1)}, f32[3,1,1,64,256]{4,3,2,1,0:T(8,128)}, u32[]{:S(2)}) copy-start(f32[3,1,1,64,256]{4,3,2,1,0:T(8,128)} %rhs.3) | copy-start | bytes 589828
  17.6 21.0 %collective-permute-start.1 = (bf16[64,256]{1,0:T(8,128)(2,1)S(1)}, bf16[64,256]{1,0:T(8,128)(2,1)S(1)}, u32[]{:S(2)}, u32[]{:S(2)}) collective-permute-start(bf16[64,256]{1,0:T(8,128)(2,1)S(1)} %get-tuple-element.27), channel_id=1, source_target_pairs={{0,256},{32,288},{64,320},{96,352},{128,384},{160,416},{192,448},{... | collective-permute-start | bytes 98312 | tf_op jit(solution)/shard_map/ppermute | solution.py:32
  32.3 6.3 %collective-permute-start.2 = (bf16[64,256]{1,0:T(8,128)(2,1)S(1)}, bf16[64,256]{1,0:T(8,128)(2,1)S(1)}, u32[]{:S(2)}, u32[]{:S(2)}) collective-permute-start(bf16[64,256]{1,0:T(8,128)(2,1)S(1)} %get-tuple-element.28), channel_id=1, source_target_pairs={{0,480},{32,64},{64,32},{96,128},{128,96},{160,192},{192,160},{224... | collective-permute-start | bytes 98312 | tf_op jit(solution)/shard_map/ppermute | solution.py:32
  38.8 10.0 %collective-permute-start.3 = (bf16[64,256]{1,0:T(8,128)(2,1)S(1)}, bf16[64,256]{1,0:T(8,128)(2,1)S(1)}, u32[]{:S(2)}, u32[]{:S(2)}) collective-permute-start(bf16[64,256]{1,0:T(8,128)(2,1)S(1)} %get-tuple-element.32), channel_id=1, source_target_pairs={{0,31},{1,2},{2,1},{3,4},{4,3},{5,6},{6,5},{7,8},{8,7},{9,10},{10,... | collective-permute-start | bytes 98312 | tf_op jit(solution)/shard_map/ppermute | solution.py:32
  49.5 13.6 %collective-permute-start.4 = (bf16[64,256]{1,0:T(8,128)(2,1)S(1)}, bf16[64,256]{1,0:T(8,128)(2,1)S(1)}, u32[]{:S(2)}, u32[]{:S(2)}) collective-permute-start(bf16[64,256]{1,0:T(8,128)(2,1)S(1)} %get-tuple-element.33), channel_id=1, source_target_pairs={{0,256},{32,288},{64,320},{96,352},{128,384},{160,416},{192,448},{... | collective-permute-start | bytes 98312 | tf_op jit(solution)/shard_map/ppermute | solution.py:32
  57.4 7.8 %collective-permute-start.5 = (bf16[64,256]{1,0:T(8,128)(2,1)S(1)}, bf16[64,256]{1,0:T(8,128)(2,1)S(1)}, u32[]{:S(2)}, u32[]{:S(2)}) collective-permute-start(bf16[64,256]{1,0:T(8,128)(2,1)S(1)} %get-tuple-element.34), channel_id=1, source_target_pairs={{0,480},{32,64},{64,32},{96,128},{128,96},{160,192},{192,160},{224... | collective-permute-start | bytes 98312 | tf_op jit(solution)/shard_map/ppermute | solution.py:32
  65.5 13.0 %collective-permute-start.7 = (bf16[64,256]{1,0:T(8,128)(2,1)S(1)}, bf16[64,256]{1,0:T(8,128)(2,1)S(1)}, u32[]{:S(2)}, u32[]{:S(2)}) collective-permute-start(bf16[64,256]{1,0:T(8,128)(2,1)S(1)} %get-tuple-element.37), channel_id=1, source_target_pairs={{0,480},{32,64},{64,32},{96,128},{128,96},{160,192},{192,160},{224... | collective-permute-start | bytes 98312 | tf_op jit(solution)/shard_map/ppermute | solution.py:32
  68.0 13.4 %collective-permute-start.6 = (bf16[64,256]{1,0:T(8,128)(2,1)S(1)}, bf16[64,256]{1,0:T(8,128)(2,1)S(1)}, u32[]{:S(2)}, u32[]{:S(2)}) collective-permute-start(bf16[64,256]{1,0:T(8,128)(2,1)S(1)} %get-tuple-element.37), channel_id=1, source_target_pairs={{0,256},{32,288},{64,320},{96,352},{128,384},{160,416},{192,448},{... | collective-permute-start | bytes 98312 | tf_op jit(solution)/shard_map/ppermute | solution.py:32
  82.3 13.6 %collective-permute-start.8 = (bf16[64,256]{1,0:T(8,128)(2,1)S(1)}, bf16[64,256]{1,0:T(8,128)(2,1)S(1)}, u32[]{:S(2)}, u32[]{:S(2)}) collective-permute-start(bf16[64,256]{1,0:T(8,128)(2,1)S(1)} %get-tuple-element.39), channel_id=1, source_target_pairs={{0,31},{1,2},{2,1},{3,4},{4,3},{5,6},{6,5},{7,8},{8,7},{9,10},{10,... | collective-permute-start | bytes 98312 | tf_op jit(solution)/shard_map/ppermute | solution.py:32
  96.0 13.8 %collective-permute-start.10 = (bf16[64,256]{1,0:T(8,128)(2,1)S(1)}, bf16[64,256]{1,0:T(8,128)(2,1)S(1)}, u32[]{:S(2)}, u32[]{:S(2)}) collective-permute-start(bf16[64,256]{1,0:T(8,128)(2,1)S(1)} %get-tuple-element.41), channel_id=1, source_target_pairs={{0,480},{32,64},{64,32},{96,128},{128,96},{160,192},{192,160},{224... | collective-permute-start | bytes 98312 | tf_op jit(solution)/shard_map/ppermute | solution.py:32
  99.9 13.7 %collective-permute-start.9 = (bf16[64,256]{1,0:T(8,128)(2,1)S(1)}, bf16[64,256]{1,0:T(8,128)(2,1)S(1)}, u32[]{:S(2)}, u32[]{:S(2)}) collective-permute-start(bf16[64,256]{1,0:T(8,128)(2,1)S(1)} %get-tuple-element.41), channel_id=1, source_target_pairs={{0,256},{32,288},{64,320},{96,352},{128,384},{160,416},{192,448},{... | collective-permute-start | bytes 98312 | tf_op jit(solution)/shard_map/ppermute | solution.py:32
  114.1 7.5 %collective-permute-start.11 = (bf16[64,256]{1,0:T(8,128)(2,1)S(1)}, bf16[64,256]{1,0:T(8,128)(2,1)S(1)}, u32[]{:S(2)}, u32[]{:S(2)}) collective-permute-start(bf16[64,256]{1,0:T(8,128)(2,1)S(1)} %get-tuple-element.44), channel_id=1, source_target_pairs={{0,1},{1,0},{2,3},{3,2},{4,5},{5,4},{6,7},{7,6},{8,9},{9,8},{10,11... | collective-permute-start | bytes 98312 | tf_op jit(solution)/shard_map/ppermute | solution.py:32
  117.4 6.2 %collective-permute-start.12 = (bf16[64,256]{1,0:T(8,128)(2,1)S(1)}, bf16[64,256]{1,0:T(8,128)(2,1)S(1)}, u32[]{:S(2)}, u32[]{:S(2)}) collective-permute-start(bf16[64,256]{1,0:T(8,128)(2,1)S(1)} %get-tuple-element.45), channel_id=1, source_target_pairs={{0,16},{1,17},{2,18},{3,19},{4,20},{5,21},{6,22},{7,23},{8,24},{9,... | collective-permute-start | bytes 98312 | tf_op jit(solution)/shard_map/ppermute | solution.py:32
  119.7 5.2 %collective-permute-start.13 = (bf16[64,256]{1,0:T(8,128)(2,1)S(1)}, bf16[64,256]{1,0:T(8,128)(2,1)S(1)}, u32[]{:S(2)}, u32[]{:S(2)}) collective-permute-start(bf16[64,256]{1,0:T(8,128)(2,1)S(1)} %get-tuple-element.46), channel_id=1, source_target_pairs={{0,31},{1,2},{2,1},{3,4},{4,3},{5,6},{6,5},{7,8},{8,7},{9,10},{10,... | collective-permute-start | bytes 98312 | tf_op jit(solution)/shard_map/ppermute | solution.py:32

commit v6 on v5

--- a/solution.py
+++ b/solution.py
@@ -15,7 +15,7 @@
 F32 = jnp.float32
 
 
-def pair_of(i, n):
+def pair_of(i):
     return i + 1 - 2 * (i % 2)
 
 
@@ -44,10 +44,6 @@
 def gather_pair(value, axis):
     pairs = [[i, i + 1] for i in range(0, lax.axis_size(axis), 2)]
     return lax.all_gather(value, axis, axis_index_groups=pairs)
-
-
-def group_place(i, n):
-    return i % 2 + 2 * (i // (n // 2))
 
 
 def call(body, out_shape, in_specs, args, flops, moved, scratch=(), out_specs=None, vmem=16 * 2**20):
@@ -81,7 +77,7 @@
     t = targets[pair_idx]
     e = sources[pair_idx]
     me, n, key = (r, n_row, t) if kind == "fwd" else (c, n_col, e)
-    goals = [key == k for k in (me, pair_of(me, n), cross_of(me, n), far_of(me, n))]
+    goals = [key == k for k in (me, pair_of(me), cross_of(me, n), far_of(me, n))]
     if kind == "fwd":
         low = c % (n_col // 2) - c % 2
         group = [low, low + 1, low + n_col // 2, low + n_col // 2 + 1]
@@ -181,15 +177,10 @@
     return body
 
 
-def backward_body(n_col):
-    def body(y, inverse, own, cross, group, z_out, send_out):
-        c = lax.axis_index("col")
-        total = (
-            own[...].astype(F32)
-            + cross[...].astype(F32)
-            + group[group_place(pair_of(c, n_col), n_col), 0].astype(F32)
-            + group[group_place(far_of(c, n_col), n_col), 1].astype(F32)
-        )
+def backward_body():
+    def body(y, inverse, own, pair, far, cross, z_out, send_out):
+        other = pair[1 - lax.axis_index("col") % 2]
+        total = own[...].astype(F32) + other.astype(F32) + far[...].astype(F32) + cross[...].astype(F32)
         z = lax.dot_general((y[...] - total).astype(BF), inverse[1, 0, 0], NN, preferred_element_type=F32)
         z_out[...] = z
         send_out[...] = z.astype(BF)
@@ -201,7 +192,8 @@
     copies = [pltpu.make_async_copy(held, out.at[i, 0, 0], sems.at[i]) for i, held in enumerate((z0, z1, z2))]
     copies[1].start()
     copies[2].start()
-    total = own[...].astype(F32) + pair[...].astype(F32) + far[...].astype(F32) + cross[...].astype(F32)
+    other = pair[1 - lax.axis_index("col") % 2]
+    total = own[...].astype(F32) + other.astype(F32) + far[...].astype(F32) + cross[...].astype(F32)
     z0[...] = lax.dot_general((y[...] - total).astype(BF), inverse[0, 0, 0], NN, preferred_element_type=F32)
     copies[0].start()
     for copy in copies:
@@ -209,7 +201,6 @@
 
 
 def shards(rhs, inverse, blocks, targets, sources):
-    n_col = lax.axis_size("col")
     panel = jax.ShapeDtypeStruct(rhs.shape[3:], F32)
     solve_flops = 2 * panel.shape[0] * panel.shape[1] ** 2
 
@@ -231,15 +222,10 @@
 
     def last_scatter(parts):
         own, pair, cross, far = parts
-        pair = swap(pair, "col", pair_of)
+        cross = swap(cross, "col", cross_of)
         far = swap(far, "col", far_of)
-        cross = swap(cross, "col", cross_of)
+        pair = gather_pair(pair, "col")
         return [own, pair, far, cross]
-
-    def scatter_cols(parts):
-        own, cross, group = parts
-        cross = swap(cross, "col", cross_of)
-        return [own, cross, gather_far(group, "col")]
 
     tables = (targets, sources)
     y0 = lax.dot_general(rhs[0, 0, 0].astype(BF), inverse[0, 0, 0], NT, preferred_element_type=F32)
@@ -255,9 +241,10 @@
     z2, b2 = call(
         forward_body(2, True), [panel, bf_like(panel)], [VMEM] * 6, (rhs, inverse, *parts), 2 * solve_flops, 2**18
     )
-    *parts, base0 = products("bwd", 2, 1, tables, blocks, gather_rows(b2), apart=False)
-    parts = scatter_cols(parts)
-    z1, b1 = call(backward_body(n_col), [panel, bf_like(panel)], [VMEM] * 5, (y1, inverse, *parts), solve_flops, 2**18)
+    h2 = gather_rows(b2)
+    parts = last_scatter(products("bwd", 2, None, tables, blocks, h2))
+    base0 = products("bwd", None, 1, tables, blocks, h2)[0]
+    z1, b1 = call(backward_body(), [panel, bf_like(panel)], [VMEM] * 6, (y1, inverse, *parts), solve_flops, 2**18)
     parts = last_scatter(products("bwd", 0, None, tables, blocks, gather_rows(b1), base0))
     return call(
         last_body,

time: 127 us -> 125 us (0.984)
  waiting for transfers between devices: 12 us -> 7.55 us
  starting transfers between devices: 66.5 us -> 69 us
    all_gather x3 -> x2, blocking collectives: 26.4 us -> 19 us  [gather_far(): lax.all_gather(value, axis, axis_index_groups=far_groups(lax.axis_size(ax...]
    all_gather x4 -> x6, blocking collectives: 14.8 us -> 21.2 us  [gather_pair(): return lax.all_gather(value, axis, axis_index_groups=pairs)]
    ppermute x14, waiting for transfers between devices: 12 us -> 7.55 us  [swap(): return lax.ppermute(value, axis, [(i, partner(i, n)) for i in range(n)])]
    ppermute x14, starting transfers between devices: 66.5 us -> 69 us  [swap(): return lax.ppermute(value, axis, [(i, partner(i, n)) for i in range(n)])]
    pallas_call x10 -> x11, Pallas kernels: 4.67 us -> 4.91 us  [call(): pl.pallas_call(body, out_shape=out_shape, in_specs=in_specs, out_specs=ou...]
  transfers between devices with their start and end apart: 14 -> 14, of which waited for: 5 -> 3; matrix products, arithmetic and copies ran while one was open for 0% -> 0% of each run, Pallas kernels for 0% -> 1%
where the time goes in v6:
time: 125 us; the launch traced here: 123 us
  starting transfers between devices  69 us (55%)
  blocking collectives  40.2 us (32%)
  waiting for transfers between devices  7.55 us (6%)
  Pallas kernels  4.91 us (4%)
    ppermute x14, starting transfers between devices, swap(): return lax.ppermute(value, axis, [(i, partner(i, n)) for i in range(n)])  69 us
    all_gather x6, blocking collectives, gather_pair(): return lax.all_gather(value, axis, axis_index_groups=pairs)  21.2 us
    all_gather x2, blocking collectives, gather_far(): lax.all_gather(value, axis, axis_index_groups=far_groups(lax.axis_size(ax...  19 us
    ppermute x14, waiting for transfers between devices, swap(): return lax.ppermute(value, axis, [(i, partner(i, n)) for i in range(n)])  7.55 us
    pallas_call x11, Pallas kernels, call(): pl.pallas_call(body, out_shape=out_shape, in_specs=in_specs, out_specs=ou...  4.91 us
  transfers between devices with their start and end apart: 14, of which 3 were waited for; matrix products, arithmetic and copies ran while one was open for 0% of the time, Pallas kernels for 1%

profile of v6, /device:TPU:1, one launch (start us, length us, event | category | flops | bytes accessed | tf_op | source)
XLA Modules:
  0.0 123.1 jit_solution(15703934927248024656)
XLA Ops:
  0.0 1.1 fusion.value.y
  1.1 0.0 copy-start
  1.1 0.0 copy-start.3
  1.1 0.0 copy-start.4
  1.2 4.8 %collective-permute-start = (bf16[64,256]{1,0:T(8,128)(2,1)S(1)}, bf16[64,256]{1,0:T(8,128)(2,1)S(1)}, u32[]{:S(2)}, u32[]{:S(2)}) collective-permute-start(bf16[64,256]{1,0:T(8,128)(2,1)S(1)} %shard_map.55), channel_id=1, source_target_pairs={{0,31},{1,2},{2,1},{3,4},{4,3},{5,6},{6,5},{7,8},{8,7},{9,10},{10,... | collective-permute-start | bytes 98312 | tf_op jit(solution)/shard_map/ppermute | solution.py:32
  6.0 10.9 %all-gather = bf16[256,256]{1,0:T(8,128)(2,1)S(1)} all-gather(bf16[64,256]{1,0:T(8,128)(2,1)S(1)} %shard_map.55), channel_id=2, replica_groups={{0,1,16,17},{2,3,18,19},{4,5,20,21},{6,7,22,23},{8,9,24,25},{10,11,26,2..., dimensions={0}, use_global_device_ids=true | all-gather | bytes 163840 | tf_op jit(solution)/shard_map/all_gather | solution.py:41
  16.9 0.0 collective-permute-done.refs_3_
  17.0 0.0 copy-done
  17.0 0.0 copy-done.3
  17.0 0.0 copy-done.4
  17.0 0.0 copy-start.1
  17.0 0.0 copy-start.2
  17.0 0.6 shard_map.56
  17.6 14.7 %collective-permute-start.1 = (bf16[64,256]{1,0:T(8,128)(2,1)S(1)}, bf16[64,256]{1,0:T(8,128)(2,1)S(1)}, u32[]{:S(2)}, u32[]{:S(2)}) collective-permute-start(bf16[64,256]{1,0:T(8,128)(2,1)S(1)} %get-tuple-element.27), channel_id=1, source_target_pairs={{0,256},{32,288},{64,320},{96,352},{128,384},{160,416},{192,448},{... | collective-permute-start | bytes 98312 | tf_op jit(solution)/shard_map/ppermute | solution.py:32
  32.3 1.9 %collective-permute-start.2 = (bf16[64,256]{1,0:T(8,128)(2,1)S(1)}, bf16[64,256]{1,0:T(8,128)(2,1)S(1)}, u32[]{:S(2)}, u32[]{:S(2)}) collective-permute-start(bf16[64,256]{1,0:T(8,128)(2,1)S(1)} %get-tuple-element.28), channel_id=1, source_target_pairs={{0,480},{32,64},{64,32},{96,128},{128,96},{160,192},{192,160},{224... | collective-permute-start | bytes 98312 | tf_op jit(solution)/shard_map/ppermute | solution.py:32
  34.2 3.8 %all-gather.1 = bf16[128,256]{1,0:T(8,128)(2,1)S(1)} all-gather(bf16[64,256]{1,0:T(8,128)(2,1)S(1)} %get-tuple-element.29), channel_id=3, replica_groups={{0,32},{64,96},{128,160},{192,224},{256,288},{320,352},{384,416},{448,4..., dimensions={0}, use_global_device_ids=true | all-gather | bytes 98304 | tf_op jit(solution)/shard_map/all_gather | solution.py:46
  38.0 0.6 shard_map.58.refs_5_
  38.6 0.0 collective-permute-done.1.far
  38.6 0.0 collective-permute-done.2.cross
  38.6 0.0 copy-done.1
  38.6 0.0 copy-done.2
  38.7 0.2 shard_map.57
  38.8 1.9 %collective-permute-start.3 = (bf16[64,256]{1,0:T(8,128)(2,1)S(1)}, bf16[64,256]{1,0:T(8,128)(2,1)S(1)}, u32[]{:S(2)}, u32[]{:S(2)}) collective-permute-start(bf16[64,256]{1,0:T(8,128)(2,1)S(1)} %get-tuple-element.32), channel_id=1, source_target_pairs={{0,31},{1,2},{2,1},{3,4},{4,3},{5,6},{6,5},{7,8},{8,7},{9,10},{10,... | collective-permute-start | bytes 98312 | tf_op jit(solution)/shard_map/ppermute | solution.py:32
  40.8 8.1 %all-gather.2 = bf16[256,256]{1,0:T(8,128)(2,1)S(1)} all-gather(bf16[64,256]{1,0:T(8,128)(2,1)S(1)} %get-tuple-element.32), channel_id=4, replica_groups={{0,1,16,17},{2,3,18,19},{4,5,20,21},{6,7,22,23},{8,9,24,25},{10,11,26,2..., dimensions={0}, use_global_device_ids=true | all-gather | bytes 163840 | tf_op jit(solution)/shard_map/all_gather | solution.py:41
  48.9 0.0 collective-permute-done.3.refs_3_
  48.9 0.6 shard_map.59
  49.4 7.9 %collective-permute-start.4 = (bf16[64,256]{1,0:T(8,128)(2,1)S(1)}, bf16[64,256]{1,0:T(8,128)(2,1)S(1)}, u32[]{:S(2)}, u32[]{:S(2)}) collective-permute-start(bf16[64,256]{1,0:T(8,128)(2,1)S(1)} %get-tuple-element.33), channel_id=1, source_target_pairs={{0,256},{32,288},{64,320},{96,352},{128,384},{160,416},{192,448},{... | collective-permute-start | bytes 98312 | tf_op jit(solution)/shard_map/ppermute | solution.py:32
  57.4 1.9 %collective-permute-start.5 = (bf16[64,256]{1,0:T(8,128)(2,1)S(1)}, bf16[64,256]{1,0:T(8,128)(2,1)S(1)}, u32[]{:S(2)}, u32[]{:S(2)}) collective-permute-start(bf16[64,256]{1,0:T(8,128)(2,1)S(1)} %get-tuple-element.34), channel_id=1, source_target_pairs={{0,480},{32,64},{64,32},{96,128},{128,96},{160,192},{192,160},{224... | collective-permute-start | bytes 98312 | tf_op jit(solution)/shard_map/ppermute | solution.py:32
  59.3 3.7 %all-gather.3 = bf16[128,256]{1,0:T(8,128)(2,1)S(1)} all-gather(bf16[64,256]{1,0:T(8,128)(2,1)S(1)} %get-tuple-element.35), channel_id=5, replica_groups={{0,32},{64,96},{128,160},{192,224},{256,288},{320,352},{384,416},{448,4..., dimensions={0}, use_global_device_ids=true | all-gather | bytes 98304 | tf_op jit(solution)/shard_map/all_gather | solution.py:46
  63.0 0.0 collective-permute-done.4.far
  63.0 2.1 %collective-permute-done.5.cross = bf16[64,256]{1,0:T(8,128)(2,1)S(1)} collective-permute-done((bf16[64,256]{1,0:T(8,128)(2,1)S(1)}, bf16[64,256]{1,0:T(8,128)(2,1)S(1)}, u32[]{:S(2)}, u32[]{:S(2)}) %collective-permute-start.5) | collective-permute-done | bytes 32800 | tf_op jit(solution)/shard_map/ppermute | solution.py:32
  65.1 0.3 shard_map.60
  65.5 2.5 %collective-permute-start.7 = (bf16[64,256]{1,0:T(8,128)(2,1)S(1)}, bf16[64,256]{1,0:T(8,128)(2,1)S(1)}, u32[]{:S(2)}, u32[]{:S(2)}) collective-permute-start(bf16[64,256]{1,0:T(8,128)(2,1)S(1)} %get-tuple-element.37), channel_id=1, source_target_pairs={{0,480},{32,64},{64,32},{96,128},{128,96},{160,192},{192,160},{224... | collective-permute-start | bytes 98312 | tf_op jit(solution)/shard_map/ppermute | solution.py:32
  68.0 6.7 %collective-permute-start.6 = (bf16[64,256]{1,0:T(8,128)(2,1)S(1)}, bf16[64,256]{1,0:T(8,128)(2,1)S(1)}, u32[]{:S(2)}, u32[]{:S(2)}) collective-permute-start(bf16[64,256]{1,0:T(8,128)(2,1)S(1)} %get-tuple-element.37), channel_id=1, source_target_pairs={{0,256},{32,288},{64,320},{96,352},{128,384},{160,416},{192,448},{... | collective-permute-start | bytes 98312 | tf_op jit(solution)/shard_map/ppermute | solution.py:32
  74.7 3.8 %all-gather.4 = bf16[128,256]{1,0:T(8,128)(2,1)S(1)} all-gather(bf16[64,256]{1,0:T(8,128)(2,1)S(1)} %get-tuple-element.37), channel_id=6, replica_groups={{0,32},{64,96},{128,160},{192,224},{256,288},{320,352},{384,416},{448,4..., dimensions={0}, use_global_device_ids=true | all-gather | bytes 98304 | tf_op jit(solution)/shard_map/all_gather | solution.py:46
  78.5 0.0 collective-permute-done.7.refs_4_
  78.5 2.9 %collective-permute-done.6.refs_3_ = bf16[64,256]{1,0:T(8,128)(2,1)S(1)} collective-permute-done((bf16[64,256]{1,0:T(8,128)(2,1)S(1)}, bf16[64,256]{1,0:T(8,128)(2,1)S(1)}, u32[]{:S(2)}, u32[]{:S(2)}) %collective-permute-start.6) | collective-permute-done | bytes 32800 | tf_op jit(solution)/shard_map/ppermute | solution.py:32
  81.4 0.6 shard_map.61
  81.9 2.9 %collective-permute-start.8 = (bf16[64,256]{1,0:T(8,128)(2,1)S(1)}, bf16[64,256]{1,0:T(8,128)(2,1)S(1)}, u32[]{:S(2)}, u32[]{:S(2)}) collective-permute-start(bf16[64,256]{1,0:T(8,128)(2,1)S(1)} %get-tuple-element.40), channel_id=1, source_target_pairs={{0,16},{1,17},{2,18},{3,19},{4,20},{5,21},{6,22},{7,23},{8,24},{9,... | collective-permute-start | bytes 98312 | tf_op jit(solution)/shard_map/ppermute | solution.py:32
  84.8 6.0 %collective-permute-start.9 = (bf16[64,256]{1,0:T(8,128)(2,1)S(1)}, bf16[64,256]{1,0:T(8,128)(2,1)S(1)}, u32[]{:S(2)}, u32[]{:S(2)}) collective-permute-start(bf16[64,256]{1,0:T(8,128)(2,1)S(1)} %get-tuple-element.41), channel_id=1, source_target_pairs={{0,31},{1,2},{2,1},{3,4},{4,3},{5,6},{6,5},{7,8},{8,7},{9,10},{10,... | collective-permute-start | bytes 98312 | tf_op jit(solution)/shard_map/ppermute | solution.py:32
  90.9 2.1 %all-gather.5 = bf16[128,256]{1,0:T(8,128)(2,1)S(1)} all-gather(bf16[64,256]{1,0:T(8,128)(2,1)S(1)} %get-tuple-element.39), channel_id=7, replica_groups={{0,1},{2,3},{4,5},{6,7},{8,9},{10,11},{12,13},{14,15},{16,17},{18,19},{..., dimensions={0}, use_global_device_ids=true | all-gather | bytes 98304 | tf_op jit(solution)/shard_map/all_gather | solution.py:46
  93.0 0.0 collective-permute-done.8.far
  93.0 0.0 collective-permute-done.9.cross
  93.0 0.1 shard_map.62
  93.2 3.3 %collective-permute-start.11 = (bf16[64,256]{1,0:T(8,128)(2,1)S(1)}, bf16[64,256]{1,0:T(8,128)(2,1)S(1)}, u32[]{:S(2)}, u32[]{:S(2)}) collective-permute-start(bf16[64,256]{1,0:T(8,128)(2,1)S(1)} %get-tuple-element.42), channel_id=1, source_target_pairs={{0,480},{32,64},{64,32},{96,128},{128,96},{160,192},{192,160},{224... | collective-permute-start | bytes 98312 | tf_op jit(solution)/shard_map/ppermute | solution.py:32
  96.5 6.8 %collective-permute-start.10 = (bf16[64,256]{1,0:T(8,128)(2,1)S(1)}, bf16[64,256]{1,0:T(8,128)(2,1)S(1)}, u32[]{:S(2)}, u32[]{:S(2)}) collective-permute-start(bf16[64,256]{1,0:T(8,128)(2,1)S(1)} %get-tuple-element.42), channel_id=1, source_target_pairs={{0,256},{32,288},{64,320},{96,352},{128,384},{160,416},{192,448},{... | collective-permute-start | bytes 98312 | tf_op jit(solution)/shard_map/ppermute | solution.py:32
  103.3 0.6 shard_map.63.refs_6_
  103.9 3.4 %all-gather.6 = bf16[128,256]{1,0:T(8,128)(2,1)S(1)} all-gather(bf16[64,256]{1,0:T(8,128)(2,1)S(1)} %get-tuple-element.42), channel_id=8, replica_groups={{0,32},{64,96},{128,160},{192,224},{256,288},{320,352},{384,416},{448,4..., dimensions={0}, use_global_device_ids=true | all-gather | bytes 98304 | tf_op jit(solution)/shard_map/all_gather | solution.py:46
  107.3 0.0 collective-permute-done.11.refs_4_
  107.3 2.6 %collective-permute-done.10.refs_3_ = bf16[64,256]{1,0:T(8,128)(2,1)S(1)} collective-permute-done((bf16[64,256]{1,0:T(8,128)(2,1)S(1)}, bf16[64,256]{1,0:T(8,128)(2,1)S(1)}, u32[]{:S(2)}, u32[]{:S(2)}) %collective-permute-start.10) | collective-permute-done | bytes 32800 | tf_op jit(solution)/shard_map/ppermute | solution.py:32
  109.9 0.6 shard_map.64
  110.5 3.9 %collective-permute-start.12 = (bf16[64,256]{1,0:T(8,128)(2,1)S(1)}, bf16[64,256]{1,0:T(8,128)(2,1)S(1)}, u32[]{:S(2)}, u32[]{:S(2)}) collective-permute-start(bf16[64,256]{1,0:T(8,128)(2,1)S(1)} %get-tuple-element.45), channel_id=1, source_target_pairs={{0,16},{1,17},{2,18},{3,19},{4,20},{5,21},{6,22},{7,23},{8,24},{9,... | collective-permute-start | bytes 98312 | tf_op jit(solution)/shard_map/ppermute | solution.py:32
  114.4 3.5 %collective-permute-start.13 = (bf16[64,256]{1,0:T(8,128)(2,1)S(1)}, bf16[64,256]{1,0:T(8,128)(2,1)S(1)}, u32[]{:S(2)}, u32[]{:S(2)}) collective-permute-start(bf16[64,256]{1,0:T(8,128)(2,1)S(1)} %get-tuple-element.46), channel_id=1, source_target_pairs={{0,31},{1,2},{2,1},{3,4},{4,3},{5,6},{6,5},{7,8},{8,7},{9,10},{10,... | collective-permute-start | bytes 98312 | tf_op jit(solution)/shard_map/ppermute | solution.py:32
  117.9 4.3 %all-gather.7 = bf16[128,256]{1,0:T(8,128)(2,1)S(1)} all-gather(bf16[64,256]{1,0:T(8,128)(2,1)S(1)} %get-tuple-element.44), channel_id=9, replica_groups={{0,1},{2,3},{4,5},{6,7},{8,9},{10,11},{12,13},{14,15},{16,17},{18,19},{..., dimensions={0}, use_global_device_ids=true | all-gather | bytes 98304 | tf_op jit(solution)/shard_map/all_gather | solution.py:46
  122.2 0.0 collective-permute-done.12.far
  122.2 0.0 collective-permute-done.13.cross
  122.3 0.8 shard_map.65
  (1 shorter events, 0.0 us)
Async XLA Ops:
  1.1 15.9 %copy-start = (bf16[3,1,10,256,256]{4,3,2,1,0:T(8,128)(2,1)S(1)}, bf16[3,1,10,256,256]{4,3,2,1,0:T(8,128)(2,1)}, u32[]{:S(2)}) copy-start(bf16[3,1,10,256,256]{4,3,2,1,0:T(8,128)(2,1)} %refs_2_.11) | copy-start | bytes 11796484
  1.1 15.9 %copy-start.3 = (s32[3,1,10]{2,1,0:T(1,128)S(1)}, s32[3,1,10]{2,1,0:T(1,128)}, u32[]{:S(2)}) copy-start(s32[3,1,10]{2,1,0:T(1,128)} %refs_0_.11) | copy-start | bytes 364
  1.1 15.8 %copy-start.4 = (s32[3,1,10]{2,1,0:T(1,128)S(1)}, s32[3,1,10]{2,1,0:T(1,128)}, u32[]{:S(2)}) copy-start(s32[3,1,10]{2,1,0:T(1,128)} %refs_1_.11) | copy-start | bytes 364
  1.2 15.8 %collective-permute-start = (bf16[64,256]{1,0:T(8,128)(2,1)S(1)}, bf16[64,256]{1,0:T(8,128)(2,1)S(1)}, u32[]{:S(2)}, u32[]{:S(2)}) collective-permute-start(bf16[64,256]{1,0:T(8,128)(2,1)S(1)} %shard_map.55), channel_id=1, source_target_pairs={{0,31},{1,2},{2,1},{3,4},{4,3},{5,6},{6,5},{7,8},{8,7},{9,10},{10,... | collective-permute-start | bytes 98312 | tf_op jit(solution)/shard_map/ppermute | solution.py:32
  17.0 21.7 %copy-start.1 = (bf16[3,1,1,256,256]{4,3,2,1,0:T(8,128)(2,1)S(1)}, bf16[3,1,1,256,256]{4,3,2,1,0:T(8,128)(2,1)}, u32[]{:S(2)}) copy-start(bf16[3,1,1,256,256]{4,3,2,1,0:T(8,128)(2,1)} %inverse.7) | copy-start | bytes 1179652
  17.0 21.7 %copy-start.2 = (f32[3,1,1,64,256]{4,3,2,1,0:T(8,128)S(1)}, f32[3,1,1,64,256]{4,3,2,1,0:T(8,128)}, u32[]{:S(2)}) copy-start(f32[3,1,1,64,256]{4,3,2,1,0:T(8,128)} %rhs.3) | copy-start | bytes 589828
  17.6 21.0 %collective-permute-start.1 = (bf16[64,256]{1,0:T(8,128)(2,1)S(1)}, bf16[64,256]{1,0:T(8,128)(2,1)S(1)}, u32[]{:S(2)}, u32[]{:S(2)}) collective-permute-start(bf16[64,256]{1,0:T(8,128)(2,1)S(1)} %get-tuple-element.27), channel_id=1, source_target_pairs={{0,256},{32,288},{64,320},{96,352},{128,384},{160,416},{192,448},{... | collective-permute-start | bytes 98312 | tf_op jit(solution)/shard_map/ppermute | solution.py:32
  32.3 6.3 %collective-permute-start.2 = (bf16[64,256]{1,0:T(8,128)(2,1)S(1)}, bf16[64,256]{1,0:T(8,128)(2,1)S(1)}, u32[]{:S(2)}, u32[]{:S(2)}) collective-permute-start(bf16[64,256]{1,0:T(8,128)(2,1)S(1)} %get-tuple-element.28), channel_id=1, source_target_pairs={{0,480},{32,64},{64,32},{96,128},{128,96},{160,192},{192,160},{224... | collective-permute-start | bytes 98312 | tf_op jit(solution)/shard_map/ppermute | solution.py:32
  38.8 10.0 %collective-permute-start.3 = (bf16[64,256]{1,0:T(8,128)(2,1)S(1)}, bf16[64,256]{1,0:T(8,128)(2,1)S(1)}, u32[]{:S(2)}, u32[]{:S(2)}) collective-permute-start(bf16[64,256]{1,0:T(8,128)(2,1)S(1)} %get-tuple-element.32), channel_id=1, source_target_pairs={{0,31},{1,2},{2,1},{3,4},{4,3},{5,6},{6,5},{7,8},{8,7},{9,10},{10,... | collective-permute-start | bytes 98312 | tf_op jit(solution)/shard_map/ppermute | solution.py:32
  49.4 13.6 %collective-permute-start.4 = (bf16[64,256]{1,0:T(8,128)(2,1)S(1)}, bf16[64,256]{1,0:T(8,128)(2,1)S(1)}, u32[]{:S(2)}, u32[]{:S(2)}) collective-permute-start(bf16[64,256]{1,0:T(8,128)(2,1)S(1)} %get-tuple-element.33), channel_id=1, source_target_pairs={{0,256},{32,288},{64,320},{96,352},{128,384},{160,416},{192,448},{... | collective-permute-start | bytes 98312 | tf_op jit(solution)/shard_map/ppermute | solution.py:32
  57.4 7.8 %collective-permute-start.5 = (bf16[64,256]{1,0:T(8,128)(2,1)S(1)}, bf16[64,256]{1,0:T(8,128)(2,1)S(1)}, u32[]{:S(2)}, u32[]{:S(2)}) collective-permute-start(bf16[64,256]{1,0:T(8,128)(2,1)S(1)} %get-tuple-element.34), channel_id=1, source_target_pairs={{0,480},{32,64},{64,32},{96,128},{128,96},{160,192},{192,160},{224... | collective-permute-start | bytes 98312 | tf_op jit(solution)/shard_map/ppermute | solution.py:32
  65.5 13.0 %collective-permute-start.7 = (bf16[64,256]{1,0:T(8,128)(2,1)S(1)}, bf16[64,256]{1,0:T(8,128)(2,1)S(1)}, u32[]{:S(2)}, u32[]{:S(2)}) collective-permute-start(bf16[64,256]{1,0:T(8,128)(2,1)S(1)} %get-tuple-element.37), channel_id=1, source_target_pairs={{0,480},{32,64},{64,32},{96,128},{128,96},{160,192},{192,160},{224... | collective-permute-start | bytes 98312 | tf_op jit(solution)/shard_map/ppermute | solution.py:32
  68.0 13.4 %collective-permute-start.6 = (bf16[64,256]{1,0:T(8,128)(2,1)S(1)}, bf16[64,256]{1,0:T(8,128)(2,1)S(1)}, u32[]{:S(2)}, u32[]{:S(2)}) collective-permute-start(bf16[64,256]{1,0:T(8,128)(2,1)S(1)} %get-tuple-element.37), channel_id=1, source_target_pairs={{0,256},{32,288},{64,320},{96,352},{128,384},{160,416},{192,448},{... | collective-permute-start | bytes 98312 | tf_op jit(solution)/shard_map/ppermute | solution.py:32
  81.9 11.1 %collective-permute-start.8 = (bf16[64,256]{1,0:T(8,128)(2,1)S(1)}, bf16[64,256]{1,0:T(8,128)(2,1)S(1)}, u32[]{:S(2)}, u32[]{:S(2)}) collective-permute-start(bf16[64,256]{1,0:T(8,128)(2,1)S(1)} %get-tuple-element.40), channel_id=1, source_target_pairs={{0,16},{1,17},{2,18},{3,19},{4,20},{5,21},{6,22},{7,23},{8,24},{9,... | collective-permute-start | bytes 98312 | tf_op jit(solution)/shard_map/ppermute | solution.py:32
  84.8 8.2 %collective-permute-start.9 = (bf16[64,256]{1,0:T(8,128)(2,1)S(1)}, bf16[64,256]{1,0:T(8,128)(2,1)S(1)}, u32[]{:S(2)}, u32[]{:S(2)}) collective-permute-start(bf16[64,256]{1,0:T(8,128)(2,1)S(1)} %get-tuple-element.41), channel_id=1, source_target_pairs={{0,31},{1,2},{2,1},{3,4},{4,3},{5,6},{6,5},{7,8},{8,7},{9,10},{10,... | collective-permute-start | bytes 98312 | tf_op jit(solution)/shard_map/ppermute | solution.py:32
  93.2 14.2 %collective-permute-start.11 = (bf16[64,256]{1,0:T(8,128)(2,1)S(1)}, bf16[64,256]{1,0:T(8,128)(2,1)S(1)}, u32[]{:S(2)}, u32[]{:S(2)}) collective-permute-start(bf16[64,256]{1,0:T(8,128)(2,1)S(1)} %get-tuple-element.42), channel_id=1, source_target_pairs={{0,480},{32,64},{64,32},{96,128},{128,96},{160,192},{192,160},{224... | collective-permute-start | bytes 98312 | tf_op jit(solution)/shard_map/ppermute | solution.py:32
  96.5 13.4 %collective-permute-start.10 = (bf16[64,256]{1,0:T(8,128)(2,1)S(1)}, bf16[64,256]{1,0:T(8,128)(2,1)S(1)}, u32[]{:S(2)}, u32[]{:S(2)}) collective-permute-start(bf16[64,256]{1,0:T(8,128)(2,1)S(1)} %get-tuple-element.42), channel_id=1, source_target_pairs={{0,256},{32,288},{64,320},{96,352},{128,384},{160,416},{192,448},{... | collective-permute-start | bytes 98312 | tf_op jit(solution)/shard_map/ppermute | solution.py:32
  110.5 11.8 %collective-permute-start.12 = (bf16[64,256]{1,0:T(8,128)(2,1)S(1)}, bf16[64,256]{1,0:T(8,128)(2,1)S(1)}, u32[]{:S(2)}, u32[]{:S(2)}) collective-permute-start(bf16[64,256]{1,0:T(8,128)(2,1)S(1)} %get-tuple-element.45), channel_id=1, source_target_pairs={{0,16},{1,17},{2,18},{3,19},{4,20},{5,21},{6,22},{7,23},{8,24},{9,... | collective-permute-start | bytes 98312 | tf_op jit(solution)/shard_map/ppermute | solution.py:32
  114.4 7.9 %collective-permute-start.13 = (bf16[64,256]{1,0:T(8,128)(2,1)S(1)}, bf16[64,256]{1,0:T(8,128)(2,1)S(1)}, u32[]{:S(2)}, u32[]{:S(2)}) collective-permute-start(bf16[64,256]{1,0:T(8,128)(2,1)S(1)} %get-tuple-element.46), channel_id=1, source_target_pairs={{0,31},{1,2},{2,1},{3,4},{4,3},{5,6},{6,5},{7,8},{8,7},{9,10},{10,... | collective-permute-start | bytes 98312 | tf_op jit(solution)/shard_map/ppermute | solution.py:32

commit v7 on v6

--- a/solution.py
+++ b/solution.py
@@ -30,15 +30,6 @@
 def swap(value, axis, partner):
     n = lax.axis_size(axis)
     return lax.ppermute(value, axis, [(i, partner(i, n)) for i in range(n)])
-
-
-def far_groups(n):
-    half = n // 2
-    return [[i, i + 1, i + half, i + half + 1] for i in range(0, half, 2)]
-
-
-def gather_far(value, axis):
-    return lax.all_gather(value, axis, axis_index_groups=far_groups(lax.axis_size(axis)))
 
 
 def gather_pair(value, axis):
@@ -79,9 +70,7 @@
     me, n, key = (r, n_row, t) if kind == "fwd" else (c, n_col, e)
     goals = [key == k for k in (me, pair_of(me), cross_of(me, n), far_of(me, n))]
     if kind == "fwd":
-        low = c % (n_col // 2) - c % 2
-        group = [low, low + 1, low + n_col // 2, low + n_col // 2 + 1]
-        picks = [e == k for k in (cross_of(c, n_col), *group)]
+        picks = [e == k for k in (cross_of(c, n_col), far_of(c, n_col), c - c % 2, c - c % 2 + 1)]
     else:
         picks = [t == k for k in (far_of(r, n_row), cross_of(r, n_row), r - r % 2, r - r % 2 + 1)]
     goals = [g.astype(F32) for g in goals]
@@ -104,7 +93,7 @@
 def product_body(kind, pair_idx, n_row, n_col, slots, add, extra, apart):
     def body(*refs):
         targets, sources, blocks, *rest = refs
-        count = 2 if kind == "fwd" else 3
+        count = 3
         panels, rest = rest[:count], rest[count:]
         if add:
             base, rest = rest[0], rest[1:]
@@ -206,7 +195,8 @@
 
     def gather_cols(value):
         cross = swap(value, "col", cross_of)
-        return [cross, gather_far(value, "col")]
+        far = swap(value, "col", far_of)
+        return [cross, far, gather_pair(value, "col")]
 
     def swap_rows(far, cross, pair):
         far = swap(far, "row", far_of)

time: 125 us -> 126 us (level)
  the two profiles are of different devices: /device:TPU:1 before, /device:TPU:4 now
where the time goes in v7:
time: 126 us
  starting transfers between devices  74.9 us (59%)
  blocking collectives  26.1 us (21%)
  waiting for transfers between devices  18.5 us (15%)
  Pallas kernels  4.9 us (4%)
    ppermute x16, starting transfers between devices, swap(): return lax.ppermute(value, axis, [(i, partner(i, n)) for i in range(n)])  74.9 us
    all_gather x8, blocking collectives, gather_pair(): return lax.all_gather(value, axis, axis_index_groups=pairs)  26.1 us
    ppermute x16, waiting for transfers between devices, swap(): return lax.ppermute(value, axis, [(i, partner(i, n)) for i in range(n)])  18.5 us
    pallas_call x11, Pallas kernels, call(): pl.pallas_call(body, out_shape=out_shape, in_specs=in_specs, out_specs=ou...  4.9 us
  transfers between devices with their start and end apart: 16, of which 8 were waited for; matrix products, arithmetic and copies ran while one was open for 0% of the time, Pallas kernels for 1%

profile of v7, /device:TPU:4, one launch (start us, length us, event | category | flops | bytes accessed | tf_op | source)
XLA Modules:
  0.0 125.8 jit_solution(4077569850445623090)
XLA Ops:
  0.0 1.1 fusion.value.y
  1.1 0.0 copy-start
  1.1 0.0 copy-start.3
  1.1 0.0 copy-start.4
  1.2 0.0 copy-start.1
  1.2 0.0 copy-start.2
  1.2 8.0 %collective-permute-start.1 = (bf16[64,256]{1,0:T(8,128)(2,1)S(1)}, bf16[64,256]{1,0:T(8,128)(2,1)S(1)}, u32[]{:S(2)}, u32[]{:S(2)}) collective-permute-start(bf16[64,256]{1,0:T(8,128)(2,1)S(1)} %shard_map.55), channel_id=1, source_target_pairs={{0,16},{1,17},{2,18},{3,19},{4,20},{5,21},{6,22},{7,23},{8,24},{9,... | collective-permute-start | bytes 98312 | tf_op jit(solution)/shard_map/ppermute | solution.py:32
  9.2 1.9 %collective-permute-start = (bf16[64,256]{1,0:T(8,128)(2,1)S(1)}, bf16[64,256]{1,0:T(8,128)(2,1)S(1)}, u32[]{:S(2)}, u32[]{:S(2)}) collective-permute-start(bf16[64,256]{1,0:T(8,128)(2,1)S(1)} %shard_map.55), channel_id=1, source_target_pairs={{0,31},{1,2},{2,1},{3,4},{4,3},{5,6},{6,5},{7,8},{8,7},{9,10},{10,... | collective-permute-start | bytes 98312 | tf_op jit(solution)/shard_map/ppermute | solution.py:32
  11.1 1.9 %all-gather = bf16[128,256]{1,0:T(8,128)(2,1)S(1)} all-gather(bf16[64,256]{1,0:T(8,128)(2,1)S(1)} %shard_map.55), channel_id=2, replica_groups={{0,1},{2,3},{4,5},{6,7},{8,9},{10,11},{12,13},{14,15},{16,17},{18,19},{..., dimensions={0}, use_global_device_ids=true | all-gather | bytes 98304 | tf_op jit(solution)/shard_map/all_gather | solution.py:37
  13.0 0.0 collective-permute-done.1.refs_4_
  13.0 3.6 %collective-permute-done.refs_3_ = bf16[64,256]{1,0:T(8,128)(2,1)S(1)} collective-permute-done((bf16[64,256]{1,0:T(8,128)(2,1)S(1)}, bf16[64,256]{1,0:T(8,128)(2,1)S(1)}, u32[]{:S(2)}, u32[]{:S(2)}) %collective-permute-start) | collective-permute-done | bytes 32800 | tf_op jit(solution)/shard_map/ppermute | solution.py:32
  16.6 0.0 copy-done
  16.6 0.0 copy-done.3
  16.6 0.0 copy-done.4
  16.6 0.6 shard_map.56
  17.2 10.7 %collective-permute-start.2 = (bf16[64,256]{1,0:T(8,128)(2,1)S(1)}, bf16[64,256]{1,0:T(8,128)(2,1)S(1)}, u32[]{:S(2)}, u32[]{:S(2)}) collective-permute-start(bf16[64,256]{1,0:T(8,128)(2,1)S(1)} %get-tuple-element.27), channel_id=1, source_target_pairs={{0,256},{32,288},{64,320},{96,352},{128,384},{160,416},{192,448},{... | collective-permute-start | bytes 98312 | tf_op jit(solution)/shard_map/ppermute | solution.py:32
  27.9 2.0 %collective-permute-start.3 = (bf16[64,256]{1,0:T(8,128)(2,1)S(1)}, bf16[64,256]{1,0:T(8,128)(2,1)S(1)}, u32[]{:S(2)}, u32[]{:S(2)}) collective-permute-start(bf16[64,256]{1,0:T(8,128)(2,1)S(1)} %get-tuple-element.28), channel_id=1, source_target_pairs={{0,480},{32,64},{64,32},{96,128},{128,96},{160,192},{192,160},{224... | collective-permute-start | bytes 98312 | tf_op jit(solution)/shard_map/ppermute | solution.py:32
  29.9 4.6 %all-gather.1 = bf16[128,256]{1,0:T(8,128)(2,1)S(1)} all-gather(bf16[64,256]{1,0:T(8,128)(2,1)S(1)} %get-tuple-element.29), channel_id=3, replica_groups={{0,32},{64,96},{128,160},{192,224},{256,288},{320,352},{384,416},{448,4..., dimensions={0}, use_global_device_ids=true | all-gather | bytes 98304 | tf_op jit(solution)/shard_map/all_gather | solution.py:37
  34.5 0.0 collective-permute-done.2.far
  34.5 0.4 collective-permute-done.3.cross
  34.9 0.0 copy-done.1
  34.9 0.0 copy-done.2
  34.9 0.2 shard_map.57
  35.1 5.8 %collective-permute-start.5 = (bf16[64,256]{1,0:T(8,128)(2,1)S(1)}, bf16[64,256]{1,0:T(8,128)(2,1)S(1)}, u32[]{:S(2)}, u32[]{:S(2)}) collective-permute-start(bf16[64,256]{1,0:T(8,128)(2,1)S(1)} %get-tuple-element.32), channel_id=1, source_target_pairs={{0,16},{1,17},{2,18},{3,19},{4,20},{5,21},{6,22},{7,23},{8,24},{9,... | collective-permute-start | bytes 98312 | tf_op jit(solution)/shard_map/ppermute | solution.py:32
  40.9 2.3 %collective-permute-start.4 = (bf16[64,256]{1,0:T(8,128)(2,1)S(1)}, bf16[64,256]{1,0:T(8,128)(2,1)S(1)}, u32[]{:S(2)}, u32[]{:S(2)}) collective-permute-start(bf16[64,256]{1,0:T(8,128)(2,1)S(1)} %get-tuple-element.32), channel_id=1, source_target_pairs={{0,31},{1,2},{2,1},{3,4},{4,3},{5,6},{6,5},{7,8},{8,7},{9,10},{10,... | collective-permute-start | bytes 98312 | tf_op jit(solution)/shard_map/ppermute | solution.py:32
  43.2 0.6 shard_map.58.refs_6_
  43.8 1.9 %all-gather.2 = bf16[128,256]{1,0:T(8,128)(2,1)S(1)} all-gather(bf16[64,256]{1,0:T(8,128)(2,1)S(1)} %get-tuple-element.32), channel_id=4, replica_groups={{0,1},{2,3},{4,5},{6,7},{8,9},{10,11},{12,13},{14,15},{16,17},{18,19},{..., dimensions={0}, use_global_device_ids=true | all-gather | bytes 98304 | tf_op jit(solution)/shard_map/all_gather | solution.py:37
  45.7 0.0 collective-permute-done.5.refs_4_
  45.7 2.6 %collective-permute-done.4.refs_3_ = bf16[64,256]{1,0:T(8,128)(2,1)S(1)} collective-permute-done((bf16[64,256]{1,0:T(8,128)(2,1)S(1)}, bf16[64,256]{1,0:T(8,128)(2,1)S(1)}, u32[]{:S(2)}, u32[]{:S(2)}) %collective-permute-start.4) | collective-permute-done | bytes 32800 | tf_op jit(solution)/shard_map/ppermute | solution.py:32
  48.2 0.6 shard_map.59
  48.8 7.8 %collective-permute-start.6 = (bf16[64,256]{1,0:T(8,128)(2,1)S(1)}, bf16[64,256]{1,0:T(8,128)(2,1)S(1)}, u32[]{:S(2)}, u32[]{:S(2)}) collective-permute-start(bf16[64,256]{1,0:T(8,128)(2,1)S(1)} %get-tuple-element.33), channel_id=1, source_target_pairs={{0,256},{32,288},{64,320},{96,352},{128,384},{160,416},{192,448},{... | collective-permute-start | bytes 98312 | tf_op jit(solution)/shard_map/ppermute | solution.py:32
  56.7 2.4 %collective-permute-start.7 = (bf16[64,256]{1,0:T(8,128)(2,1)S(1)}, bf16[64,256]{1,0:T(8,128)(2,1)S(1)}, u32[]{:S(2)}, u32[]{:S(2)}) collective-permute-start(bf16[64,256]{1,0:T(8,128)(2,1)S(1)} %get-tuple-element.34), channel_id=1, source_target_pairs={{0,480},{32,64},{64,32},{96,128},{128,96},{160,192},{192,160},{224... | collective-permute-start | bytes 98312 | tf_op jit(solution)/shard_map/ppermute | solution.py:32
  59.1 4.8 %all-gather.3 = bf16[128,256]{1,0:T(8,128)(2,1)S(1)} all-gather(bf16[64,256]{1,0:T(8,128)(2,1)S(1)} %get-tuple-element.35), channel_id=5, replica_groups={{0,32},{64,96},{128,160},{192,224},{256,288},{320,352},{384,416},{448,4..., dimensions={0}, use_global_device_ids=true | all-gather | bytes 98304 | tf_op jit(solution)/shard_map/all_gather | solution.py:37
  63.9 0.0 collective-permute-done.6.far
  63.9 0.0 collective-permute-done.7.cross
  63.9 0.3 shard_map.60
  64.2 4.4 %collective-permute-start.9 = (bf16[64,256]{1,0:T(8,128)(2,1)S(1)}, bf16[64,256]{1,0:T(8,128)(2,1)S(1)}, u32[]{:S(2)}, u32[]{:S(2)}) collective-permute-start(bf16[64,256]{1,0:T(8,128)(2,1)S(1)} %get-tuple-element.37), channel_id=1, source_target_pairs={{0,480},{32,64},{64,32},{96,128},{128,96},{160,192},{192,160},{224... | collective-permute-start | bytes 98312 | tf_op jit(solution)/shard_map/ppermute | solution.py:32
  68.6 6.7 %collective-permute-start.8 = (bf16[64,256]{1,0:T(8,128)(2,1)S(1)}, bf16[64,256]{1,0:T(8,128)(2,1)S(1)}, u32[]{:S(2)}, u32[]{:S(2)}) collective-permute-start(bf16[64,256]{1,0:T(8,128)(2,1)S(1)} %get-tuple-element.37), channel_id=1, source_target_pairs={{0,256},{32,288},{64,320},{96,352},{128,384},{160,416},{192,448},{... | collective-permute-start | bytes 98312 | tf_op jit(solution)/shard_map/ppermute | solution.py:32
  75.4 4.8 %all-gather.4 = bf16[128,256]{1,0:T(8,128)(2,1)S(1)} all-gather(bf16[64,256]{1,0:T(8,128)(2,1)S(1)} %get-tuple-element.37), channel_id=6, replica_groups={{0,32},{64,96},{128,160},{192,224},{256,288},{320,352},{384,416},{448,4..., dimensions={0}, use_global_device_ids=true | all-gather | bytes 98304 | tf_op jit(solution)/shard_map/all_gather | solution.py:37
  80.1 0.0 collective-permute-done.9.refs_4_
  80.1 3.4 %collective-permute-done.8.refs_3_ = bf16[64,256]{1,0:T(8,128)(2,1)S(1)} collective-permute-done((bf16[64,256]{1,0:T(8,128)(2,1)S(1)}, bf16[64,256]{1,0:T(8,128)(2,1)S(1)}, u32[]{:S(2)}, u32[]{:S(2)}) %collective-permute-start.8) | collective-permute-done | bytes 32800 | tf_op jit(solution)/shard_map/ppermute | solution.py:32
  83.5 0.6 shard_map.61
  84.1 3.0 %collective-permute-start.10 = (bf16[64,256]{1,0:T(8,128)(2,1)S(1)}, bf16[64,256]{1,0:T(8,128)(2,1)S(1)}, u32[]{:S(2)}, u32[]{:S(2)}) collective-permute-start(bf16[64,256]{1,0:T(8,128)(2,1)S(1)} %get-tuple-element.40), channel_id=1, source_target_pairs={{0,16},{1,17},{2,18},{3,19},{4,20},{5,21},{6,22},{7,23},{8,24},{9,... | collective-permute-start | bytes 98312 | tf_op jit(solution)/shard_map/ppermute | solution.py:32
  87.1 1.9 %collective-permute-start.11 = (bf16[64,256]{1,0:T(8,128)(2,1)S(1)}, bf16[64,256]{1,0:T(8,128)(2,1)S(1)}, u32[]{:S(2)}, u32[]{:S(2)}) collective-permute-start(bf16[64,256]{1,0:T(8,128)(2,1)S(1)} %get-tuple-element.41), channel_id=1, source_target_pairs={{0,31},{1,2},{2,1},{3,4},{4,3},{5,6},{6,5},{7,8},{8,7},{9,10},{10,... | collective-permute-start | bytes 98312 | tf_op jit(solution)/shard_map/ppermute | solution.py:32
  89.0 1.9 %all-gather.5 = bf16[128,256]{1,0:T(8,128)(2,1)S(1)} all-gather(bf16[64,256]{1,0:T(8,128)(2,1)S(1)} %get-tuple-element.39), channel_id=7, replica_groups={{0,1},{2,3},{4,5},{6,7},{8,9},{10,11},{12,13},{14,15},{16,17},{18,19},{..., dimensions={0}, use_global_device_ids=true | all-gather | bytes 98304 | tf_op jit(solution)/shard_map/all_gather | solution.py:37
  90.9 0.5 collective-permute-done.10.far
  91.4 3.0 %collective-permute-done.11.cross = bf16[64,256]{1,0:T(8,128)(2,1)S(1)} collective-permute-done((bf16[64,256]{1,0:T(8,128)(2,1)S(1)}, bf16[64,256]{1,0:T(8,128)(2,1)S(1)}, u32[]{:S(2)}, u32[]{:S(2)}) %collective-permute-start.11) | collective-permute-done | bytes 32800 | tf_op jit(solution)/shard_map/ppermute | solution.py:32
  94.4 0.1 shard_map.62
  94.6 2.6 %collective-permute-start.13 = (bf16[64,256]{1,0:T(8,128)(2,1)S(1)}, bf16[64,256]{1,0:T(8,128)(2,1)S(1)}, u32[]{:S(2)}, u32[]{:S(2)}) collective-permute-start(bf16[64,256]{1,0:T(8,128)(2,1)S(1)} %get-tuple-element.42), channel_id=1, source_target_pairs={{0,480},{32,64},{64,32},{96,128},{128,96},{160,192},{192,160},{224... | collective-permute-start | bytes 98312 | tf_op jit(solution)/shard_map/ppermute | solution.py:32
  97.2 8.6 %collective-permute-start.12 = (bf16[64,256]{1,0:T(8,128)(2,1)S(1)}, bf16[64,256]{1,0:T(8,128)(2,1)S(1)}, u32[]{:S(2)}, u32[]{:S(2)}) collective-permute-start(bf16[64,256]{1,0:T(8,128)(2,1)S(1)} %get-tuple-element.42), channel_id=1, source_target_pairs={{0,256},{32,288},{64,320},{96,352},{128,384},{160,416},{192,448},{... | collective-permute-start | bytes 98312 | tf_op jit(solution)/shard_map/ppermute | solution.py:32
  105.8 0.6 shard_map.63.refs_6_
  106.4 4.6 %all-gather.6 = bf16[128,256]{1,0:T(8,128)(2,1)S(1)} all-gather(bf16[64,256]{1,0:T(8,128)(2,1)S(1)} %get-tuple-element.42), channel_id=8, replica_groups={{0,32},{64,96},{128,160},{192,224},{256,288},{320,352},{384,416},{448,4..., dimensions={0}, use_global_device_ids=true | all-gather | bytes 98304 | tf_op jit(solution)/shard_map/all_gather | solution.py:37
  111.0 0.0 collective-permute-done.13.refs_4_
  111.0 1.4 %collective-permute-done.12.refs_3_ = bf16[64,256]{1,0:T(8,128)(2,1)S(1)} collective-permute-done((bf16[64,256]{1,0:T(8,128)(2,1)S(1)}, bf16[64,256]{1,0:T(8,128)(2,1)S(1)}, u32[]{:S(2)}, u32[]{:S(2)}) %collective-permute-start.12) | collective-permute-done | bytes 32800 | tf_op jit(solution)/shard_map/ppermute | solution.py:32
  112.5 0.6 shard_map.64
  113.0 4.6 %collective-permute-start.14 = (bf16[64,256]{1,0:T(8,128)(2,1)S(1)}, bf16[64,256]{1,0:T(8,128)(2,1)S(1)}, u32[]{:S(2)}, u32[]{:S(2)}) collective-permute-start(bf16[64,256]{1,0:T(8,128)(2,1)S(1)} %get-tuple-element.45), channel_id=1, source_target_pairs={{0,16},{1,17},{2,18},{3,19},{4,20},{5,21},{6,22},{7,23},{8,24},{9,... | collective-permute-start | bytes 98312 | tf_op jit(solution)/shard_map/ppermute | solution.py:32
  117.7 1.9 %collective-permute-start.15 = (bf16[64,256]{1,0:T(8,128)(2,1)S(1)}, bf16[64,256]{1,0:T(8,128)(2,1)S(1)}, u32[]{:S(2)}, u32[]{:S(2)}) collective-permute-start(bf16[64,256]{1,0:T(8,128)(2,1)S(1)} %get-tuple-element.46), channel_id=1, source_target_pairs={{0,31},{1,2},{2,1},{3,4},{4,3},{5,6},{6,5},{7,8},{8,7},{9,10},{10,... | collective-permute-start | bytes 98312 | tf_op jit(solution)/shard_map/ppermute | solution.py:32
  119.6 1.9 %all-gather.7 = bf16[128,256]{1,0:T(8,128)(2,1)S(1)} all-gather(bf16[64,256]{1,0:T(8,128)(2,1)S(1)} %get-tuple-element.44), channel_id=9, replica_groups={{0,1},{2,3},{4,5},{6,7},{8,9},{10,11},{12,13},{14,15},{16,17},{18,19},{..., dimensions={0}, use_global_device_ids=true | all-gather | bytes 98304 | tf_op jit(solution)/shard_map/all_gather | solution.py:37
  121.4 0.0 collective-permute-done.14.far
  121.4 3.6 %collective-permute-done.15.cross = bf16[64,256]{1,0:T(8,128)(2,1)S(1)} collective-permute-done((bf16[64,256]{1,0:T(8,128)(2,1)S(1)}, bf16[64,256]{1,0:T(8,128)(2,1)S(1)}, u32[]{:S(2)}, u32[]{:S(2)}) %collective-permute-start.15) | collective-permute-done | bytes 32800 | tf_op jit(solution)/shard_map/ppermute | solution.py:32
  125.0 0.8 shard_map.65
  (1 shorter events, 0.0 us)
Async XLA Ops:
  1.1 15.5 %copy-start = (bf16[3,1,10,256,256]{4,3,2,1,0:T(8,128)(2,1)S(1)}, bf16[3,1,10,256,256]{4,3,2,1,0:T(8,128)(2,1)}, u32[]{:S(2)}) copy-start(bf16[3,1,10,256,256]{4,3,2,1,0:T(8,128)(2,1)} %refs_2_.11) | copy-start | bytes 11796484
  1.1 15.5 %copy-start.3 = (s32[3,1,10]{2,1,0:T(1,128)S(1)}, s32[3,1,10]{2,1,0:T(1,128)}, u32[]{:S(2)}) copy-start(s32[3,1,10]{2,1,0:T(1,128)} %refs_0_.11) | copy-start | bytes 364
  1.1 15.4 %copy-start.4 = (s32[3,1,10]{2,1,0:T(1,128)S(1)}, s32[3,1,10]{2,1,0:T(1,128)}, u32[]{:S(2)}) copy-start(s32[3,1,10]{2,1,0:T(1,128)} %refs_1_.11) | copy-start | bytes 364
  1.2 33.7 %copy-start.1 = (bf16[3,1,1,256,256]{4,3,2,1,0:T(8,128)(2,1)S(1)}, bf16[3,1,1,256,256]{4,3,2,1,0:T(8,128)(2,1)}, u32[]{:S(2)}) copy-start(bf16[3,1,1,256,256]{4,3,2,1,0:T(8,128)(2,1)} %inverse.7) | copy-start | bytes 1179652
  1.2 33.7 %copy-start.2 = (f32[3,1,1,64,256]{4,3,2,1,0:T(8,128)S(1)}, f32[3,1,1,64,256]{4,3,2,1,0:T(8,128)}, u32[]{:S(2)}) copy-start(f32[3,1,1,64,256]{4,3,2,1,0:T(8,128)} %rhs.3) | copy-start | bytes 589828
  1.2 11.8 %collective-permute-start.1 = (bf16[64,256]{1,0:T(8,128)(2,1)S(1)}, bf16[64,256]{1,0:T(8,128)(2,1)S(1)}, u32[]{:S(2)}, u32[]{:S(2)}) collective-permute-start(bf16[64,256]{1,0:T(8,128)(2,1)S(1)} %shard_map.55), channel_id=1, source_target_pairs={{0,16},{1,17},{2,18},{3,19},{4,20},{5,21},{6,22},{7,23},{8,24},{9,... | collective-permute-start | bytes 98312 | tf_op jit(solution)/shard_map/ppermute | solution.py:32
  9.2 7.3 %collective-permute-start = (bf16[64,256]{1,0:T(8,128)(2,1)S(1)}, bf16[64,256]{1,0:T(8,128)(2,1)S(1)}, u32[]{:S(2)}, u32[]{:S(2)}) collective-permute-start(bf16[64,256]{1,0:T(8,128)(2,1)S(1)} %shard_map.55), channel_id=1, source_target_pairs={{0,31},{1,2},{2,1},{3,4},{4,3},{5,6},{6,5},{7,8},{8,7},{9,10},{10,... | collective-permute-start | bytes 98312 | tf_op jit(solution)/shard_map/ppermute | solution.py:32
  17.2 17.3 %collective-permute-start.2 = (bf16[64,256]{1,0:T(8,128)(2,1)S(1)}, bf16[64,256]{1,0:T(8,128)(2,1)S(1)}, u32[]{:S(2)}, u32[]{:S(2)}) collective-permute-start(bf16[64,256]{1,0:T(8,128)(2,1)S(1)} %get-tuple-element.27), channel_id=1, source_target_pairs={{0,256},{32,288},{64,320},{96,352},{128,384},{160,416},{192,448},{... | collective-permute-start | bytes 98312 | tf_op jit(solution)/shard_map/ppermute | solution.py:32
  27.9 7.0 %collective-permute-start.3 = (bf16[64,256]{1,0:T(8,128)(2,1)S(1)}, bf16[64,256]{1,0:T(8,128)(2,1)S(1)}, u32[]{:S(2)}, u32[]{:S(2)}) collective-permute-start(bf16[64,256]{1,0:T(8,128)(2,1)S(1)} %get-tuple-element.28), channel_id=1, source_target_pairs={{0,480},{32,64},{64,32},{96,128},{128,96},{160,192},{192,160},{224... | collective-permute-start | bytes 98312 | tf_op jit(solution)/shard_map/ppermute | solution.py:32
  35.1 10.6 %collective-permute-start.5 = (bf16[64,256]{1,0:T(8,128)(2,1)S(1)}, bf16[64,256]{1,0:T(8,128)(2,1)S(1)}, u32[]{:S(2)}, u32[]{:S(2)}) collective-permute-start(bf16[64,256]{1,0:T(8,128)(2,1)S(1)} %get-tuple-element.32), channel_id=1, source_target_pairs={{0,16},{1,17},{2,18},{3,19},{4,20},{5,21},{6,22},{7,23},{8,24},{9,... | collective-permute-start | bytes 98312 | tf_op jit(solution)/shard_map/ppermute | solution.py:32
  40.9 7.3 %collective-permute-start.4 = (bf16[64,256]{1,0:T(8,128)(2,1)S(1)}, bf16[64,256]{1,0:T(8,128)(2,1)S(1)}, u32[]{:S(2)}, u32[]{:S(2)}) collective-permute-start(bf16[64,256]{1,0:T(8,128)(2,1)S(1)} %get-tuple-element.32), channel_id=1, source_target_pairs={{0,31},{1,2},{2,1},{3,4},{4,3},{5,6},{6,5},{7,8},{8,7},{9,10},{10,... | collective-permute-start | bytes 98312 | tf_op jit(solution)/shard_map/ppermute | solution.py:32
  48.8 15.1 %collective-permute-start.6 = (bf16[64,256]{1,0:T(8,128)(2,1)S(1)}, bf16[64,256]{1,0:T(8,128)(2,1)S(1)}, u32[]{:S(2)}, u32[]{:S(2)}) collective-permute-start(bf16[64,256]{1,0:T(8,128)(2,1)S(1)} %get-tuple-element.33), channel_id=1, source_target_pairs={{0,256},{32,288},{64,320},{96,352},{128,384},{160,416},{192,448},{... | collective-permute-start | bytes 98312 | tf_op jit(solution)/shard_map/ppermute | solution.py:32
  56.7 7.2 %collective-permute-start.7 = (bf16[64,256]{1,0:T(8,128)(2,1)S(1)}, bf16[64,256]{1,0:T(8,128)(2,1)S(1)}, u32[]{:S(2)}, u32[]{:S(2)}) collective-permute-start(bf16[64,256]{1,0:T(8,128)(2,1)S(1)} %get-tuple-element.34), channel_id=1, source_target_pairs={{0,480},{32,64},{64,32},{96,128},{128,96},{160,192},{192,160},{224... | collective-permute-start | bytes 98312 | tf_op jit(solution)/shard_map/ppermute | solution.py:32
  64.2 15.9 %collective-permute-start.9 = (bf16[64,256]{1,0:T(8,128)(2,1)S(1)}, bf16[64,256]{1,0:T(8,128)(2,1)S(1)}, u32[]{:S(2)}, u32[]{:S(2)}) collective-permute-start(bf16[64,256]{1,0:T(8,128)(2,1)S(1)} %get-tuple-element.37), channel_id=1, source_target_pairs={{0,480},{32,64},{64,32},{96,128},{128,96},{160,192},{192,160},{224... | collective-permute-start | bytes 98312 | tf_op jit(solution)/shard_map/ppermute | solution.py:32
  68.6 14.9 %collective-permute-start.8 = (bf16[64,256]{1,0:T(8,128)(2,1)S(1)}, bf16[64,256]{1,0:T(8,128)(2,1)S(1)}, u32[]{:S(2)}, u32[]{:S(2)}) collective-permute-start(bf16[64,256]{1,0:T(8,128)(2,1)S(1)} %get-tuple-element.37), channel_id=1, source_target_pairs={{0,256},{32,288},{64,320},{96,352},{128,384},{160,416},{192,448},{... | collective-permute-start | bytes 98312 | tf_op jit(solution)/shard_map/ppermute | solution.py:32
  84.1 7.3 %collective-permute-start.10 = (bf16[64,256]{1,0:T(8,128)(2,1)S(1)}, bf16[64,256]{1,0:T(8,128)(2,1)S(1)}, u32[]{:S(2)}, u32[]{:S(2)}) collective-permute-start(bf16[64,256]{1,0:T(8,128)(2,1)S(1)} %get-tuple-element.40), channel_id=1, source_target_pairs={{0,16},{1,17},{2,18},{3,19},{4,20},{5,21},{6,22},{7,23},{8,24},{9,... | collective-permute-start | bytes 98312 | tf_op jit(solution)/shard_map/ppermute | solution.py:32
  87.1 7.3 %collective-permute-start.11 = (bf16[64,256]{1,0:T(8,128)(2,1)S(1)}, bf16[64,256]{1,0:T(8,128)(2,1)S(1)}, u32[]{:S(2)}, u32[]{:S(2)}) collective-permute-start(bf16[64,256]{1,0:T(8,128)(2,1)S(1)} %get-tuple-element.41), channel_id=1, source_target_pairs={{0,31},{1,2},{2,1},{3,4},{4,3},{5,6},{6,5},{7,8},{8,7},{9,10},{10,... | collective-permute-start | bytes 98312 | tf_op jit(solution)/shard_map/ppermute | solution.py:32
  94.6 16.4 %collective-permute-start.13 = (bf16[64,256]{1,0:T(8,128)(2,1)S(1)}, bf16[64,256]{1,0:T(8,128)(2,1)S(1)}, u32[]{:S(2)}, u32[]{:S(2)}) collective-permute-start(bf16[64,256]{1,0:T(8,128)(2,1)S(1)} %get-tuple-element.42), channel_id=1, source_target_pairs={{0,480},{32,64},{64,32},{96,128},{128,96},{160,192},{192,160},{224... | collective-permute-start | bytes 98312 | tf_op jit(solution)/shard_map/ppermute | solution.py:32
  97.2 15.3 %collective-permute-start.12 = (bf16[64,256]{1,0:T(8,128)(2,1)S(1)}, bf16[64,256]{1,0:T(8,128)(2,1)S(1)}, u32[]{:S(2)}, u32[]{:S(2)}) collective-permute-start(bf16[64,256]{1,0:T(8,128)(2,1)S(1)} %get-tuple-element.42), channel_id=1, source_target_pairs={{0,256},{32,288},{64,320},{96,352},{128,384},{160,416},{192,448},{... | collective-permute-start | bytes 98312 | tf_op jit(solution)/shard_map/ppermute | solution.py:32
  113.0 8.4 %collective-permute-start.14 = (bf16[64,256]{1,0:T(8,128)(2,1)S(1)}, bf16[64,256]{1,0:T(8,128)(2,1)S(1)}, u32[]{:S(2)}, u32[]{:S(2)}) collective-permute-start(bf16[64,256]{1,0:T(8,128)(2,1)S(1)} %get-tuple-element.45), channel_id=1, source_target_pairs={{0,16},{1,17},{2,18},{3,19},{4,20},{5,21},{6,22},{7,23},{8,24},{9,... | collective-permute-start | bytes 98312 | tf_op jit(solution)/shard_map/ppermute | solution.py:32
  117.7 7.3 %collective-permute-start.15 = (bf16[64,256]{1,0:T(8,128)(2,1)S(1)}, bf16[64,256]{1,0:T(8,128)(2,1)S(1)}, u32[]{:S(2)}, u32[]{:S(2)}) collective-permute-start(bf16[64,256]{1,0:T(8,128)(2,1)S(1)} %get-tuple-element.46), channel_id=1, source_target_pairs={{0,31},{1,2},{2,1},{3,4},{4,3},{5,6},{6,5},{7,8},{8,7},{9,10},{10,... | collective-permute-start | bytes 98312 | tf_op jit(solution)/shard_map/ppermute | solution.py:32
